TPU v7x, 128 devices: a whole 4x4x4 slice. The times are simulated.
128 devices in a mesh: ax: 8 (over x, core), rad: 16 (over z, y).
Axes of the slice: x: 4, y: 4, z: 4, core: 2. Of those that a mesh axis runs over, the one named last changes fastest.
Arguments:
- sources: float32 [16, 32, 200, 128], P('ax', 'rad'), may hold values from -0.6 to 0.6
- block_inverse: float32 [16, 32, 200, 200], P('ax', 'rad'), may hold values from -2 to 2, as said below
- radial_coupling: float32 [16, 32, 2, 200], P('ax', 'rad'), may hold values from 0.2 to 1.2
- axial_coupling: float32 [16, 32, 4, 200], P('ax', 'rad'), may hold values from 0.01 to 0.05
Outputs:
- correction: float32 [16, 32, 200, 128], P('ax', 'rad')
Inputs may be any that keep to these rules, and one draw needn't show every extreme that they name: `block_inverse`: the given inverse of each cell's diagonal block.
All inputs are finite; a program needn't handle non-finite values.
Results may differ from a plain program's by a relative error of at most 0.00014.
Values sent between devices are 32-bit elements; how exact they have to be, the bound alone decides.
No kernel may reach another device: no remote copies, remote signals or barrier semaphores. Data moves between devices by JAX's collectives and lax.ppermute only.
A program may use at most 64 MiB of HBM per device.

v0:
```python
import jax
import jax.numpy as jnp
from jax import lax
from jax.sharding import Mesh
from jax.sharding import PartitionSpec as P

SWEEPS = 2
RAD = ("rad_0", "rad_1")


def padded_2(block, sides, width):
    for axis, dim in sides:
        count = lax.axis_size(axis)
        forward = [(i, i + 1) for i in range(count - 1)]
        backward = [(target, source) for source, target in forward]
        low = lax.ppermute(
            lax.slice_in_dim(block, block.shape[dim] - width, None, axis=dim), axis, forward
        )
        high = lax.ppermute(lax.slice_in_dim(block, 0, width, axis=dim), axis, backward)
        block = jnp.concatenate([low, block, high], axis=dim)
    return block


def neutral_like(x, identity):
    return jax.tree.map(
        lambda part, zero: jnp.zeros_like(part) + jnp.asarray(zero, part.dtype), x, identity
    )


def prefix_by_axis(x, axes, combine, identity, reverse):
    before = start = neutral_like(x, identity)
    so_far = x
    for axis in reversed(axes):
        length, mine = (lax.axis_size(axis), lax.axis_index(axis))
        pieces = jax.tree.map(lambda part: lax.all_gather(part, axis), so_far)
        inside, so_far = (start, start)
        for k in reversed(range(length)) if reverse else range(length):
            passed = k > mine if reverse else k < mine
            so_far = combine(so_far, jax.tree.map(lambda part: part[k], pieces))
            inside = jax.tree.map(lambda new, old: jnp.where(passed, new, old), so_far, inside)
        before = combine(inside, before)
    return before


def apply_block(inverse_row, operand):
    return jnp.einsum("aij,ajk->aik", inverse_row, operand, precision=lax.Precision.HIGHEST)


def inner_pass(line_source, block_inverse, inward_coupling, incoming):
    values = []
    previous = incoming
    for radial in range(line_source.shape[1]):
        shifted = line_source[:, radial] - inward_coupling[:, radial, :, None] * previous
        previous = apply_block(block_inverse[:, radial], shifted)
        values.append(previous)
    return (jnp.stack(values, 1), previous)


def outer_pass(inner_value, block_inverse, outward_coupling, incoming):
    values = []
    following = incoming
    for radial in reversed(range(inner_value.shape[1])):
        shifted = outward_coupling[:, radial, :, None] * following
        following = inner_value[:, radial] - apply_block(block_inverse[:, radial], shifted)
        values.append(following)
    return (jnp.stack(values[::-1], 1), following)


def chain_matrix(block_inverse, coupling, visiting):
    stations, species = (block_inverse.shape[0], block_inverse.shape[2])
    product = jnp.broadcast_to(jnp.eye(species, dtype=jnp.float32), (stations, species, species))
    for radial in visiting:
        product = -apply_block(block_inverse[:, radial], coupling[:, radial, :, None] * product)
    return product


def compose(earlier, subsequent):
    matrix_early, vector_early = earlier
    matrix_late, vector_late = subsequent
    return (
        apply_block(matrix_late, matrix_early),
        apply_block(matrix_late, vector_early) + vector_late,
    )


def on_device(sources, block_inverse, radial_coupling, axial_coupling):
    stations, radial_cells, species, columns = sources.shape
    inward_coupling = radial_coupling[:, :, 0]
    outward_coupling = radial_coupling[:, :, 1]
    zero_field = jnp.zeros((stations, species, columns), jnp.float32)
    identity = (
        jnp.broadcast_to(jnp.eye(species, dtype=jnp.float32), (stations, species, species)),
        zero_field,
    )
    inner_matrix = chain_matrix(block_inverse, inward_coupling, list(range(radial_cells)))
    outer_matrix = chain_matrix(
        block_inverse, outward_coupling, list(reversed(range(radial_cells)))
    )
    correction = jnp.zeros(sources.shape, jnp.float32)
    for sweep_index in range(SWEEPS):
        if sweep_index == 0:
            line_source = sources
        else:
            padded = padded_2(correction, (("ax", 0),), 2)
            line_source = sources
            line_source = line_source - axial_coupling[:, :, 0, :, None] * padded[0:stations]
            line_source = line_source - axial_coupling[:, :, 1, :, None] * padded[1 : stations + 1]
            line_source = line_source - axial_coupling[:, :, 2, :, None] * padded[3 : stations + 3]
            line_source = line_source - axial_coupling[:, :, 3, :, None] * padded[4 : stations + 4]
        _, local_last = inner_pass(line_source, block_inverse, inward_coupling, zero_field)
        _, arriving = prefix_by_axis((inner_matrix, local_last), RAD, compose, identity, False)
        inner_value, _ = inner_pass(line_source, block_inverse, inward_coupling, arriving)
        _, local_first = outer_pass(inner_value, block_inverse, outward_coupling, zero_field)
        _, arriving = prefix_by_axis((outer_matrix, local_first), RAD, compose, identity, True)
        correction, _ = outer_pass(inner_value, block_inverse, outward_coupling, arriving)
    return correction


def solution(mesh):
    torus = Mesh(mesh.devices.reshape(mesh.shape["ax"], 4, 4), ("ax", "rad_0", "rad_1"))
    placed = (
        P("ax", RAD, None, None),
        P("ax", RAD, None, None),
        P("ax", RAD, None, None),
        P("ax", RAD, None, None),
    )
    return jax.shard_map(
        on_device, mesh=torus, in_specs=placed, out_specs=P("ax", RAD, None, None), check_vma=False
    )
```

profile of v0, /device:TPU:4, one launch (start us, length us, event | category | flops | bytes accessed | tf_op | source)
XLA Modules:
  0.0 241.5 jit_solution(7222533782568774929)
XLA Ops:
  7.4 2.1 fusion.2
  9.5 1.6 fusion.1
  14.8 1.3 fusion.32
  17.2 17.1 %all-gather.2 = f32[8,200,128]{2,1,0:T(8,128)S(1)} all-gather(f32[2,200,128]{2,1,0:T(8,128)S(1)} %convolution_bitcast_fusion.1), channel_id=4, replica_groups=mesh['ax'=8,'rad_0'=4,'rad_1'=4] {'rad_1'}, dimensions={0}, use_global_device_ids=true | all-gather | bytes 1024000 | tf_op jit(solution)/shard_map/all_gather | solution.py:35
  34.3 10.0 %all-gather.17.cloned.1.call-done = f32[8,200,200]{2,1,0:T(8,128)} async-done(((f32[2,200,200]{2,1,0:T(8,128)}), f32[8,200,200]{2,1,0:T(8,128)}) %all-gather.17.cloned.1.call-update) | async-done | bytes 1280016 | tf_op jit(solution)/shard_map/all_gather | solution.py:35
  44.3 1.6 fusion.107
  49.3 1.3 fusion.183
  53.6 1.2 convolution_add_fusion.25
  54.8 18.6 %all-gather.21.cloned.1.call-done = f32[8,200,200]{2,1,0:T(8,128)} async-done(((f32[2,200,200]{2,1,0:T(8,128)}), f32[8,200,200]{2,1,0:T(8,128)}) %all-gather.21.cloned.1.call-update) | async-done | bytes 1280016 | tf_op jit(solution)/shard_map/all_gather | solution.py:35
  73.4 1.6 fusion.101
  78.6 1.3 fusion.186
  79.9 21.0 %all-gather.3 = f32[8,200,128]{2,1,0:T(8,128)} all-gather(f32[2,200,128]{2,1,0:T(8,128)} %convolution_add_fusion.25), channel_id=5, replica_groups=mesh['ax'=8,'rad_0'=4,'rad_1'=4] {'rad_0'}, dimensions={0}, use_global_device_ids=true | all-gather | bytes 1024000 | tf_op jit(solution)/shard_map/all_gather | solution.py:35
  101.0 1.4 fusion.57
  102.3 1.3 fusion.51
  103.7 1.1 fusion.141
  104.8 2.4 %all-gather.19.cloned.1.call-done = f32[8,200,200]{2,1,0:T(8,128)} async-done(((f32[2,200,200]{2,1,0:T(8,128)}), f32[8,200,200]{2,1,0:T(8,128)}) %all-gather.19.cloned.1.call-update) | async-done | bytes 1280016 | tf_op jit(solution)/shard_map/all_gather | solution.py:35
  107.3 1.6 fusion.148
  108.9 1.7 convolution_add_fusion.24
  112.5 1.5 fusion.16
  115.8 13.6 %all-gather.6 = f32[8,200,128]{2,1,0:T(8,128)S(1)} all-gather(f32[2,200,128]{2,1,0:T(8,128)S(1)} %fusion.12), channel_id=8, replica_groups=mesh['ax'=8,'rad_0'=4,'rad_1'=4] {'rad_1'}, dimensions={0}, use_global_device_ids=true | all-gather | bytes 1024000 | tf_op jit(solution)/shard_map/all_gather | solution.py:35
  131.9 14.9 %all-gather.7 = f32[8,200,128]{2,1,0:T(8,128)} all-gather(f32[2,200,128]{2,1,0:T(8,128)S(1)} %convolution_add_fusion.19), channel_id=9, replica_groups=mesh['ax'=8,'rad_0'=4,'rad_1'=4] {'rad_0'}, dimensions={0}, use_global_device_ids=true | all-gather | bytes 1024000 | tf_op jit(solution)/shard_map/all_gather | solution.py:35
  146.8 1.6 fusion.143
  148.5 1.7 convolution_add_fusion.18
  151.9 1.5 fusion.11
  154.5 1.9 collective-permute-start.1
  156.4 2.6 %collective-permute-start = (f32[2,2,200,128]{3,2,0,1:T(8,128)S(1)}, f32[2,2,200,128]{3,2,0,1:T(8,128)S(1)}, u32[]{:S(2)}, u32[]{:S(2)}) collective-permute-start(f32[2,2,200,128]{3,2,0,1:T(8,128)S(1)} %pad_maximum_fusion.4), channel_id=1, source_target_pairs={{0,16},{16,32},{32,48},{48,64},{64,80},{80,96},{96,112},{1,17},{17... | collective-permute-start | bytes 1228808 | tf_op jit(solution)/shard_map/ppermute | solution.py:16
  159.1 2.8 %collective-permute-done.1 = f32[2,2,200,128]{3,2,0,1:T(8,128)S(1)} collective-permute-done((f32[2,2,200,128]{3,2,0,1:T(8,128)S(1)}, f32[2,2,200,128]{3,2,0,1:T(8,128)S(1)}, u32[]{:S(2)}, u32[]{:S(2)}) %collective-permute-start.1) | collective-permute-done | bytes 409632 | tf_op jit(solution)/shard_map/ppermute | solution.py:19
  161.9 3.8 %collective-permute-done = f32[2,2,200,128]{3,2,0,1:T(8,128)S(1)} collective-permute-done((f32[2,2,200,128]{3,2,0,1:T(8,128)S(1)}, f32[2,2,200,128]{3,2,0,1:T(8,128)S(1)}, u32[]{:S(2)}, u32[]{:S(2)}) %collective-permute-start) | collective-permute-done | bytes 409632 | tf_op jit(solution)/shard_map/ppermute | solution.py:16
  167.3 14.4 %all-gather.8 = f32[8,200,128]{2,1,0:T(8,128)S(1)} all-gather(f32[2,200,128]{2,1,0:T(8,128)S(1)} %convolution_bitcast_fusion), channel_id=10, replica_groups=mesh['ax'=8,'rad_0'=4,'rad_1'=4] {'rad_1'}, dimensions={0}, use_global_device_ids=true | all-gather | bytes 1024000 | tf_op jit(solution)/shard_map/all_gather | solution.py:35
  183.3 14.1 %all-gather.9 = f32[8,200,128]{2,1,0:T(8,128)S(1)} all-gather(f32[2,200,128]{2,1,0:T(8,128)S(1)} %convolution_add_fusion.13), channel_id=11, replica_groups=mesh['ax'=8,'rad_0'=4,'rad_1'=4] {'rad_0'}, dimensions={0}, use_global_device_ids=true | all-gather | bytes 1024000 | tf_op jit(solution)/shard_map/all_gather | solution.py:35
  201.8 13.4 %all-gather.10 = f32[8,200,128]{2,1,0:T(8,128)S(1)} all-gather(f32[2,200,128]{2,1,0:T(8,128)S(1)} %fusion.6), channel_id=12, replica_groups=mesh['ax'=8,'rad_0'=4,'rad_1'=4] {'rad_1'}, dimensions={0}, use_global_device_ids=true | all-gather | bytes 1024000 | tf_op jit(solution)/shard_map/all_gather | solution.py:35
  216.7 13.6 %all-gather.11 = f32[8,200,128]{2,1,0:T(8,128)S(1)} all-gather(f32[2,200,128]{2,1,0:T(8,128)S(1)} %convolution_add_fusion.7), channel_id=13, replica_groups=mesh['ax'=8,'rad_0'=4,'rad_1'=4] {'rad_0'}, dimensions={0}, use_global_device_ids=true | all-gather | bytes 1024000 | tf_op jit(solution)/shard_map/all_gather | solution.py:35
  (182 shorter events, 37.3 us)
Async XLA Ops:
  6.5 37.7 %all-gather.17.cloned.1.call-start = ((), (), s32[]{:S(2)}) async-start(), calls=%async_computation | async-start | bytes 2048000 | tf_op jit(solution)/shard_map/all_gather | solution.py:35
  7.4 4.8 %copy-start.2 = (f32[2,2,200,200]{3,2,1,0:T(8,128)S(1)}, f32[2,2,200,200]{3,2,1,0:T(8,128)}, u32[]{:S(2)}) copy-start(f32[2,2,200,200]{3,2,1,0:T(8,128)} %param.5) | copy-start | bytes 1920004
  12.0 61.4 %all-gather.21.cloned.1.call-start = ((), (), s32[]{:S(2)}) async-start(), calls=%async_computation.2 | async-start | bytes 2048000 | tf_op jit(solution)/shard_map/all_gather | solution.py:35
  13.2 2.9 %copy-start.52 = (f32[2,2,4,200]{3,2,1,0:T(4,128)S(1)}, f32[2,2,4,200]{3,2,1,0:T(4,128)}, u32[]{:S(2)}) copy-start(f32[2,2,4,200]{3,2,1,0:T(4,128)} %param.7) | copy-start | bytes 38404
  13.2 2.9 %copy-start.32 = (f32[2,2,200,128]{3,2,1,0:T(8,128)S(1)}, f32[2,2,200,128]{3,2,1,0:T(8,128)}, u32[]{:S(2)}) copy-start(f32[2,2,200,128]{3,2,1,0:T(8,128)} %param.4) | copy-start | bytes 1228804
  14.7 92.6 %all-gather.19.cloned.1.call-start = ((), (), s32[]{:S(2)}) async-start(), calls=%async_computation.1 | async-start | bytes 2048000 | tf_op jit(solution)/shard_map/all_gather | solution.py:35
  34.3 18.6 %copy-start.28 = (f32[8,200,128]{2,1,0:T(8,128)}, f32[8,200,128]{2,1,0:T(8,128)S(1)}, u32[]{:S(2)}) copy-start(f32[8,200,128]{2,1,0:T(8,128)S(1)} %all-gather.2) | copy-start | bytes 2457604
  44.3 2.4 copy-start.1
  50.6 96.2 %all-gather.23.cloned.1.call-start = ((), (), s32[]{:S(2)}) async-start(), calls=%async_computation.3 | async-start | bytes 2048000 | tf_op jit(solution)/shard_map/all_gather | solution.py:35
  51.1 1.8 copy-start.10
  73.4 2.5 %copy-start = (f32[8,200,200]{2,1,0:T(8,128)S(1)}, f32[8,200,200]{2,1,0:T(8,128)}, u32[]{:S(2)}) copy-start(f32[8,200,200]{2,1,0:T(8,128)} %all-gather.21.cloned.1.call-done) | copy-start | bytes 3840004
  100.9 1.4 copy-start.18
  107.3 3.4 %copy-start.6 = (f32[8,200,200]{2,1,0:T(8,128)S(1)}, f32[8,200,200]{2,1,0:T(8,128)}, u32[]{:S(2)}) copy-start(f32[8,200,200]{2,1,0:T(8,128)} %all-gather.19.cloned.1.call-done) | copy-start | bytes 3840004
  107.3 3.4 %copy-start.35 = (f32[8,200,128]{2,1,0:T(8,128)S(1)}, f32[8,200,128]{2,1,0:T(8,128)}, u32[]{:S(2)}) copy-start(f32[8,200,128]{2,1,0:T(8,128)} %all-gather.3) | copy-start | bytes 2457604
  108.9 2.3 copy-start.13
  111.8 2.2 copy-start.3
  112.5 2.6 %copy-start.45 = (f32[2,128,200]{1,2,0:T(8,128)S(1)}, f32[2,128,200]{1,2,0:T(8,128)}, u32[]{:S(2)}) copy-start(f32[2,128,200]{1,2,0:T(8,128)} %fusion.32) | copy-start | bytes 614404
  114.6 14.9 %copy-start.30 = (f32[2,128,200]{1,2,0:T(8,128)}, f32[2,128,200]{1,2,0:T(8,128)S(1)}, u32[]{:S(2)}) copy-start(f32[2,128,200]{1,2,0:T(8,128)S(1)} %fusion.47) | copy-start | bytes 614404
  114.6 14.9 %copy-start.8 = (f32[2,200,128]{2,1,0:T(8,128)S(1)}, f32[2,200,128]{2,1,0:T(8,128)}, u32[]{:S(2)}) copy-start(f32[2,200,128]{2,1,0:T(8,128)} %fusion.141) | copy-start | bytes 614404
  115.2 14.8 %copy-start.50 = (f32[2,128,200]{1,2,0:T(8,128)}, f32[2,128,200]{1,2,0:T(8,128)S(1)}, u32[]{:S(2)}) copy-start(f32[2,128,200]{1,2,0:T(8,128)S(1)} %fusion.35) | copy-start | bytes 614404
  146.8 3.3 %copy-start.5 = (f32[8,200,200]{2,1,0:T(8,128)S(1)}, f32[8,200,200]{2,1,0:T(8,128)}, u32[]{:S(2)}) copy-start(f32[8,200,200]{2,1,0:T(8,128)} %all-gather.23.cloned.1.call-done) | copy-start | bytes 3840004
  146.8 3.3 %copy-start.36 = (f32[8,200,128]{2,1,0:T(8,128)S(1)}, f32[8,200,128]{2,1,0:T(8,128)}, u32[]{:S(2)}) copy-start(f32[8,200,128]{2,1,0:T(8,128)} %all-gather.7) | copy-start | bytes 2457604
  151.3 2.1 copy-start.4
  151.3 2.1 copy-start.51
  151.3 2.6 %copy-start.31 = (f32[2,128,200]{1,2,0:T(8,128)S(1)}, f32[2,128,200]{1,2,0:T(8,128)}, u32[]{:S(2)}) copy-start(f32[2,128,200]{1,2,0:T(8,128)} %copy-done.30) | copy-start | bytes 614404
  153.4 12.4 %copy-start.34 = (f32[2,2,200,128]{3,2,1,0:T(8,128)S(1)}, f32[2,2,200,128]{3,2,1,0:T(8,128)}, u32[]{:S(2)}) copy-start(f32[2,2,200,128]{3,2,1,0:T(8,128)} %param.4) | copy-start | bytes 1228804
  154.5 7.4 %collective-permute-start.1 = (f32[2,2,200,128]{3,2,0,1:T(8,128)S(1)}, f32[2,2,200,128]{3,2,0,1:T(8,128)S(1)}, u32[]{:S(2)}, u32[]{:S(2)}) collective-permute-start(f32[2,2,200,128]{3,2,0,1:T(8,128)S(1)} %pad_maximum_fusion.4), channel_id=1, source_target_pairs={{16,0},{32,16},{48,32},{64,48},{80,64},{96,80},{112,96},{17,1},{33... | collective-permute-start | bytes 1228808 | tf_op jit(solution)/shard_map/ppermute | solution.py:19
  156.4 9.3 %collective-permute-start = (f32[2,2,200,128]{3,2,0,1:T(8,128)S(1)}, f32[2,2,200,128]{3,2,0,1:T(8,128)S(1)}, u32[]{:S(2)}, u32[]{:S(2)}) collective-permute-start(f32[2,2,200,128]{3,2,0,1:T(8,128)S(1)} %pad_maximum_fusion.4), channel_id=1, source_target_pairs={{0,16},{16,32},{32,48},{48,64},{64,80},{80,96},{96,112},{1,17},{17... | collective-permute-start | bytes 1228808 | tf_op jit(solution)/shard_map/ppermute | solution.py:16
  166.2 15.5 %copy-start.12 = (f32[2,200,128]{2,1,0:T(8,128)S(1)}, f32[2,200,128]{2,1,0:T(8,128)}, u32[]{:S(2)}) copy-start(f32[2,200,128]{2,1,0:T(8,128)} %copy-done.10) | copy-start | bytes 614404
  182.7 14.7 %copy-start.7 = (f32[8,200,200]{2,1,0:T(8,128)S(1)}, f32[8,200,200]{2,1,0:T(8,128)}, u32[]{:S(2)}) copy-start(f32[8,200,200]{2,1,0:T(8,128)} %all-gather.19.cloned.1.call-done) | copy-start | bytes 3840004
  182.8 14.7 %copy-start.14 = (f32[2,200,128]{2,1,0:T(8,128)S(1)}, f32[2,200,128]{2,1,0:T(8,128)}, u32[]{:S(2)}) copy-start(f32[2,200,128]{2,1,0:T(8,128)} %copy-done.13) | copy-start | bytes 614404
  199.5 1.6 copy-start.46
  (27 other events, 27.5 us)
Sparse Core Ops, SparseCore 0:
  12.1 32.0 all-gather.16
  45.9 27.4 all-gather.20
  75.1 32.1 all-gather.18
  108.8 25.5 all-gather.22
where the time goes:
time: 242 us; the launch traced here: 241 us
  blocking collectives  122 us (50%)
  matrix products  51.4 us (21%)
  waiting for transfers between devices  37.7 us (16%)
  between operations  14.3 us (6%)
  local copies, waits for them, and re-layouts  10.7 us (4%)
  starting transfers between devices  4.68 us (2%)
    all_gather x8, blocking collectives, prefix_by_axis(): pieces = jax.tree.map(lambda part: lax.all_gather(part, axis), so_far)  122 us
    dot_general x65, matrix products, apply_block(): jnp.einsum('aij,ajk->aik', inverse_row, operand, precision=lax.Precision....  51.4 us
    all_gather x4, waiting for transfers between devices, prefix_by_axis(): pieces = jax.tree.map(lambda part: lax.all_gather(part, axis), so_far)  31.1 us
    unnamed x110, local copies, waits for them, and re-layouts  7.21 us
  transfers between devices with their start and end apart: 6, of which 5 were waited for; matrix products, arithmetic and copies ran while one was open for 12% of the time, Pallas kernels for 0%

commit v1 on v0

v1 whole, which is shorter than its diff:
```python
import jax
import jax.numpy as jnp
from jax import lax
from jax.experimental import pallas as pl
from jax.experimental.pallas import tpu as pltpu
from jax.sharding import Mesh
from jax.sharding import PartitionSpec as P

SWEEPS = 2
RAD = ("rad_0", "rad_1")
GROUP = 4
F32 = jnp.float32
BF16 = jnp.bfloat16


def split(value):
    high = value.astype(BF16)
    return high, (value - high.astype(F32)).astype(BF16)


def dot(a, b, contract):
    dims = (((1,), (contract,)), ((), ()))
    return lax.dot_general(a, b, dims, preferred_element_type=F32)


def times(value, high, low, contract):
    value_high, value_low = split(value)
    return (
        dot(value_high, high, contract)
        + dot(value_low, high, contract)
        + dot(value_high, low, contract)
    )


def call(body, out, flops, scratch=(), scalars=0):
    def run(*operands):
        specs = [pl.BlockSpec(memory_space=pltpu.SMEM)] * scalars
        specs += [pl.BlockSpec(memory_space=pltpu.VMEM)] * (len(operands) - scalars)
        moved = sum(o.size * o.dtype.itemsize for o in operands)
        return pl.pallas_call(
            body,
            out_shape=[jax.ShapeDtypeStruct(shape, kind) for shape, kind in out],
            in_specs=specs,
            out_specs=[pl.BlockSpec(memory_space=pltpu.VMEM)] * len(out),
            scratch_shapes=list(scratch),
            name=body.__name__,
            cost_estimate=pl.CostEstimate(
                flops=flops, transcendentals=0, bytes_accessed=moved
            ),
            compiler_params=pltpu.CompilerParams(vmem_limit_bytes=48 * 1024 * 1024),
        )(*operands)

    return run


def pack(mine_ref, sources_ref, radial_ref, axial_ref, m0, m1, m2, m3, turned):
    mine = mine_ref[0]
    width = m0.shape[2] - 8
    for station in range(sources_ref.shape[0]):
        for cell in range(sources_ref.shape[1]):
            turned[...] = sources_ref[station, cell].T
            for ahead, message in enumerate((m0, m1, m2, m3)):
                row = pl.multiple_of(lax.rem(mine + ahead, GROUP) * width, 8)
                message[station, cell, 0:width] = turned[pl.ds(row, width)]
                message[station, cell, width : width + 2] = radial_ref[station, cell]
                message[station, cell, width + 2 : width + 6] = axial_ref[station, cell]
                message[station, cell, width + 6 : width + 8] = jnp.zeros(
                    (2, turned.shape[1]), F32
                )


def first_inner(
    mine_ref, b0, b1, b2a, b2b, b3, m0, m1, m2, m3,
    fields, high, low, local, carry_high, carry_low, last, chain,
):
    mine = mine_ref[0]
    cells = b0.shape[1]
    width = local.shape[2]
    species = b0.shape[2]
    for station in range(2):
        opposite = (b2a, b2b)[station]
        for ahead in range(GROUP):
            base = lax.rem(mine + ahead, GROUP) * cells
            for cell in range(cells):
                if ahead == 2:
                    block = opposite[0, cell]
                else:
                    block = (b0, b1, None, b3)[ahead][station, cell]
                block_high, block_low = split(block)
                high[station, base + cell] = block_high
                low[station, base + cell] = block_low
                fields[station, base + cell] = (m0, m1, m2, m3)[ahead][station, cell]
    rows = lax.broadcasted_iota(jnp.int32, (species, species), 0)
    lanes = lax.broadcasted_iota(jnp.int32, (species, species), 1)
    unit = jnp.where(rows == lanes, 1.0, 0.0).astype(F32)
    matrix = [unit, unit]
    value = [None, None]
    for cell in range(GROUP * cells):
        for station in range(2):
            coupling = fields[station, cell, width : width + 1]
            shifted = fields[station, cell, 0:width]
            if cell:
                shifted = shifted - coupling * value[station]
            block_high, block_low = high[station, cell], low[station, cell]
            value[station] = times(shifted, block_high, block_low, 1)
            matrix[station] = times(-coupling * matrix[station], block_high, block_low, 1)
            local[station, cell] = value[station]
            part_high, part_low = split(matrix[station])
            carry_high[station, cell] = part_high
            carry_low[station, cell] = part_low
    for station in range(2):
        last[station] = value[station]
        chain[station] = matrix[station]


def outer_matrices(fields, high, low, carry_high, carry_low, chain):
    cells = high.shape[1]
    species = high.shape[2]
    width = fields.shape[2] - 8
    rows = lax.broadcasted_iota(jnp.int32, (species, species), 0)
    lanes = lax.broadcasted_iota(jnp.int32, (species, species), 1)
    unit = jnp.where(rows == lanes, 1.0, 0.0).astype(F32)
    matrix = [unit, unit]
    for cell in reversed(range(cells)):
        for station in range(2):
            coupling = fields[station, cell, width + 1 : width + 2]
            matrix[station] = times(
                -coupling * matrix[station], high[station, cell], low[station, cell], 1
            )
            part_high, part_low = split(matrix[station])
            carry_high[station, cell] = part_high
            carry_low[station, cell] = part_low
    for station in range(2):
        chain[station] = matrix[station]


def advance(ends, near, carry_high, carry_low, cell, joined):
    for station in range(2):
        joined[station] = ends[station] + times(
            near[station], carry_high[station, cell], carry_low[station, cell], 0
        )


def advance_inner(ends, near, carry_high, carry_low, joined):
    advance(ends, near, carry_high, carry_low, carry_high.shape[1] - 1, joined)


def advance_outer(ends, near, carry_high, carry_low, joined):
    advance(ends, near, carry_high, carry_low, 0, joined)


def incoming(near, middle, far, chain, station):
    matrix_high, matrix_low = split(chain[station])
    return near[station] + middle[station] + times(far[station], matrix_high, matrix_low, 0)


def outer_local(
    near, middle, far, chain, inner, carry_high, carry_low, fields, high, low, local, last
):
    cells = inner.shape[1]
    width = inner.shape[2]
    arriving = [incoming(near, middle, far, chain, station) for station in range(2)]
    value = [None, None]
    for cell in reversed(range(cells)):
        for station in range(2):
            whole = inner[station, cell] + times(
                arriving[station], carry_high[station, cell], carry_low[station, cell], 0
            )
            if value[station] is not None:
                coupling = fields[station, cell, width + 1 : width + 2]
                whole = whole - times(
                    coupling * value[station], high[station, cell], low[station, cell], 1
                )
            value[station] = whole
            local[station, cell] = whole
    for station in range(2):
        last[station] = value[station]


def finish(near, middle, far, chain, outer, carry_high, carry_low, correction):
    for station in range(2):
        arriving = incoming(near, middle, far, chain, station)
        for cell in range(outer.shape[1]):
            correction[station, cell] = outer[station, cell] + times(
                arriving, carry_high[station, cell], carry_low[station, cell], 0
            )


def next_inner(below, own, above, fields, high, low, local, last):
    cells = own.shape[1]
    width = own.shape[2]
    value = [None, None]
    for cell in range(cells):
        around = [part[s, cell] for part in (below, own, above) for s in range(2)]
        for station in range(2):
            source = fields[station, cell, 0:width]
            for term, place in enumerate((0, 1, 3, 4)):
                factor = fields[station, cell, width + 2 + term : width + 3 + term]
                source = source - factor * around[station + place]
            if value[station] is not None:
                coupling = fields[station, cell, width : width + 1]
                source = source - coupling * value[station]
            value[station] = times(source, high[station, cell], low[station, cell], 1)
            local[station, cell] = value[station]
    for station in range(2):
        last[station] = value[station]


def finish_last(
    mine_ref, near, middle, far, chain, outer, carry_high, carry_low, m0, m1, m2, m3, whole
):
    finish(near, middle, far, chain, outer, carry_high, carry_low, whole)
    mine = mine_ref[0]
    cells = m0.shape[1]
    for station in range(2):
        for ahead, message in enumerate((m0, m1, m2, m3)):
            base = lax.rem(mine + ahead, GROUP) * cells
            for cell in range(cells):
                message[station, cell] = whole[station, base + cell]


def unpack(mine_ref, m0, m1, m2, m3, correction, turned):
    mine = mine_ref[0]
    width = m0.shape[2]
    for station in range(2):
        for cell in range(m0.shape[1]):
            for ahead, message in enumerate((m0, m1, m2, m3)):
                row = pl.multiple_of(lax.rem(mine + ahead, GROUP) * width, 8)
                turned[pl.ds(row, width)] = message[station, cell]
            correction[station, cell] = turned[...].T


def shift(value, axis, step):
    count = lax.axis_size(axis)
    return lax.ppermute(value, axis, [(i, (i + step) % count) for i in range(count)])


def scan(ends, carry, chain, step, pairs, then, advance_body):
    stations, width, species = ends.shape
    near = lax.ppermute(ends, "rad_0", pairs)
    (joined,) = call(advance_body, [(ends.shape, F32)], 6 * stations * width * species**2)(
        ends, near, *carry
    )
    middle = lax.ppermute(joined, "rad_0", [then[0]])
    far = lax.ppermute(joined, "rad_0", [then[1]])
    return near, middle, far, chain


def on_device(sources, block_inverse, radial_coupling, axial_coupling):
    stations, own_cells, species, columns = sources.shape
    cells = own_cells * GROUP
    width = columns // GROUP
    mine = lax.axis_index("rad_1").astype(jnp.int32).reshape(1)
    step = 6 * stations * cells * species**2
    field = (stations, cells, width, species)
    square = (stations, cells, species, species)
    edge = (stations, width, species)

    half = [block_inverse[s : s + 1] for s in range(2)]
    below = [None, None]
    above = [None, None]
    below[0] = shift(half[0], "rad_1", 1)
    above[1] = shift(half[1], "rad_1", -1)
    message = [(stations, own_cells, width + 8, species)] * GROUP
    sent = call(
        pack,
        [(shape, F32) for shape in message],
        1000,
        scratch=[pltpu.VMEM((columns, species), F32)],
        scalars=1,
    )(mine, sources, radial_coupling, axial_coupling)
    got = [sent[0]] + [None] * 3
    for ahead in range(1, GROUP):
        got[GROUP - ahead] = shift(sent[ahead], "rad_1", ahead)
    below[1] = shift(half[1], "rad_1", 1)
    above[0] = shift(half[0], "rad_1", -1)
    across = [shift(below[0], "rad_1", 1), shift(above[1], "rad_1", -1)]
    below_all = jnp.concatenate(below, 0)
    above_all = jnp.concatenate(above, 0)

    fields, high, low, inner, in_high, in_low, last, in_chain = call(
        first_inner,
        [
            ((stations, cells, width + 8, species), F32),
            (square, BF16),
            (square, BF16),
            (field, F32),
            (square, BF16),
            (square, BF16),
            (edge, F32),
            ((stations, species, species), F32),
        ],
        step * (width + species),
        scalars=1,
    )(mine, block_inverse, above_all, *across, below_all, *got)
    in_next = lax.ppermute(in_chain, "rad_0", [(2, 3)])
    inner_carry = (in_high, in_low)
    arriving = scan(last, inner_carry, in_next, step, [(0, 1), (2, 3)], [(1, 2), (1, 3)], advance_inner)
    out_high, out_low, out_chain = call(
        outer_matrices,
        [(square, BF16), (square, BF16), ((stations, species, species), F32)],
        step * species,
    )(fields, high, low)
    out_next = lax.ppermute(out_chain, "rad_0", [(1, 0)])
    outer_carry = (out_high, out_low)

    for sweep_index in range(SWEEPS):
        if sweep_index:
            count = lax.axis_size("ax")
            up = lax.ppermute(correction, "ax", [(i, i + 1) for i in range(count - 1)])
            down = lax.ppermute(correction, "ax", [(i + 1, i) for i in range(count - 1)])
            inner, last = call(next_inner, [(field, F32), (edge, F32)], step * width)(
                up, correction, down, fields, high, low
            )
            arriving = scan(
                last, inner_carry, in_next, step, [(0, 1), (2, 3)], [(1, 2), (1, 3)], advance_inner
            )
        outer, last = call(outer_local, [(field, F32), (edge, F32)], 2 * step * width)(
            *arriving, inner, *inner_carry, fields, high, low
        )
        arriving = scan(
            last, outer_carry, out_next, step, [(1, 0), (3, 2)], [(2, 1), (2, 0)], advance_outer
        )
        if sweep_index + 1 < SWEEPS:
            (correction,) = call(finish, [(field, F32)], step * width)(
                *arriving, outer, *outer_carry
            )
    message = [(stations, own_cells, width, species)] * GROUP
    sent = call(
        finish_last,
        [(shape, F32) for shape in message],
        step * width,
        scratch=[pltpu.VMEM(field, F32)],
        scalars=1,
    )(mine, *arriving, outer, *outer_carry)
    got = [sent[0]] + [None] * 3
    for ahead in range(1, GROUP):
        got[GROUP - ahead] = shift(sent[ahead], "rad_1", ahead)
    (correction,) = call(
        unpack,
        [(sources.shape, F32)],
        1000,
        scratch=[pltpu.VMEM((columns, species), F32)],
        scalars=1,
    )(mine, *got)
    return correction


def solution(mesh):
    torus = Mesh(mesh.devices.reshape(mesh.shape["ax"], GROUP, GROUP), ("ax", "rad_0", "rad_1"))
    placed = (P("ax", RAD, None, None),) * 4
    return jax.shard_map(
        on_device, mesh=torus, in_specs=placed, out_specs=P("ax", RAD, None, None), check_vma=False
    )
```

time: 242 us -> 142 us (0.59)
  blocking collectives: 122 us -> 0 us
  matrix products: 51.4 us -> 0 us
  starting transfers between devices: 4.68 us -> 40.9 us
  waiting for transfers between devices: 37.7 us -> 72.4 us
  Pallas kernels: 0 us -> 24.6 us
  between operations: 14.3 us -> 0.28 us
  local copies, waits for them, and re-layouts: 10.7 us -> 2.7 us
    all_gather x8 -> x0, blocking collectives: 122 us -> none  [prefix_by_axis(): pieces = jax.tree.map(lambda part: lax.all_gather(part, axis), so_far)]
    ppermute x2 -> x28, waiting for transfers between devices: 6.61 us -> 72.4 us  [the longest x12 29.1 us: shift(): lax.ppermute(value, axis, [(i, (i + step) % count) for i in range(count)])]
    dot_general x65 -> x0, matrix products: 51.4 us -> none  [apply_block(): jnp.einsum('aij,ajk->aik', inverse_row, operand, precision=lax.Precision....]
    ppermute x2 -> x28, starting transfers between devices: 4.55 us -> 40.9 us  [the longest x12 17.5 us: shift(): lax.ppermute(value, axis, [(i, (i + step) % count) for i in range(count)])]
    all_gather x4 -> x0, waiting for transfers between devices: 31.1 us -> none  [prefix_by_axis(): pieces = jax.tree.map(lambda part: lax.all_gather(part, axis), so_far)]
    pallas_call x0 -> x13, Pallas kernels: none -> 24.6 us  [run(): pl.pallas_call(body, out_shape=[jax.ShapeDtypeStruct(shape, kind) for sha...]
    unnamed x110 -> x18, local copies, waits for them, and re-layouts: 7.21 us -> 1.45 us
  transfers between devices with their start and end apart: 6 -> 28, of which waited for: 5 -> 15; matrix products, arithmetic and copies ran while one was open for 12% -> 1% of each run, Pallas kernels for 0% -> 6%
where the time goes in v1:
time: 142 us
  waiting for transfers between devices  72.4 us (51%)
  starting transfers between devices  40.9 us (29%)
  Pallas kernels  24.6 us (17%)
  local copies, waits for them, and re-layouts  2.7 us (2%)
    ppermute x12, waiting for transfers between devices, shift(): lax.ppermute(value, axis, [(i, (i + step) % count) for i in range(count)])  29.1 us
    pallas_call x13, Pallas kernels, run(): pl.pallas_call(body, out_shape=[jax.ShapeDtypeStruct(shape, kind) for sha...  24.6 us
    ppermute x4, waiting for transfers between devices, scan(): near = lax.ppermute(ends, 'rad_0', pairs)  22.1 us
    ppermute x12, starting transfers between devices, shift(): lax.ppermute(value, axis, [(i, (i + step) % count) for i in range(count)])  17.5 us
    ppermute x4, waiting for transfers between devices, scan(): far = lax.ppermute(joined, 'rad_0', [then[1]])  13.2 us
    ppermute x4, starting transfers between devices, scan(): near = lax.ppermute(ends, 'rad_0', pairs)  10.3 us
    ppermute x1, waiting for transfers between devices, on_device(): lax.ppermute(correction, 'ax', [(i + 1, i) for i in range(count - 1)])  4.08 us
    ppermute x4, starting transfers between devices, scan(): far = lax.ppermute(joined, 'rad_0', [then[1]])  3.91 us
  transfers between devices with their start and end apart: 28, of which 15 were waited for; matrix products, arithmetic and copies ran while one was open for 1% of the time, Pallas kernels for 6%

profile of v1, /device:TPU:4, one launch (start us, length us, event | category | flops | bytes accessed | tf_op | source)
XLA Modules:
  0.0 141.9 jit_solution(6681373636294733286)
XLA Ops:
  1.3 1.6 %collective-permute-start.2 = (f32[1,2,200,200]{3,2,1,0:T(8,128)S(1)}, f32[1,2,200,200]{3,2,1,0:T(8,128)S(1)}, u32[]{:S(2)}, u32[]{:S(2)}) collective-permute-start(f32[1,2,200,200]{3,2,1,0:T(8,128)S(1)} %get-tuple-element.55), channel_id=1, source_target_pairs={{0,1},{1,2},{2,3},{3,0},{4,5},{5,6},{6,7},{7,4},{8,9},{9,10},{10,1... | collective-permute-start | bytes 960008 | tf_op jit(solution)/shard_map/ppermute | solution.py:235
  2.9 1.7 %collective-permute-start.1 = (f32[1,2,200,200]{3,2,1,0:T(8,128)S(1)}, f32[1,2,200,200]{3,2,1,0:T(8,128)S(1)}, u32[]{:S(2)}, u32[]{:S(2)}) collective-permute-start(f32[1,2,200,200]{3,2,1,0:T(8,128)S(1)} %get-tuple-element.56), channel_id=1, source_target_pairs={{0,3},{1,0},{2,1},{3,2},{4,7},{5,4},{6,5},{7,6},{8,11},{9,8},{10,9... | collective-permute-start | bytes 960008 | tf_op jit(solution)/shard_map/ppermute | solution.py:235
  4.9 2.9 %collective-permute-start = (f32[1,2,200,200]{3,2,1,0:T(8,128)S(1)}, f32[1,2,200,200]{3,2,1,0:T(8,128)S(1)}, u32[]{:S(2)}, u32[]{:S(2)}) collective-permute-start(f32[1,2,200,200]{3,2,1,0:T(8,128)S(1)} %get-tuple-element.55), channel_id=1, source_target_pairs={{0,3},{1,0},{2,1},{3,2},{4,7},{5,4},{6,5},{7,6},{8,11},{9,8},{10,9... | collective-permute-start | bytes 960008 | tf_op jit(solution)/shard_map/ppermute | solution.py:235
  7.8 7.1 %collective-permute-done.2 = f32[1,2,200,200]{3,2,1,0:T(8,128)S(1)} collective-permute-done((f32[1,2,200,200]{3,2,1,0:T(8,128)S(1)}, f32[1,2,200,200]{3,2,1,0:T(8,128)S(1)}, u32[]{:S(2)}, u32[]{:S(2)}) %collective-permute-start.2) | collective-permute-done | bytes 320032 | tf_op jit(solution)/shard_map/ppermute | solution.py:235
  15.2 2.9 %collective-permute-start.4 = (f32[1,2,200,200]{3,2,1,0:T(8,128)S(1)}, f32[1,2,200,200]{3,2,1,0:T(8,128)S(1)}, u32[]{:S(2)}, u32[]{:S(2)}) collective-permute-start(f32[1,2,200,200]{3,2,1,0:T(8,128)S(1)} %collective-permute-done.1), channel_id=1, source_target_pairs={{0,3},{1,0},{2,1},{3,2},{4,7},{5,4},{6,5},{7,6},{8,11},{9,8},{10,9... | collective-permute-start | bytes 960008 | tf_op jit(solution)/shard_map/ppermute | solution.py:235
  19.0 4.7 %collective-permute-done.5 = f32[1,2,200,200]{3,2,1,0:T(8,128)} collective-permute-done((f32[1,2,200,200]{3,2,1,0:T(8,128)S(1)}, f32[1,2,200,200]{3,2,1,0:T(8,128)}, u32[]{:S(2)}, u32[]{:S(2)}) %collective-permute-start.5) | collective-permute-done | bytes 320032 | tf_op jit(solution)/shard_map/ppermute | solution.py:235
  23.8 2.0 %collective-permute-start.7 = (f32[2,2,40,200]{3,2,1,0:T(8,128)S(1)}, f32[2,2,40,200]{3,2,1,0:T(8,128)S(1)}, u32[]{:S(2)}, u32[]{:S(2)}) collective-permute-start(f32[2,2,40,200]{3,2,1,0:T(8,128)S(1)} %get-tuple-element.32), channel_id=1, source_target_pairs={{0,2},{1,3},{2,0},{3,1},{4,6},{5,7},{6,4},{7,5},{8,10},{9,11},{10,... | collective-permute-start | bytes 384008 | tf_op jit(solution)/shard_map/ppermute | solution.py:235
  27.6 10.1 %collective-permute-done.6.m1 = f32[2,2,40,200]{3,2,1,0:T(8,128)S(1)} collective-permute-done((f32[2,2,40,200]{3,2,1,0:T(8,128)S(1)}, f32[2,2,40,200]{3,2,1,0:T(8,128)S(1)}, u32[]{:S(2)}, u32[]{:S(2)}) %collective-permute-start.6) | collective-permute-done | bytes 128032 | tf_op jit(solution)/shard_map/ppermute | solution.py:235
  38.4 5.2 %first_inner.1 = (f32[2,8,40,200]{3,2,1,0:T(8,128)S(1)}, bf16[2,8,200,200]{3,2,1,0:T(8,128)(2,1)}, bf16[2,8,200,200]{3,2,1,0:T(8,128)(2,1)}, f32[2,8,32,200]{3,2...) custom-call(s32[1]{0:T(128)} %bitcast.mine_ref, ...), custom_call_target="tpu_custom_call" | custom-call | flops 890880000 | bytes 3072004 | tf_op jit(solution)/shard_map/first_inner/pallas_call | solution.py:40
  44.3 1.4 %copy-done = bf16[2,8,200,200]{3,2,1,0:T(8,128)(2,1)S(1)} copy-done((bf16[2,8,200,200]{3,2,1,0:T(8,128)(2,1)S(1)}, bf16[2,8,200,200]{3,2,1,0:T(8,128)(2,1)}, u32[]{:S(2)}) %copy-start) | copy-done | bytes 1280024
  45.7 4.0 %outer_matrices.1 = (bf16[2,8,200,200]{3,2,1,0:T(8,128)(2,1)S(1)}, bf16[2,8,200,200]{3,2,1,0:T(8,128)(2,1)S(1)}, f32[2,200,200]{2,1,0:T(8,128)S(1)}) custom-call(f32[2,8,40,200]{3,2,1,0:T(8,128)S(1)} %get-tuple-element.39.fields, bf16[2,8,200,200]{3,2,1,0:T(8,128)(2,1)S(1)} %copy-done, bf16[2,8,200,200]{3,2,1,0:T(8,128)(2,1)} %get-tuple-element.41.low), custom_call_target="tpu_custom_call" | custom-call | flops 768000000 | bytes 3072000 | tf_op jit(solution)/shard_map/outer_matrices/pallas_call | solution.py:40
  51.0 4.6 %collective-permute-start.9 = (f32[2,32,200]{2,1,0:T(8,128)S(1)}, f32[2,32,200]{2,1,0:T(8,128)S(1)}, u32[]{:S(2)}, u32[]{:S(2)}) collective-permute-start(f32[2,32,200]{2,1,0:T(8,128)S(1)} %get-tuple-element.34.ends), channel_id=1, source_target_pairs={{0,4},{8,12},{1,5},{9,13},{2,6},{10,14},{3,7},{11,15},{16,20},{24,... | collective-permute-start | bytes 153608 | tf_op jit(solution)/shard_map/ppermute | solution.py:240
  55.5 1.9 %collective-permute-done.9.near = f32[2,32,200]{2,1,0:T(8,128)S(1)} collective-permute-done((f32[2,32,200]{2,1,0:T(8,128)S(1)}, f32[2,32,200]{2,1,0:T(8,128)S(1)}, u32[]{:S(2)}, u32[]{:S(2)}) %collective-permute-start.9) | collective-permute-done | bytes 51232 | tf_op jit(solution)/shard_map/ppermute | solution.py:240
  59.0 4.2 %outer_local.2 = (f32[2,8,32,200]{3,2,1,0:T(8,128)S(1)}, f32[2,32,200]{2,1,0:T(8,128)S(1)}) custom-call(f32[2,32,200]{2,1,0:T(8,128)S(1)} %collective-permute-done.9.near, f32[2,32,200]{2,1,0:T(8,128)S(1)} %collective-permute-done.10.middle, f32[2,32,200]{2,1,0:T(8,128)S(1)} %collective-permute-done.11.far, ...), custom_call_target="tpu_custom_call" | custom-call | flops 245760000 | bytes 6515200 | tf_op jit(solution)/shard_map/outer_local/pallas_call | solution.py:40
  64.6 10.7 %collective-permute-done.13.near = f32[2,32,200]{2,1,0:T(8,128)S(1)} collective-permute-done((f32[2,32,200]{2,1,0:T(8,128)S(1)}, f32[2,32,200]{2,1,0:T(8,128)S(1)}, u32[]{:S(2)}, u32[]{:S(2)}) %collective-permute-start.13) | collective-permute-done | bytes 51232 | tf_op jit(solution)/shard_map/ppermute | solution.py:240
  77.4 6.6 %collective-permute-done.15.far = f32[2,32,200]{2,1,0:T(8,128)S(1)} collective-permute-done((f32[2,32,200]{2,1,0:T(8,128)S(1)}, f32[2,32,200]{2,1,0:T(8,128)S(1)}, u32[]{:S(2)}, u32[]{:S(2)}) %collective-permute-start.15) | collective-permute-done | bytes 51232 | tf_op jit(solution)/shard_map/ppermute | solution.py:245
  84.0 1.4 finish.1.own
  85.4 1.9 %collective-permute-start.18 = (f32[2,8,32,200]{3,2,1,0:T(8,128)S(1)}, f32[2,8,32,200]{3,2,1,0:T(8,128)S(1)}, u32[]{:S(2)}, u32[]{:S(2)}) collective-permute-start(f32[2,8,32,200]{3,2,1,0:T(8,128)S(1)} %finish.1.own), channel_id=1, source_target_pairs={{16,0},{32,16},{48,32},{64,48},{80,64},{96,80},{112,96},{17,1},{33... | collective-permute-start | bytes 1228808 | tf_op jit(solution)/shard_map/ppermute | solution.py:311
  87.3 2.6 %collective-permute-start.17 = (f32[2,8,32,200]{3,2,1,0:T(8,128)S(1)}, f32[2,8,32,200]{3,2,1,0:T(8,128)S(1)}, u32[]{:S(2)}, u32[]{:S(2)}) collective-permute-start(f32[2,8,32,200]{3,2,1,0:T(8,128)S(1)} %finish.1.own), channel_id=1, source_target_pairs={{0,16},{16,32},{32,48},{48,64},{64,80},{80,96},{96,112},{1,17},{17... | collective-permute-start | bytes 1228808 | tf_op jit(solution)/shard_map/ppermute | solution.py:310
  89.9 4.1 %collective-permute-done.18.above = f32[2,8,32,200]{3,2,1,0:T(8,128)S(1)} collective-permute-done((f32[2,8,32,200]{3,2,1,0:T(8,128)S(1)}, f32[2,8,32,200]{3,2,1,0:T(8,128)S(1)}, u32[]{:S(2)}, u32[]{:S(2)}) %collective-permute-start.18) | collective-permute-done | bytes 409632 | tf_op jit(solution)/shard_map/ppermute | solution.py:311
  94.0 3.8 %collective-permute-done.17.below = f32[2,8,32,200]{3,2,1,0:T(8,128)S(1)} collective-permute-done((f32[2,8,32,200]{3,2,1,0:T(8,128)S(1)}, f32[2,8,32,200]{3,2,1,0:T(8,128)S(1)}, u32[]{:S(2)}, u32[]{:S(2)}) %collective-permute-start.17) | collective-permute-done | bytes 409632 | tf_op jit(solution)/shard_map/ppermute | solution.py:310
  97.8 2.0 %next_inner.1 = (f32[2,8,32,200]{3,2,1,0:T(8,128)S(1)}, f32[2,32,200]{2,1,0:T(8,128)S(1)}) custom-call(f32[2,8,32,200]{3,2,1,0:T(8,128)S(1)} %collective-permute-done.17.below, f32[2,8,32,200]{3,2,1,0:T(8,128)S(1)} %finish.1.own, f32[2,8,32,200]{3,2,1,0:T(8,128)S(1)} %collective-permute-done.18.above, f32[2,8,40,200]{3,2,1,0:T(8,128)S(1)} %get-tuple-element.39.fields, ...), custom_call_target="tpu_custom_call" | custom-call | flops 122880000 | bytes 4300800 | tf_op jit(solution)/shard_map/next_inner/pallas_call | solution.py:40
  99.9 3.2 %collective-permute-start.19 = (f32[2,32,200]{2,1,0:T(8,128)S(1)}, f32[2,32,200]{2,1,0:T(8,128)S(1)}, u32[]{:S(2)}, u32[]{:S(2)}) collective-permute-start(f32[2,32,200]{2,1,0:T(8,128)S(1)} %get-tuple-element.47.ends), channel_id=1, source_target_pairs={{0,4},{8,12},{1,5},{9,13},{2,6},{10,14},{3,7},{11,15},{16,20},{24,... | collective-permute-start | bytes 153608 | tf_op jit(solution)/shard_map/ppermute | solution.py:240
  103.1 1.9 %collective-permute-done.19.near = f32[2,32,200]{2,1,0:T(8,128)S(1)} collective-permute-done((f32[2,32,200]{2,1,0:T(8,128)S(1)}, f32[2,32,200]{2,1,0:T(8,128)S(1)}, u32[]{:S(2)}, u32[]{:S(2)}) %collective-permute-start.19) | collective-permute-done | bytes 51232 | tf_op jit(solution)/shard_map/ppermute | solution.py:240
  106.5 4.2 %outer_local.3 = (f32[2,8,32,200]{3,2,1,0:T(8,128)S(1)}, f32[2,32,200]{2,1,0:T(8,128)S(1)}) custom-call(f32[2,32,200]{2,1,0:T(8,128)S(1)} %collective-permute-done.19.near, f32[2,32,200]{2,1,0:T(8,128)S(1)} %collective-permute-done.20.middle, f32[2,32,200]{2,1,0:T(8,128)S(1)} %collective-permute-done.21.far, ...), custom_call_target="tpu_custom_call" | custom-call | flops 245760000 | bytes 6515200 | tf_op jit(solution)/shard_map/outer_local/pallas_call | solution.py:40
  112.1 7.7 %collective-permute-done.22.near = f32[2,32,200]{2,1,0:T(8,128)S(1)} collective-permute-done((f32[2,32,200]{2,1,0:T(8,128)S(1)}, f32[2,32,200]{2,1,0:T(8,128)S(1)}, u32[]{:S(2)}, u32[]{:S(2)}) %collective-permute-start.22) | collective-permute-done | bytes 51232 | tf_op jit(solution)/shard_map/ppermute | solution.py:240
  122.0 6.6 %collective-permute-done.24.far = f32[2,32,200]{2,1,0:T(8,128)S(1)} collective-permute-done((f32[2,32,200]{2,1,0:T(8,128)S(1)}, f32[2,32,200]{2,1,0:T(8,128)S(1)}, u32[]{:S(2)}, u32[]{:S(2)}) %collective-permute-start.24) | collective-permute-done | bytes 51232 | tf_op jit(solution)/shard_map/ppermute | solution.py:245
  128.5 1.4 %finish_last.1 = (f32[2,2,32,200]{3,2,1,0:T(8,128)S(1)}, f32[2,2,32,200]{3,2,1,0:T(8,128)S(1)}, f32[2,2,32,200]{3,2,1,0:T(8,128)S(1)}, f32[2,2,32,200]{3,2,1,0:T(8,128)S(1)}) custom-call(s32[1]{0:T(128)} %bitcast.mine_ref, f32[2,32,200]{2,1,0:T(8,128)S(1)} %collective-permute-done.22.near, f32[2,32,200]{2,1,0:T(8,128)S(1)} %collective-permute-done.23.middle, ...), custom_call_target="tpu_custom_call" | custom-call | flops 122880000 | bytes 3443204 | tf_op jit(solution)/shard_map/finish_last/pallas_call | solution.py:40
  130.0 3.0 %collective-permute-start.25 = (f32[2,2,32,200]{3,2,1,0:T(8,128)S(1)}, f32[2,2,32,200]{3,2,1,0:T(8,128)S(1)}, u32[]{:S(2)}, u32[]{:S(2)}) collective-permute-start(f32[2,2,32,200]{3,2,1,0:T(8,128)S(1)} %get-tuple-element.52), channel_id=1, source_target_pairs={{0,3},{1,0},{2,1},{3,2},{4,7},{5,4},{6,5},{7,6},{8,11},{9,8},{10,9... | collective-permute-start | bytes 307208 | tf_op jit(solution)/shard_map/ppermute | solution.py:235
  134.3 2.6 %collective-permute-done.25.m1 = f32[2,2,32,200]{3,2,1,0:T(8,128)S(1)} collective-permute-done((f32[2,2,32,200]{3,2,1,0:T(8,128)S(1)}, f32[2,2,32,200]{3,2,1,0:T(8,128)S(1)}, u32[]{:S(2)}, u32[]{:S(2)}) %collective-permute-start.25) | collective-permute-done | bytes 102432 | tf_op jit(solution)/shard_map/ppermute | solution.py:235
  136.9 2.6 %collective-permute-done.26.m2 = f32[2,2,32,200]{3,2,1,0:T(8,128)S(1)} collective-permute-done((f32[2,2,32,200]{3,2,1,0:T(8,128)S(1)}, f32[2,2,32,200]{3,2,1,0:T(8,128)S(1)}, u32[]{:S(2)}, u32[]{:S(2)}) %collective-permute-start.26) | collective-permute-done | bytes 102432 | tf_op jit(solution)/shard_map/ppermute | solution.py:235
  139.5 1.4 collective-permute-done.27.m3
  (58 shorter events, 19.8 us)
Async XLA Ops:
  0.0 18.1 %copy-start.7 = (f32[2,2,4,200]{3,2,1,0:T(4,128)S(1)}, f32[2,2,4,200]{3,2,1,0:T(4,128)}, u32[]{:S(2)}) copy-start(f32[2,2,4,200]{3,2,1,0:T(4,128)} %axial_ref.1) | copy-start | bytes 38404
  0.0 18.1 %copy-start.8 = (f32[2,2,2,200]{3,2,1,0:T(2,128)S(1)}, f32[2,2,2,200]{3,2,1,0:T(2,128)}, u32[]{:S(2)}) copy-start(f32[2,2,2,200]{3,2,1,0:T(2,128)} %radial_ref.1) | copy-start | bytes 19204
  0.0 18.1 %copy-start.6 = (f32[2,2,200,128]{3,2,1,0:T(8,128)S(1)}, f32[2,2,200,128]{3,2,1,0:T(8,128)}, u32[]{:S(2)}) copy-start(f32[2,2,200,128]{3,2,1,0:T(8,128)} %sources_ref.1) | copy-start | bytes 1228804
  1.3 13.6 %collective-permute-start.2 = (f32[1,2,200,200]{3,2,1,0:T(8,128)S(1)}, f32[1,2,200,200]{3,2,1,0:T(8,128)S(1)}, u32[]{:S(2)}, u32[]{:S(2)}) collective-permute-start(f32[1,2,200,200]{3,2,1,0:T(8,128)S(1)} %get-tuple-element.55), channel_id=1, source_target_pairs={{0,1},{1,2},{2,3},{3,0},{4,5},{5,6},{6,7},{7,4},{8,9},{9,10},{10,1... | collective-permute-start | bytes 960008 | tf_op jit(solution)/shard_map/ppermute | solution.py:235
  2.9 12.3 %collective-permute-start.1 = (f32[1,2,200,200]{3,2,1,0:T(8,128)S(1)}, f32[1,2,200,200]{3,2,1,0:T(8,128)S(1)}, u32[]{:S(2)}, u32[]{:S(2)}) collective-permute-start(f32[1,2,200,200]{3,2,1,0:T(8,128)S(1)} %get-tuple-element.56), channel_id=1, source_target_pairs={{0,3},{1,0},{2,1},{3,2},{4,7},{5,4},{6,5},{7,6},{8,11},{9,8},{10,9... | collective-permute-start | bytes 960008 | tf_op jit(solution)/shard_map/ppermute | solution.py:235
  4.6 19.2 %collective-permute-start.5 = (f32[1,2,200,200]{3,2,1,0:T(8,128)S(1)}, f32[1,2,200,200]{3,2,1,0:T(8,128)}, u32[]{:S(2)}, u32[]{:S(2)}) collective-permute-start(f32[1,2,200,200]{3,2,1,0:T(8,128)S(1)} %get-tuple-element.56), channel_id=1, source_target_pairs={{0,1},{1,2},{2,3},{3,0},{4,5},{5,6},{6,7},{7,4},{8,9},{9,10},{10,1... | collective-permute-start | bytes 960008 | tf_op jit(solution)/shard_map/ppermute | solution.py:235
  4.9 21.9 %collective-permute-start = (f32[1,2,200,200]{3,2,1,0:T(8,128)S(1)}, f32[1,2,200,200]{3,2,1,0:T(8,128)S(1)}, u32[]{:S(2)}, u32[]{:S(2)}) collective-permute-start(f32[1,2,200,200]{3,2,1,0:T(8,128)S(1)} %get-tuple-element.55), channel_id=1, source_target_pairs={{0,3},{1,0},{2,1},{3,2},{4,7},{5,4},{6,5},{7,6},{8,11},{9,8},{10,9... | collective-permute-start | bytes 960008 | tf_op jit(solution)/shard_map/ppermute | solution.py:235
  14.9 23.5 %collective-permute-start.3 = (f32[1,2,200,200]{3,2,1,0:T(8,128)S(1)}, f32[1,2,200,200]{3,2,1,0:T(8,128)S(1)}, u32[]{:S(2)}, u32[]{:S(2)}) collective-permute-start(f32[1,2,200,200]{3,2,1,0:T(8,128)S(1)} %collective-permute-done.2), channel_id=1, source_target_pairs={{0,1},{1,2},{2,3},{3,0},{4,5},{5,6},{6,7},{7,4},{8,9},{9,10},{10,1... | collective-permute-start | bytes 960008 | tf_op jit(solution)/shard_map/ppermute | solution.py:235
  15.2 23.1 %collective-permute-start.4 = (f32[1,2,200,200]{3,2,1,0:T(8,128)S(1)}, f32[1,2,200,200]{3,2,1,0:T(8,128)S(1)}, u32[]{:S(2)}, u32[]{:S(2)}) collective-permute-start(f32[1,2,200,200]{3,2,1,0:T(8,128)S(1)} %collective-permute-done.1), channel_id=1, source_target_pairs={{0,3},{1,0},{2,1},{3,2},{4,7},{5,4},{6,5},{7,6},{8,11},{9,8},{10,9... | collective-permute-start | bytes 960008 | tf_op jit(solution)/shard_map/ppermute | solution.py:235
  18.4 19.4 %collective-permute-start.6 = (f32[2,2,40,200]{3,2,1,0:T(8,128)S(1)}, f32[2,2,40,200]{3,2,1,0:T(8,128)S(1)}, u32[]{:S(2)}, u32[]{:S(2)}) collective-permute-start(f32[2,2,40,200]{3,2,1,0:T(8,128)S(1)} %get-tuple-element.31), channel_id=1, source_target_pairs={{0,3},{1,0},{2,1},{3,2},{4,7},{5,4},{6,5},{7,6},{8,11},{9,8},{10,9... | collective-permute-start | bytes 384008 | tf_op jit(solution)/shard_map/ppermute | solution.py:235
  23.8 14.6 %copy-start.5 = (f32[2,2,200,200]{3,2,1,0:T(8,128)S(1)}, f32[2,2,200,200]{3,2,1,0:T(8,128)}, u32[]{:S(2)}) copy-start(f32[2,2,200,200]{3,2,1,0:T(8,128)} %b0.1) | copy-start | bytes 1920004
  23.8 14.0 %collective-permute-start.7 = (f32[2,2,40,200]{3,2,1,0:T(8,128)S(1)}, f32[2,2,40,200]{3,2,1,0:T(8,128)S(1)}, u32[]{:S(2)}, u32[]{:S(2)}) collective-permute-start(f32[2,2,40,200]{3,2,1,0:T(8,128)S(1)} %get-tuple-element.32), channel_id=1, source_target_pairs={{0,2},{1,3},{2,0},{3,1},{4,6},{5,7},{6,4},{7,5},{8,10},{9,11},{10,... | collective-permute-start | bytes 384008 | tf_op jit(solution)/shard_map/ppermute | solution.py:235
  26.8 11.6 %collective-permute-start.8 = (f32[2,2,40,200]{3,2,1,0:T(8,128)S(1)}, f32[2,2,40,200]{3,2,1,0:T(8,128)S(1)}, u32[]{:S(2)}, u32[]{:S(2)}) collective-permute-start(f32[2,2,40,200]{3,2,1,0:T(8,128)S(1)} %get-tuple-element.33), channel_id=1, source_target_pairs={{0,1},{1,2},{2,3},{3,0},{4,5},{5,6},{6,7},{7,4},{8,9},{9,10},{10,1... | collective-permute-start | bytes 384008 | tf_op jit(solution)/shard_map/ppermute | solution.py:235
  43.6 15.4 %collective-permute-start.12 = (f32[2,200,200]{2,1,0:T(8,128)S(1)}, f32[2,200,200]{2,1,0:T(8,128)S(1)}, u32[]{:S(2)}, u32[]{:S(2)}) collective-permute-start(f32[2,200,200]{2,1,0:T(8,128)S(1)} %get-tuple-element.37), channel_id=1, source_target_pairs={{8,12},{9,13},{10,14},{11,15},{24,28},{25,29},{26,30},{27,31},{40,... | collective-permute-start | bytes 960008 | tf_op jit(solution)/shard_map/ppermute | solution.py:296
  49.7 27.8 %collective-permute-start.16 = (f32[2,200,200]{2,1,0:T(8,128)S(1)}, f32[2,200,200]{2,1,0:T(8,128)S(1)}, u32[]{:S(2)}, u32[]{:S(2)}) collective-permute-start(f32[2,200,200]{2,1,0:T(8,128)S(1)} %get-tuple-element.45), channel_id=1, source_target_pairs={{4,0},{5,1},{6,2},{7,3},{20,16},{21,17},{22,18},{23,19},{36,32},{3... | collective-permute-start | bytes 960008 | tf_op jit(solution)/shard_map/ppermute | solution.py:304
  51.0 6.5 %collective-permute-start.9 = (f32[2,32,200]{2,1,0:T(8,128)S(1)}, f32[2,32,200]{2,1,0:T(8,128)S(1)}, u32[]{:S(2)}, u32[]{:S(2)}) collective-permute-start(f32[2,32,200]{2,1,0:T(8,128)S(1)} %get-tuple-element.34.ends), channel_id=1, source_target_pairs={{0,4},{8,12},{1,5},{9,13},{2,6},{10,14},{3,7},{11,15},{16,20},{24,... | collective-permute-start | bytes 153608 | tf_op jit(solution)/shard_map/ppermute | solution.py:240
  57.7 1.3 collective-permute-start.11
  58.3 0.7 collective-permute-start.10
  63.3 12.0 %collective-permute-start.13 = (f32[2,32,200]{2,1,0:T(8,128)S(1)}, f32[2,32,200]{2,1,0:T(8,128)S(1)}, u32[]{:S(2)}, u32[]{:S(2)}) collective-permute-start(f32[2,32,200]{2,1,0:T(8,128)S(1)} %get-tuple-element.42.ends), channel_id=1, source_target_pairs={{4,0},{12,8},{5,1},{13,9},{6,2},{14,10},{7,3},{15,11},{20,16},{28,... | collective-permute-start | bytes 153608 | tf_op jit(solution)/shard_map/ppermute | solution.py:240
  75.5 8.6 %collective-permute-start.15 = (f32[2,32,200]{2,1,0:T(8,128)S(1)}, f32[2,32,200]{2,1,0:T(8,128)S(1)}, u32[]{:S(2)}, u32[]{:S(2)}) collective-permute-start(f32[2,32,200]{2,1,0:T(8,128)S(1)} %advance_outer.2), channel_id=1, source_target_pairs={{8,0},{9,1},{10,2},{11,3},{24,16},{25,17},{26,18},{27,19},{40,32},... | collective-permute-start | bytes 153608 | tf_op jit(solution)/shard_map/ppermute | solution.py:245
  76.8 7.3 %collective-permute-start.14 = (f32[2,32,200]{2,1,0:T(8,128)S(1)}, f32[2,32,200]{2,1,0:T(8,128)S(1)}, u32[]{:S(2)}, u32[]{:S(2)}) collective-permute-start(f32[2,32,200]{2,1,0:T(8,128)S(1)} %advance_outer.2), channel_id=1, source_target_pairs={{8,4},{9,5},{10,6},{11,7},{24,20},{25,21},{26,22},{27,23},{40,36},... | collective-permute-start | bytes 153608 | tf_op jit(solution)/shard_map/ppermute | solution.py:244
  85.4 8.6 %collective-permute-start.18 = (f32[2,8,32,200]{3,2,1,0:T(8,128)S(1)}, f32[2,8,32,200]{3,2,1,0:T(8,128)S(1)}, u32[]{:S(2)}, u32[]{:S(2)}) collective-permute-start(f32[2,8,32,200]{3,2,1,0:T(8,128)S(1)} %finish.1.own), channel_id=1, source_target_pairs={{16,0},{32,16},{48,32},{64,48},{80,64},{96,80},{112,96},{17,1},{33... | collective-permute-start | bytes 1228808 | tf_op jit(solution)/shard_map/ppermute | solution.py:311
  87.3 10.5 %collective-permute-start.17 = (f32[2,8,32,200]{3,2,1,0:T(8,128)S(1)}, f32[2,8,32,200]{3,2,1,0:T(8,128)S(1)}, u32[]{:S(2)}, u32[]{:S(2)}) collective-permute-start(f32[2,8,32,200]{3,2,1,0:T(8,128)S(1)} %finish.1.own), channel_id=1, source_target_pairs={{0,16},{16,32},{32,48},{48,64},{64,80},{80,96},{96,112},{1,17},{17... | collective-permute-start | bytes 1228808 | tf_op jit(solution)/shard_map/ppermute | solution.py:310
  99.9 5.1 %collective-permute-start.19 = (f32[2,32,200]{2,1,0:T(8,128)S(1)}, f32[2,32,200]{2,1,0:T(8,128)S(1)}, u32[]{:S(2)}, u32[]{:S(2)}) collective-permute-start(f32[2,32,200]{2,1,0:T(8,128)S(1)} %get-tuple-element.47.ends), channel_id=1, source_target_pairs={{0,4},{8,12},{1,5},{9,13},{2,6},{10,14},{3,7},{11,15},{16,20},{24,... | collective-permute-start | bytes 153608 | tf_op jit(solution)/shard_map/ppermute | solution.py:240
  105.2 1.3 collective-permute-start.21
  105.8 0.7 collective-permute-start.20
  110.8 9.0 %collective-permute-start.22 = (f32[2,32,200]{2,1,0:T(8,128)S(1)}, f32[2,32,200]{2,1,0:T(8,128)S(1)}, u32[]{:S(2)}, u32[]{:S(2)}) collective-permute-start(f32[2,32,200]{2,1,0:T(8,128)S(1)} %get-tuple-element.49.ends), channel_id=1, source_target_pairs={{4,0},{12,8},{5,1},{13,9},{6,2},{14,10},{7,3},{15,11},{20,16},{28,... | collective-permute-start | bytes 153608 | tf_op jit(solution)/shard_map/ppermute | solution.py:240
  120.0 8.6 %collective-permute-start.24 = (f32[2,32,200]{2,1,0:T(8,128)S(1)}, f32[2,32,200]{2,1,0:T(8,128)S(1)}, u32[]{:S(2)}, u32[]{:S(2)}) collective-permute-start(f32[2,32,200]{2,1,0:T(8,128)S(1)} %advance_outer.3), channel_id=1, source_target_pairs={{8,0},{9,1},{10,2},{11,3},{24,16},{25,17},{26,18},{27,19},{40,32},... | collective-permute-start | bytes 153608 | tf_op jit(solution)/shard_map/ppermute | solution.py:245
  121.3 7.3 %collective-permute-start.23 = (f32[2,32,200]{2,1,0:T(8,128)S(1)}, f32[2,32,200]{2,1,0:T(8,128)S(1)}, u32[]{:S(2)}, u32[]{:S(2)}) collective-permute-start(f32[2,32,200]{2,1,0:T(8,128)S(1)} %advance_outer.3), channel_id=1, source_target_pairs={{8,4},{9,5},{10,6},{11,7},{24,20},{25,21},{26,22},{27,23},{40,36},... | collective-permute-start | bytes 153608 | tf_op jit(solution)/shard_map/ppermute | solution.py:244
  130.0 6.9 %collective-permute-start.25 = (f32[2,2,32,200]{3,2,1,0:T(8,128)S(1)}, f32[2,2,32,200]{3,2,1,0:T(8,128)S(1)}, u32[]{:S(2)}, u32[]{:S(2)}) collective-permute-start(f32[2,2,32,200]{3,2,1,0:T(8,128)S(1)} %get-tuple-element.52), channel_id=1, source_target_pairs={{0,3},{1,0},{2,1},{3,2},{4,7},{5,4},{6,5},{7,6},{8,11},{9,8},{10,9... | collective-permute-start | bytes 307208 | tf_op jit(solution)/shard_map/ppermute | solution.py:235
  133.0 6.5 %collective-permute-start.26 = (f32[2,2,32,200]{3,2,1,0:T(8,128)S(1)}, f32[2,2,32,200]{3,2,1,0:T(8,128)S(1)}, u32[]{:S(2)}, u32[]{:S(2)}) collective-permute-start(f32[2,2,32,200]{3,2,1,0:T(8,128)S(1)} %get-tuple-element.53), channel_id=1, source_target_pairs={{0,2},{1,3},{2,0},{3,1},{4,6},{5,7},{6,4},{7,5},{8,10},{9,11},{10,... | collective-permute-start | bytes 307208 | tf_op jit(solution)/shard_map/ppermute | solution.py:235
  134.3 6.5 %collective-permute-start.27 = (f32[2,2,32,200]{3,2,1,0:T(8,128)S(1)}, f32[2,2,32,200]{3,2,1,0:T(8,128)S(1)}, u32[]{:S(2)}, u32[]{:S(2)}) collective-permute-start(f32[2,2,32,200]{3,2,1,0:T(8,128)S(1)} %get-tuple-element.54), channel_id=1, source_target_pairs={{0,1},{1,2},{2,3},{3,0},{4,5},{5,6},{6,7},{7,4},{8,9},{9,10},{10,1... | collective-permute-start | bytes 307208 | tf_op jit(solution)/shard_map/ppermute | solution.py:235
  (5 other events, 52.6 us)

commit v2 on v0

v2 whole, which is shorter than its diff:
```python
import jax
import jax.numpy as jnp
from jax import lax
from jax.experimental import pallas as pl
from jax.experimental.pallas import tpu as pltpu
from jax.sharding import Mesh
from jax.sharding import PartitionSpec as P

SWEEPS = 2
RAD = ("rad_0", "rad_1")
GROUP = 4
F32 = jnp.float32
BF16 = jnp.bfloat16


def split(value):
    high = value.astype(BF16)
    return high, (value - high.astype(F32)).astype(BF16)


def dot(a, b, contract):
    dims = (((1,), (contract,)), ((), ()))
    return lax.dot_general(a, b, dims, preferred_element_type=F32)


def times(value, high, low, contract):
    value_high, value_low = split(value)
    return (
        dot(value_high, high, contract)
        + dot(value_low, high, contract)
        + dot(value_high, low, contract)
    )


def call(body, out, scratch=(), scalars=0):
    def run(*operands):
        specs = [pl.BlockSpec(memory_space=pltpu.SMEM)] * scalars
        specs += [pl.BlockSpec(memory_space=pltpu.VMEM)] * (len(operands) - scalars)
        return pl.pallas_call(
            body,
            out_shape=[jax.ShapeDtypeStruct(shape, kind) for shape, kind in out],
            in_specs=specs,
            out_specs=[pl.BlockSpec(memory_space=pltpu.VMEM)] * len(out),
            scratch_shapes=list(scratch),
            cost_estimate=pl.CostEstimate(
                flops=1000, transcendentals=0, bytes_accessed=1000
            ),
            compiler_params=pltpu.CompilerParams(vmem_limit_bytes=12 * 1024 * 1024),
        )(*operands)

    return run


def pack_blocks(block_ref, radial_ref, axial_ref, first, second):
    for station, packed in enumerate((first, second)):
        for cell in range(2):
            packed[200 * cell : 200 * cell + 200] = block_ref[station, cell, :, 0:128]
            packed[400:600, 64 * cell : 64 * cell + 64] = block_ref[station, cell, :, 128:192]
            for chunk in range(7):
                start, stop = 32 * chunk, min(32 * chunk + 32, 200)
                lane = 16 * chunk + 8 * cell
                packed[600 : 600 + stop - start, lane : lane + 8] = block_ref[
                    station, cell, start:stop, 192:200
                ]
            low = 632 + 8 * cell
            packed[low : low + 2] = radial_ref[station, cell, :, 0:128]
            packed[low + 2 : low + 6] = axial_ref[station, cell, :, 0:128]
            packed[low + 16 : low + 18, 0:72] = radial_ref[station, cell, :, 128:200]
            packed[low + 18 : low + 22, 0:72] = axial_ref[station, cell, :, 128:200]


def unpack_block(packed, cell, whole, coupling_whole):
    whole[:, 0:128] = packed[200 * cell : 200 * cell + 200]
    whole[:, 128:192] = packed[400:600, 64 * cell : 64 * cell + 64]
    for chunk in range(7):
        start, stop = 32 * chunk, min(32 * chunk + 32, 200)
        lane = 16 * chunk + 8 * cell
        whole[start:stop, 192:200] = packed[600 : 600 + stop - start, lane : lane + 8]
    low = 632 + 8 * cell
    coupling_whole[:, 0:128] = packed[low : low + 8]
    coupling_whole[:, 128:200] = packed[low + 16 : low + 24, 0:72]
    return split(whole[...]) + (coupling_whole[...],)


def take_near(own0, own1, above0, above1, below0, below1, high, low, coupling, whole, rows):
    for place, pair in enumerate(((own0, own1), (above0, above1), (below0, below1))):
        for station in range(2):
            for cell in range(2):
                block_high, block_low, couple = unpack_block(pair[station], cell, whole, rows)
                high[place, station, cell] = block_high
                low[place, station, cell] = block_low
                coupling[place, station, cell] = couple


def unit_matrix(species):
    rows = lax.broadcasted_iota(jnp.int32, (species, species), 0)
    lanes = lax.broadcasted_iota(jnp.int32, (species, species), 1)
    return jnp.where(rows == lanes, 1.0, 0.0).astype(F32)


def inner_matrices(
    mine_ref, near_high, near_low, near_coupling, across0, across1,
    high, low, coupling, carry, chain, whole, rows,
):
    mine = mine_ref[0]
    for ahead, place in ((0, 0), (1, 1), (3, 2), (2, None)):
        base = lax.rem(mine + ahead, GROUP) * 2
        for station in range(2):
            for cell in range(2):
                if place is None:
                    packed = (across0, across1)[station]
                    parts = unpack_block(packed, cell, whole, rows)
                else:
                    parts = tuple(
                        near[place, station, cell]
                        for near in (near_high, near_low, near_coupling)
                    )
                high[station, base + cell] = parts[0]
                low[station, base + cell] = parts[1]
                coupling[station, base + cell] = parts[2]
    matrix = [unit_matrix(high.shape[2])] * 2
    for cell in range(high.shape[1]):
        for station in range(2):
            inward = coupling[station, cell, 0:1]
            matrix[station] = times(
                -inward * matrix[station], high[station, cell], low[station, cell], 1
            )
            carry[station, cell] = matrix[station]
    for station in range(2):
        chain[station] = matrix[station]


def outer_matrices(high, low, coupling, carry_high, carry_low, chain):
    matrix = [unit_matrix(high.shape[2])] * 2
    for cell in reversed(range(high.shape[1])):
        for station in range(2):
            outward = coupling[station, cell, 1:2]
            matrix[station] = times(
                -outward * matrix[station], high[station, cell], low[station, cell], 1
            )
            part_high, part_low = split(matrix[station])
            carry_high[station, cell] = part_high
            carry_low[station, cell] = part_low
    for station in range(2):
        chain[station] = matrix[station]


def turned_matrices(high, low, coupling, carry, turn_high, turn_low, first):
    matrix = [None, None]
    for cell in reversed(range(high.shape[1])):
        for station in range(2):
            whole = carry[station, cell]
            if matrix[station] is not None:
                outward = coupling[station, cell, 1:2]
                whole = whole - times(
                    outward * matrix[station], high[station, cell], low[station, cell], 1
                )
            matrix[station] = whole
            part_high, part_low = split(whole)
            turn_high[station, cell] = part_high
            turn_low[station, cell] = part_low
    for station in range(2):
        first[station] = matrix[station]


def pack(mine_ref, sources_ref, m0, m1, m2, m3, turned):
    mine = mine_ref[0]
    width = m0.shape[2]
    for station in range(2):
        for cell in range(2):
            turned[...] = sources_ref[station, cell].T
            for ahead, message in enumerate((m0, m1, m2, m3)):
                row = pl.multiple_of(lax.rem(mine + ahead, GROUP) * width, 8)
                message[station, cell] = turned[pl.ds(row, width)]


def first_inner(mine_ref, m0, m1, m2, m3, high, low, coupling, sources, local, last):
    mine = mine_ref[0]
    for station in range(2):
        for ahead, message in enumerate((m0, m1, m2, m3)):
            base = lax.rem(mine + ahead, GROUP) * 2
            for cell in range(2):
                sources[station, base + cell] = message[station, cell]
    inner_chain(lambda station, cell: sources[station, cell], high, low, coupling, local, last)


def inner_chain(source_of, high, low, coupling, local, last):
    value = [None, None]
    for cell in range(high.shape[1]):
        for station in range(2):
            shifted = source_of(station, cell)
            if value[station] is not None:
                shifted = shifted - coupling[station, cell, 0:1] * value[station]
            value[station] = times(shifted, high[station, cell], low[station, cell], 1)
            local[station, cell] = value[station]
    for station in range(2):
        last[station] = value[station]


def next_inner(below, own, above, sources, high, low, coupling, local, last):
    def source_of(station, cell):
        around = [part[s, cell] for part in (below, own, above) for s in range(2)]
        source = sources[station, cell]
        for term, place in enumerate((0, 1, 3, 4)):
            source = source - coupling[station, cell, 2 + term : 3 + term] * around[station + place]
        return source

    inner_chain(source_of, high, low, coupling, local, last)


def outer_local(inner, high, low, coupling, local, last):
    value = [None, None]
    for cell in reversed(range(high.shape[1])):
        for station in range(2):
            whole = inner[station, cell]
            if value[station] is not None:
                shifted = coupling[station, cell, 1:2] * value[station]
                whole = whole - times(shifted, high[station, cell], low[station, cell], 1)
            value[station] = whole
            local[station, cell] = whole
    for station in range(2):
        last[station] = value[station]


def by_matrix(value, matrix):
    high, low = split(matrix)
    return times(value, high, low, 0)


def join_plain(ends, near, chain, joined):
    for station in range(2):
        joined[station] = ends[station] + by_matrix(near[station], chain[station])


def join(place_ref, ends, near, chain, chain_beside, joined):
    outermost = place_ref[0] == 0
    for station in range(2):
        mine, other = ends[station], near[station]
        matrix = jnp.where(outermost, chain_beside[station], chain[station])
        joined[station] = jnp.where(outermost, other, mine) + by_matrix(
            jnp.where(outermost, mine, other), matrix
        )


def incoming(place_ref, near, middle, chain_beside, station):
    place = place_ref[0]
    far = by_matrix(middle[station], chain_beside[station])
    arriving = near[station] + jnp.where(place == GROUP - 1, far, middle[station])
    return jnp.where(place == 0, 0.0, arriving)


def turn_first(near, middle, far, chain_beside, ends, matrix, arriving, turned):
    for station in range(2):
        value = near[station] + middle[station] + by_matrix(far[station], chain_beside[station])
        arriving[station] = value
        turned[station] = ends[station] + by_matrix(value, matrix[station])


def turn(place_ref, near, middle, chain_beside, ends, matrix, arriving, turned):
    for station in range(2):
        value = incoming(place_ref, near, middle, chain_beside, station)
        arriving[station] = value
        turned[station] = ends[station] + by_matrix(value, matrix[station])


def deepen(arriving, outer, turn_high, turn_low, deeper):
    for station in range(2):
        value = arriving[station]
        for cell in range(outer.shape[1]):
            deeper[station, cell] = outer[station, cell] + times(
                value, turn_high[station, cell], turn_low[station, cell], 0
            )


def finish(place_ref, near, middle, chain_beside, outer, carry_high, carry_low, correction):
    for station in range(2):
        arriving = incoming(place_ref, near, middle, chain_beside, station)
        for cell in range(outer.shape[1]):
            correction[station, cell] = outer[station, cell] + times(
                arriving, carry_high[station, cell], carry_low[station, cell], 0
            )


def finish_last(
    place_ref, mine_ref, near, middle, chain_beside, outer, carry_high, carry_low,
    m0, m1, m2, m3, whole,
):
    finish(place_ref, near, middle, chain_beside, outer, carry_high, carry_low, whole)
    mine = mine_ref[0]
    for station in range(2):
        for ahead, message in enumerate((m0, m1, m2, m3)):
            base = lax.rem(mine + ahead, GROUP) * 2
            for cell in range(2):
                message[station, cell] = whole[station, base + cell]


def unpack(mine_ref, m0, m1, m2, m3, correction, turned):
    mine = mine_ref[0]
    width = m0.shape[2]
    for station in range(2):
        for cell in range(2):
            for ahead, message in enumerate((m0, m1, m2, m3)):
                row = pl.multiple_of(lax.rem(mine + ahead, GROUP) * width, 8)
                turned[pl.ds(row, width)] = message[station, cell]
            correction[station, cell] = turned[...].T


def shift(value, axis, step):
    count = lax.axis_size(axis)
    return lax.ppermute(value, axis, [(i, (i + step) % count) for i in range(count)])


def hop(value, pairs):
    return lax.ppermute(value, "rad_0", pairs)


def mirrored(pairs):
    return [(GROUP - 1 - source, GROUP - 1 - target) for source, target in pairs]


def relax(sources, block_inverse, radial_coupling, axial_coupling):
    stations, own_cells, species, columns = sources.shape
    cells = own_cells * GROUP
    width = columns // GROUP
    mine = lax.axis_index("rad_1").astype(jnp.int32).reshape(1)
    place = lax.axis_index("rad_0").astype(jnp.int32).reshape(1)
    places = (place, GROUP - 1 - place)
    field = ((stations, cells, width, species), F32)
    square = ((stations, cells, species, species), BF16)
    wide = ((stations, cells, species, species), F32)
    edge = ((stations, width, species), F32)
    single = ((stations, species, species), F32)
    message = [((stations, own_cells, width, species), F32)] * GROUP
    rows = [pltpu.VMEM((species, species), F32), pltpu.VMEM((8, species), F32)]

    own = call(pack_blocks, [((664, 128), F32)] * 2)(block_inverse, radial_coupling, axial_coupling)
    below = [shift(own[0], "rad_1", 1), None]
    above = [None, shift(own[1], "rad_1", -1)]
    below[1] = shift(own[1], "rad_1", 1)
    above[0] = shift(own[0], "rad_1", -1)
    across = [shift(below[0], "rad_1", 1)]
    across += [shift(above[1], "rad_1", -1)]
    sent = call(
        pack, message, scratch=[pltpu.VMEM((columns, species), F32)], scalars=1
    )(mine, sources)
    got = [sent[0]] + [None] * 3
    for ahead in range(1, GROUP):
        got[GROUP - ahead] = shift(sent[ahead], "rad_1", ahead)
    near_shape = (3, stations, own_cells, species, species)
    taken = call(
        take_near,
        [(near_shape, BF16)] * 2 + [((3, stations, own_cells, 8, species), F32)],
        scratch=rows,
    )(*own, *above, *below)
    high, low, coupling, carry, in_chain = call(
        inner_matrices,
        [square, square, ((stations, cells, 8, species), F32), wide, single],
        scratch=rows,
        scalars=1,
    )(mine, *taken, *across)
    system = (high, low, coupling)
    beside = [(1, 0), (2, 3)]
    in_beside = hop(in_chain, beside)

    source, inner, last = call(first_inner, [field, field, edge], scalars=1)(mine, *got, *system)
    near = hop(last, [(0, 1), (2, 3)])
    out_high, out_low, out_chain = call(outer_matrices, [square, square, single])(*system)
    out_beside = hop(out_chain, beside)
    (joined,) = call(join_plain, [edge])(last, near, in_chain)
    middle = hop(joined, [(1, 2)])
    far = hop(joined, [(1, 3)])
    turn_high, turn_low, turn_chain = call(
        turned_matrices, [square, square, single]
    )(*system, carry)
    outer, ends = call(outer_local, [field, edge])(inner, *system)
    arriving, last = call(turn_first, [edge, edge])(near, middle, far, in_beside, ends, turn_chain)

    for sweep_index in range(SWEEPS):
        if sweep_index:
            count = lax.axis_size("ax")
            up = lax.ppermute(correction, "ax", [(i, i + 1) for i in range(count - 1)])
            down = lax.ppermute(correction, "ax", [(i + 1, i) for i in range(count - 1)])
            inner, last = call(next_inner, [field, edge])(up, correction, down, source, *system)
            near = hop(last, [(0, 1), (1, 0), (2, 3)])
            outer, ends = call(outer_local, [field, edge])(inner, *system)
            (joined,) = call(join, [edge], scalars=1)(places[0], last, near, in_chain, in_beside)
            middle = hop(joined, [(1, 2), (0, 3)])
            arriving, last = call(turn, [edge, edge], scalars=1)(
                places[0], near, middle, in_beside, ends, turn_chain
            )
        near = hop(last, mirrored([(0, 1), (1, 0), (2, 3)]))
        (outer,) = call(deepen, [field])(arriving, outer, turn_high, turn_low)
        (joined,) = call(join, [edge], scalars=1)(places[1], last, near, out_chain, out_beside)
        middle = hop(joined, mirrored([(1, 2), (0, 3)]))
        reach = (near, middle, out_beside, outer, out_high, out_low)
        if sweep_index + 1 < SWEEPS:
            (correction,) = call(finish, [field], scalars=1)(places[1], *reach)
    sent = call(
        finish_last, message, scratch=[pltpu.VMEM(*field)], scalars=2
    )(places[1], mine, *reach)
    got = [sent[0]] + [None] * 3
    for ahead in range(1, GROUP):
        got[GROUP - ahead] = shift(sent[ahead], "rad_1", ahead)
    (correction,) = call(
        unpack, [(sources.shape, F32)], scratch=[pltpu.VMEM((columns, species), F32)], scalars=1
    )(mine, *got)
    return correction


def solution(mesh):
    torus = Mesh(mesh.devices.reshape(mesh.shape["ax"], GROUP, GROUP), ("ax", "rad_0", "rad_1"))
    placed = (P("ax", RAD, None, None),) * 4
    return jax.shard_map(
        relax, mesh=torus, in_specs=placed, out_specs=P("ax", RAD, None, None), check_vma=False
    )
```

time: 242 us -> 148 us (0.61)
  blocking collectives: 122 us -> 0 us
  matrix products: 51.4 us -> 0 us
  starting transfers between devices: 4.68 us -> 40.7 us
  Pallas kernels: 0 us -> 29.4 us
  waiting for transfers between devices: 37.7 us -> 63.6 us
  between operations: 14.3 us -> 0.38 us
    all_gather x8 -> x0, blocking collectives: 122 us -> none  [prefix_by_axis(): pieces = jax.tree.map(lambda part: lax.all_gather(part, axis), so_far)]
    ppermute x2 -> x25, waiting for transfers between devices: 6.61 us -> 63.6 us  [the longest x12 29.6 us: shift(): lax.ppermute(value, axis, [(i, (i + step) % count) for i in range(count)])]
    dot_general x65 -> x0, matrix products: 51.4 us -> none  [apply_block(): jnp.einsum('aij,ajk->aik', inverse_row, operand, precision=lax.Precision....]
    ppermute x2 -> x25, starting transfers between devices: 4.55 us -> 40.7 us  [the longest x11 22 us: hop(): return lax.ppermute(value, 'rad_0', pairs)]
    all_gather x4 -> x0, waiting for transfers between devices: 31.1 us -> none  [prefix_by_axis(): pieces = jax.tree.map(lambda part: lax.all_gather(part, axis), so_far)]
    pallas_call x0 -> x21, Pallas kernels: none -> 29.4 us  [run(): pl.pallas_call(body, out_shape=[jax.ShapeDtypeStruct(shape, kind) for sha...]
    unnamed x110 -> x56, local copies, waits for them, and re-layouts: 7.21 us -> 13.1 us
  transfers between devices with their start and end apart: 6 -> 25, of which waited for: 5 -> 17; matrix products, arithmetic and copies ran while one was open for 12% -> 0% of each run, Pallas kernels for 0% -> 10%
where the time goes in v2:
time: 148 us; the launch traced here: 147 us
  waiting for transfers between devices  63.6 us (43%)
  starting transfers between devices  40.7 us (28%)
  Pallas kernels  29.4 us (20%)
  local copies, waits for them, and re-layouts  13.1 us (9%)
    ppermute x12, waiting for transfers between devices, shift(): lax.ppermute(value, axis, [(i, (i + step) % count) for i in range(count)])  29.6 us
    pallas_call x21, Pallas kernels, run(): pl.pallas_call(body, out_shape=[jax.ShapeDtypeStruct(shape, kind) for sha...  29.4 us
    ppermute x11, waiting for transfers between devices, hop(): return lax.ppermute(value, 'rad_0', pairs)  25.9 us
    ppermute x11, starting transfers between devices, hop(): return lax.ppermute(value, 'rad_0', pairs)  22 us
    ppermute x12, starting transfers between devices, shift(): lax.ppermute(value, axis, [(i, (i + step) % count) for i in range(count)])  14.3 us
    unnamed x56, local copies, waits for them, and re-layouts  13.1 us
    ppermute x1, waiting for transfers between devices, relax(): lax.ppermute(correction, 'ax', [(i + 1, i) for i in range(count - 1)])  4.26 us
    ppermute x1, waiting for transfers between devices, relax(): up = lax.ppermute(correction, 'ax', [(i, i + 1) for i in range(count - 1)])  3.82 us
  transfers between devices with their start and end apart: 25, of which 17 were waited for; matrix products, arithmetic and copies ran while one was open for 0% of the time, Pallas kernels for 10%

profile of v2, /device:TPU:4, one launch (start us, length us, event | category | flops | bytes accessed | tf_op | source)
XLA Modules:
  0.0 147.2 jit_solution(8930040901592037959)
XLA Ops:
  4.4 1.7 %collective-permute-start.4 = (f32[664,128]{1,0:T(8,128)S(1)}, f32[664,128]{1,0:T(8,128)S(1)}, u32[]{:S(2)}, u32[]{:S(2)}) collective-permute-start(f32[664,128]{1,0:T(8,128)S(1)} %get-tuple-element.47.own1), channel_id=1, source_target_pairs={{0,3},{1,0},{2,1},{3,2},{4,7},{5,4},{6,5},{7,6},{8,11},{9,8},{10,9... | collective-permute-start | bytes 1019912 | tf_op jit(solution)/shard_map/ppermute | solution.py:310
  6.1 1.8 %collective-permute-start.3 = (f32[664,128]{1,0:T(8,128)S(1)}, f32[664,128]{1,0:T(8,128)S(1)}, u32[]{:S(2)}, u32[]{:S(2)}) collective-permute-start(f32[664,128]{1,0:T(8,128)S(1)} %get-tuple-element.46.own0), channel_id=1, source_target_pairs={{0,3},{1,0},{2,1},{3,2},{4,7},{5,4},{6,5},{7,6},{8,11},{9,8},{10,9... | collective-permute-start | bytes 1019912 | tf_op jit(solution)/shard_map/ppermute | solution.py:310
  8.1 6.8 %collective-permute-done.5.below0 = f32[664,128]{1,0:T(8,128)S(1)} collective-permute-done((f32[664,128]{1,0:T(8,128)S(1)}, f32[664,128]{1,0:T(8,128)S(1)}, u32[]{:S(2)}, u32[]{:S(2)}) %collective-permute-start.5) | collective-permute-done | bytes 340000 | tf_op jit(solution)/shard_map/ppermute | solution.py:310
  15.3 2.9 %collective-permute-start.8 = (f32[664,128]{1,0:T(8,128)S(1)}, f32[664,128]{1,0:T(8,128)S(1)}, u32[]{:S(2)}, u32[]{:S(2)}) collective-permute-start(f32[664,128]{1,0:T(8,128)S(1)} %collective-permute-done.4.above1), channel_id=1, source_target_pairs={{0,3},{1,0},{2,1},{3,2},{4,7},{5,4},{6,5},{7,6},{8,11},{9,8},{10,9... | collective-permute-start | bytes 1019912 | tf_op jit(solution)/shard_map/ppermute | solution.py:310
  18.1 4.4 %collective-permute-done.3.above0 = f32[664,128]{1,0:T(8,128)S(1)} collective-permute-done((f32[664,128]{1,0:T(8,128)S(1)}, f32[664,128]{1,0:T(8,128)S(1)}, u32[]{:S(2)}, u32[]{:S(2)}) %collective-permute-start.3) | collective-permute-done | bytes 340000 | tf_op jit(solution)/shard_map/ppermute | solution.py:310
  23.3 5.2 %collective-permute-done.7.across0 = f32[664,128]{1,0:T(8,128)S(1)} collective-permute-done((f32[664,128]{1,0:T(8,128)S(1)}, f32[664,128]{1,0:T(8,128)S(1)}, u32[]{:S(2)}, u32[]{:S(2)}) %collective-permute-start.7) | collective-permute-done | bytes 340000 | tf_op jit(solution)/shard_map/ppermute | solution.py:310
  31.8 2.5 %shard_map.49 = (bf16[2,8,200,200]{3,2,1,0:T(8,128)(2,1)S(1)}, bf16[2,8,200,200]{3,2,1,0:T(8,128)(2,1)S(1)}, f32[2,8,8,200]{3,2,1,0:T(8,128)S(1)}, f32[2,8,200,200]{3,2,1,0:T(8,128)S(1)}, f32[2,200,200]{2,1,0:T(8,128)S(1)}) custom-call(s32[1]{0:T(128)} %bitcast.mine_ref, bf16[3,2,2,200,200]{4,3,2,1,0:T(8,128)(2,1)S(1)} %get-tuple-element.48.near_high, ...), custom_call_target="tpu_custom_call" | custom-call | flops 1000 | bytes 1000 | tf_op jit(solution)/shard_map/pallas_call | solution.py:39
  35.6 3.1 %shard_map.55 = (bf16[2,8,200,200]{3,2,1,0:T(8,128)(2,1)S(1)}, bf16[2,8,200,200]{3,2,1,0:T(8,128)(2,1)S(1)}, f32[2,200,200]{2,1,0:T(8,128)}) custom-call(bf16[2,8,200,200]{3,2,1,0:T(8,128)(2,1)S(1)} %get-tuple-element.51.high, bf16[2,8,200,200]{3,2,1,0:T(8,128)(2,1)S(1)} %get-tuple-element.52.low, f32[2,8,8,200]{3,2,1,0:T(8,128)S(1)} %get-tuple-element.53.coupling), custom_call_target="tpu_custom_call" | custom-call | flops 1000 | bytes 1000 | tf_op jit(solution)/shard_map/pallas_call | solution.py:39
  42.7 2.4 %collective-permute-start = (f32[2,2,32,200]{3,2,1,0:T(8,128)S(1)}, f32[2,2,32,200]{3,2,1,0:T(8,128)S(1)}, u32[]{:S(2)}, u32[]{:S(2)}) collective-permute-start(f32[2,2,32,200]{3,2,1,0:T(8,128)S(1)} %get-tuple-element.43), channel_id=1, source_target_pairs={{0,3},{1,0},{2,1},{3,2},{4,7},{5,4},{6,5},{7,6},{8,11},{9,8},{10,9... | collective-permute-start | bytes 307208 | tf_op jit(solution)/shard_map/ppermute | solution.py:310
  46.4 3.3 %collective-permute-done.m1 = f32[2,2,32,200]{3,2,1,0:T(8,128)S(1)} collective-permute-done((f32[2,2,32,200]{3,2,1,0:T(8,128)S(1)}, f32[2,2,32,200]{3,2,1,0:T(8,128)S(1)}, u32[]{:S(2)}, u32[]{:S(2)}) %collective-permute-start) | collective-permute-done | bytes 102432 | tf_op jit(solution)/shard_map/ppermute | solution.py:310
  49.7 2.3 %collective-permute-done.1.m2 = f32[2,2,32,200]{3,2,1,0:T(8,128)S(1)} collective-permute-done((f32[2,2,32,200]{3,2,1,0:T(8,128)S(1)}, f32[2,2,32,200]{3,2,1,0:T(8,128)S(1)}, u32[]{:S(2)}, u32[]{:S(2)}) %collective-permute-start.1) | collective-permute-done | bytes 102432 | tf_op jit(solution)/shard_map/ppermute | solution.py:310
  53.3 2.0 %shard_map.50 = (f32[2,8,32,200]{3,2,1,0:T(8,128)S(1)}, f32[2,8,32,200]{3,2,1,0:T(8,128)S(1)}, f32[2,32,200]{2,1,0:T(8,128)S(1)}) custom-call(s32[1]{0:T(128)} %bitcast.mine_ref, f32[2,2,32,200]{3,2,1,0:T(8,128)S(1)} %get-tuple-element.42.m0, f32[2,2,32,200]{3,2,1,0:T(8,128)S(1)} %collective-permute-done.m1, ...), custom_call_target="tpu_custom_call" | custom-call | flops 1000 | bytes 1000 | tf_op jit(solution)/shard_map/pallas_call | solution.py:39
  55.3 5.2 %collective-permute-start.9 = (f32[2,32,200]{2,1,0:T(8,128)S(1)}, f32[2,32,200]{2,1,0:T(8,128)S(1)}, u32[]{:S(2)}, u32[]{:S(2)}) collective-permute-start(f32[2,32,200]{2,1,0:T(8,128)S(1)} %get-tuple-element.54.ends), channel_id=1, source_target_pairs={{0,4},{8,12},{1,5},{9,13},{2,6},{10,14},{3,7},{11,15},{16,20},{24,... | collective-permute-start | bytes 153608 | tf_op jit(solution)/shard_map/ppermute | solution.py:314
  60.5 1.9 %collective-permute-done.9.near = f32[2,32,200]{2,1,0:T(8,128)S(1)} collective-permute-done((f32[2,32,200]{2,1,0:T(8,128)S(1)}, f32[2,32,200]{2,1,0:T(8,128)S(1)}, u32[]{:S(2)}, u32[]{:S(2)}) %collective-permute-start.9) | collective-permute-done | bytes 51232 | tf_op jit(solution)/shard_map/ppermute | solution.py:314
  64.0 2.2 %shard_map.53 = (bf16[2,8,200,200]{3,2,1,0:T(8,128)(2,1)S(1)}, bf16[2,8,200,200]{3,2,1,0:T(8,128)(2,1)S(1)}, f32[2,200,200]{2,1,0:T(8,128)S(1)}) custom-call(bf16[2,8,200,200]{3,2,1,0:T(8,128)(2,1)S(1)} %get-tuple-element.51.high, bf16[2,8,200,200]{3,2,1,0:T(8,128)(2,1)S(1)} %get-tuple-element.52.low, f32[2,8,8,200]{3,2,1,0:T(8,128)S(1)} %get-tuple-element.53.coupling, ...), custom_call_target="tpu_custom_call" | custom-call | flops 1000 | bytes 1000 | tf_op jit(solution)/shard_map/pallas_call | solution.py:39
  66.3 1.8 %shard_map.52 = (f32[2,8,32,200]{3,2,1,0:T(8,128)S(1)}, f32[2,32,200]{2,1,0:T(8,128)S(1)}) custom-call(f32[2,8,32,200]{3,2,1,0:T(8,128)S(1)} %get-tuple-element.56.inner, bf16[2,8,200,200]{3,2,1,0:T(8,128)(2,1)S(1)} %get-tuple-element.51.high, bf16[2,8,200,200]{3,2,1,0:T(8,128)(2,1)S(1)} %get-tuple-element.52.low, ...), custom_call_target="tpu_custom_call" | custom-call | flops 1000 | bytes 1000 | tf_op jit(solution)/shard_map/pallas_call | solution.py:39
  71.3 8.9 %collective-permute-done.13.near = f32[2,32,200]{2,1,0:T(8,128)S(1)} collective-permute-done((f32[2,32,200]{2,1,0:T(8,128)}, f32[2,32,200]{2,1,0:T(8,128)S(1)}, u32[]{:S(2)}, u32[]{:S(2)}) %collective-permute-start.13) | collective-permute-done | bytes 51232 | tf_op jit(solution)/shard_map/ppermute | solution.py:314
  89.0 2.4 %shard_map.58.own = f32[2,8,32,200]{3,2,1,0:T(8,128)S(1)} custom-call(s32[1]{0:T(128)S(6)} %sub.3.place_ref, f32[2,32,200]{2,1,0:T(8,128)S(1)} %collective-permute-done.13.near, f32[2,32,200]{2,1,0:T(8,128)S(1)} %collective-permute-done.15.middle, f32[2,200,200]{2,1,0:T(8,128)} %collective-permute-done.14.chain_beside, ...), custom_call_target="tpu_custom_call" | custom-call | flops 1000 | bytes 1000 | tf_op jit(solution)/shard_map/pallas_call | solution.py:39
  91.4 1.9 %collective-permute-start.17 = (f32[2,8,32,200]{3,2,1,0:T(8,128)S(1)}, f32[2,8,32,200]{3,2,1,0:T(8,128)S(1)}, u32[]{:S(2)}, u32[]{:S(2)}) collective-permute-start(f32[2,8,32,200]{3,2,1,0:T(8,128)S(1)} %shard_map.58.own), channel_id=1, source_target_pairs={{16,0},{32,16},{48,32},{64,48},{80,64},{96,80},{112,96},{17,1},{33... | collective-permute-start | bytes 1228808 | tf_op jit(solution)/shard_map/ppermute | solution.py:382
  93.3 2.4 %collective-permute-start.16 = (f32[2,8,32,200]{3,2,1,0:T(8,128)S(1)}, f32[2,8,32,200]{3,2,1,0:T(8,128)S(1)}, u32[]{:S(2)}, u32[]{:S(2)}) collective-permute-start(f32[2,8,32,200]{3,2,1,0:T(8,128)S(1)} %shard_map.58.own), channel_id=1, source_target_pairs={{0,16},{16,32},{32,48},{48,64},{64,80},{80,96},{96,112},{1,17},{17... | collective-permute-start | bytes 1228808 | tf_op jit(solution)/shard_map/ppermute | solution.py:381
  95.8 4.3 %collective-permute-done.17.above = f32[2,8,32,200]{3,2,1,0:T(8,128)S(1)} collective-permute-done((f32[2,8,32,200]{3,2,1,0:T(8,128)S(1)}, f32[2,8,32,200]{3,2,1,0:T(8,128)S(1)}, u32[]{:S(2)}, u32[]{:S(2)}) %collective-permute-start.17) | collective-permute-done | bytes 409632 | tf_op jit(solution)/shard_map/ppermute | solution.py:382
  100.0 3.8 %collective-permute-done.16.below = f32[2,8,32,200]{3,2,1,0:T(8,128)S(1)} collective-permute-done((f32[2,8,32,200]{3,2,1,0:T(8,128)S(1)}, f32[2,8,32,200]{3,2,1,0:T(8,128)S(1)}, u32[]{:S(2)}, u32[]{:S(2)}) %collective-permute-start.16) | collective-permute-done | bytes 409632 | tf_op jit(solution)/shard_map/ppermute | solution.py:381
  103.8 2.0 %shard_map.59 = (f32[2,8,32,200]{3,2,1,0:T(8,128)S(1)}, f32[2,32,200]{2,1,0:T(8,128)S(1)}) custom-call(f32[2,8,32,200]{3,2,1,0:T(8,128)S(1)} %collective-permute-done.16.below, f32[2,8,32,200]{3,2,1,0:T(8,128)S(1)} %shard_map.58.own, f32[2,8,32,200]{3,2,1,0:T(8,128)S(1)} %collective-permute-done.17.above, f32[2,8,32,200]{3,2,1,0:T(8,128)S(1)} %copy-done.20, ...), custom_call_target="tpu_custom_call" | custom-call | flops 1000 | bytes 1000 | tf_op jit(solution)/shard_map/pallas_call | solution.py:39
  105.9 1.9 %collective-permute-start.18 = (f32[2,32,200]{2,1,0:T(8,128)S(1)}, f32[2,32,200]{2,1,0:T(8,128)S(1)}, u32[]{:S(2)}, u32[]{:S(2)}) collective-permute-start(f32[2,32,200]{2,1,0:T(8,128)S(1)} %get-tuple-element.69.ends), channel_id=1, source_target_pairs={{0,4},{4,0},{8,12},{1,5},{5,1},{9,13},{2,6},{6,2},{10,14},{3,7},{7... | collective-permute-start | bytes 153608 | tf_op jit(solution)/shard_map/ppermute | solution.py:314
  107.8 4.2 %collective-permute-done.18.near = f32[2,32,200]{2,1,0:T(8,128)S(1)} collective-permute-done((f32[2,32,200]{2,1,0:T(8,128)S(1)}, f32[2,32,200]{2,1,0:T(8,128)S(1)}, u32[]{:S(2)}, u32[]{:S(2)}) %collective-permute-start.18) | collective-permute-done | bytes 51232 | tf_op jit(solution)/shard_map/ppermute | solution.py:314
  112.3 5.7 %collective-permute-start.19 = (f32[2,32,200]{2,1,0:T(8,128)S(1)}, f32[2,32,200]{2,1,0:T(8,128)S(1)}, u32[]{:S(2)}, u32[]{:S(2)}) collective-permute-start(f32[2,32,200]{2,1,0:T(8,128)S(1)} %shard_map.60), channel_id=1, source_target_pairs={{4,8},{0,12},{5,9},{1,13},{6,10},{2,14},{7,11},{3,15},{20,24},{16,... | collective-permute-start | bytes 153608 | tf_op jit(solution)/shard_map/ppermute | solution.py:314
  118.0 1.8 %shard_map.61 = (f32[2,8,32,200]{3,2,1,0:T(8,128)S(1)}, f32[2,32,200]{2,1,0:T(8,128)S(1)}) custom-call(f32[2,8,32,200]{3,2,1,0:T(8,128)S(1)} %get-tuple-element.70.inner, bf16[2,8,200,200]{3,2,1,0:T(8,128)(2,1)S(1)} %get-tuple-element.51.high, bf16[2,8,200,200]{3,2,1,0:T(8,128)(2,1)S(1)} %get-tuple-element.52.low, ...), custom_call_target="tpu_custom_call" | custom-call | flops 1000 | bytes 1000 | tf_op jit(solution)/shard_map/pallas_call | solution.py:39
  121.7 4.9 %collective-permute-done.20.near = f32[2,32,200]{2,1,0:T(8,128)S(1)} collective-permute-done((f32[2,32,200]{2,1,0:T(8,128)S(1)}, f32[2,32,200]{2,1,0:T(8,128)S(1)}, u32[]{:S(2)}, u32[]{:S(2)}) %collective-permute-start.20) | collective-permute-done | bytes 51232 | tf_op jit(solution)/shard_map/ppermute | solution.py:314
  130.2 5.0 %collective-permute-done.21.middle = f32[2,32,200]{2,1,0:T(8,128)S(1)} collective-permute-done((f32[2,32,200]{2,1,0:T(8,128)S(1)}, f32[2,32,200]{2,1,0:T(8,128)S(1)}, u32[]{:S(2)}, u32[]{:S(2)}) %collective-permute-start.21) | collective-permute-done | bytes 51232 | tf_op jit(solution)/shard_map/ppermute | solution.py:314
  135.3 2.4 %shard_map.65 = (f32[2,2,32,200]{3,2,1,0:T(8,128)S(1)}, f32[2,2,32,200]{3,2,1,0:T(8,128)S(1)}, f32[2,2,32,200]{3,2,1,0:T(8,128)S(1)}, f32[2,2,32,200]{3,2,1,0:T(8,128)S(1)}) custom-call(s32[1]{0:T(128)S(6)} %sub.3.place_ref, s32[1]{0:T(128)} %bitcast.mine_ref, f32[2,32,200]{2,1,0:T(8,128)S(1)} %collective-permute-done.20.near, ...), custom_call_target="tpu_custom_call" | custom-call | flops 1000 | bytes 1000 | tf_op jit(solution)/shard_map/pallas_call | solution.py:39
  139.8 2.9 %collective-permute-done.22.m1 = f32[2,2,32,200]{3,2,1,0:T(8,128)S(1)} collective-permute-done((f32[2,2,32,200]{3,2,1,0:T(8,128)S(1)}, f32[2,2,32,200]{3,2,1,0:T(8,128)S(1)}, u32[]{:S(2)}, u32[]{:S(2)}) %collective-permute-start.22) | collective-permute-done | bytes 102432 | tf_op jit(solution)/shard_map/ppermute | solution.py:310
  142.7 2.2 %collective-permute-done.23.m2 = f32[2,2,32,200]{3,2,1,0:T(8,128)S(1)} collective-permute-done((f32[2,2,32,200]{3,2,1,0:T(8,128)S(1)}, f32[2,2,32,200]{3,2,1,0:T(8,128)S(1)}, u32[]{:S(2)}, u32[]{:S(2)}) %collective-permute-start.23) | collective-permute-done | bytes 102432 | tf_op jit(solution)/shard_map/ppermute | solution.py:310
  (95 shorter events, 40.6 us)
Async XLA Ops:
  2.8 12.1 %collective-permute-start.5 = (f32[664,128]{1,0:T(8,128)S(1)}, f32[664,128]{1,0:T(8,128)S(1)}, u32[]{:S(2)}, u32[]{:S(2)}) collective-permute-start(f32[664,128]{1,0:T(8,128)S(1)} %get-tuple-element.46.own0), channel_id=1, source_target_pairs={{0,1},{1,2},{2,3},{3,0},{4,5},{5,6},{6,7},{7,4},{8,9},{9,10},{10,1... | collective-permute-start | bytes 1019912 | tf_op jit(solution)/shard_map/ppermute | solution.py:310
  4.4 10.8 %collective-permute-start.4 = (f32[664,128]{1,0:T(8,128)S(1)}, f32[664,128]{1,0:T(8,128)S(1)}, u32[]{:S(2)}, u32[]{:S(2)}) collective-permute-start(f32[664,128]{1,0:T(8,128)S(1)} %get-tuple-element.47.own1), channel_id=1, source_target_pairs={{0,3},{1,0},{2,1},{3,2},{4,7},{5,4},{6,5},{7,6},{8,11},{9,8},{10,9... | collective-permute-start | bytes 1019912 | tf_op jit(solution)/shard_map/ppermute | solution.py:310
  6.1 16.5 %collective-permute-start.3 = (f32[664,128]{1,0:T(8,128)S(1)}, f32[664,128]{1,0:T(8,128)S(1)}, u32[]{:S(2)}, u32[]{:S(2)}) collective-permute-start(f32[664,128]{1,0:T(8,128)S(1)} %get-tuple-element.46.own0), channel_id=1, source_target_pairs={{0,3},{1,0},{2,1},{3,2},{4,7},{5,4},{6,5},{7,6},{8,11},{9,8},{10,9... | collective-permute-start | bytes 1019912 | tf_op jit(solution)/shard_map/ppermute | solution.py:310
  7.9 14.7 %collective-permute-start.6 = (f32[664,128]{1,0:T(8,128)S(1)}, f32[664,128]{1,0:T(8,128)S(1)}, u32[]{:S(2)}, u32[]{:S(2)}) collective-permute-start(f32[664,128]{1,0:T(8,128)S(1)} %get-tuple-element.47.own1), channel_id=1, source_target_pairs={{0,1},{1,2},{2,3},{3,0},{4,5},{5,6},{6,7},{7,4},{8,9},{9,10},{10,1... | collective-permute-start | bytes 1019912 | tf_op jit(solution)/shard_map/ppermute | solution.py:310
  14.9 13.5 %collective-permute-start.7 = (f32[664,128]{1,0:T(8,128)S(1)}, f32[664,128]{1,0:T(8,128)S(1)}, u32[]{:S(2)}, u32[]{:S(2)}) collective-permute-start(f32[664,128]{1,0:T(8,128)S(1)} %collective-permute-done.5.below0), channel_id=1, source_target_pairs={{0,1},{1,2},{2,3},{3,0},{4,5},{5,6},{6,7},{7,4},{8,9},{9,10},{10,1... | collective-permute-start | bytes 1019912 | tf_op jit(solution)/shard_map/ppermute | solution.py:310
  15.3 13.9 %collective-permute-start.8 = (f32[664,128]{1,0:T(8,128)S(1)}, f32[664,128]{1,0:T(8,128)S(1)}, u32[]{:S(2)}, u32[]{:S(2)}) collective-permute-start(f32[664,128]{1,0:T(8,128)S(1)} %collective-permute-done.4.above1), channel_id=1, source_target_pairs={{0,3},{1,0},{2,1},{3,2},{4,7},{5,4},{6,5},{7,6},{8,11},{9,8},{10,9... | collective-permute-start | bytes 1019912 | tf_op jit(solution)/shard_map/ppermute | solution.py:310
  34.3 28.1 %copy-start.12 = (f32[2,200,200]{2,1,0:T(8,128)}, f32[2,200,200]{2,1,0:T(8,128)S(1)}, u32[]{:S(2)}) copy-start(f32[2,200,200]{2,1,0:T(8,128)S(1)} %get-tuple-element.55.chain) | copy-start | bytes 960004
  34.3 33.8 %collective-permute-start.12 = (f32[2,200,200]{2,1,0:T(8,128)S(1)}, f32[2,200,200]{2,1,0:T(8,128)S(1)}, u32[]{:S(2)}, u32[]{:S(2)}) collective-permute-start(f32[2,200,200]{2,1,0:T(8,128)S(1)} %get-tuple-element.55.chain), channel_id=1, source_target_pairs={{4,0},{8,12},{5,1},{9,13},{6,2},{10,14},{7,3},{11,15},{20,16},{24,... | collective-permute-start | bytes 960008 | tf_op jit(solution)/shard_map/ppermute | solution.py:314
  41.2 30.1 %collective-permute-start.14 = (f32[2,200,200]{2,1,0:T(8,128)}, f32[2,200,200]{2,1,0:T(8,128)}, u32[]{:S(2)}, u32[]{:S(2)}) collective-permute-start(f32[2,200,200]{2,1,0:T(8,128)} %get-tuple-element.61.chain), channel_id=1, source_target_pairs={{4,0},{8,12},{5,1},{9,13},{6,2},{10,14},{7,3},{11,15},{20,16},{24,... | collective-permute-start | bytes 960008 | tf_op jit(solution)/shard_map/ppermute | solution.py:314
  42.7 7.0 %collective-permute-start = (f32[2,2,32,200]{3,2,1,0:T(8,128)S(1)}, f32[2,2,32,200]{3,2,1,0:T(8,128)S(1)}, u32[]{:S(2)}, u32[]{:S(2)}) collective-permute-start(f32[2,2,32,200]{3,2,1,0:T(8,128)S(1)} %get-tuple-element.43), channel_id=1, source_target_pairs={{0,3},{1,0},{2,1},{3,2},{4,7},{5,4},{6,5},{7,6},{8,11},{9,8},{10,9... | collective-permute-start | bytes 307208 | tf_op jit(solution)/shard_map/ppermute | solution.py:310
  45.1 6.9 %collective-permute-start.1 = (f32[2,2,32,200]{3,2,1,0:T(8,128)S(1)}, f32[2,2,32,200]{3,2,1,0:T(8,128)S(1)}, u32[]{:S(2)}, u32[]{:S(2)}) collective-permute-start(f32[2,2,32,200]{3,2,1,0:T(8,128)S(1)} %get-tuple-element.44), channel_id=1, source_target_pairs={{0,2},{1,3},{2,0},{3,1},{4,6},{5,7},{6,4},{7,5},{8,10},{9,11},{10,... | collective-permute-start | bytes 307208 | tf_op jit(solution)/shard_map/ppermute | solution.py:310
  45.7 7.6 %collective-permute-start.2 = (f32[2,2,32,200]{3,2,1,0:T(8,128)S(1)}, f32[2,2,32,200]{3,2,1,0:T(8,128)S(1)}, u32[]{:S(2)}, u32[]{:S(2)}) collective-permute-start(f32[2,2,32,200]{3,2,1,0:T(8,128)S(1)} %get-tuple-element.45), channel_id=1, source_target_pairs={{0,1},{1,2},{2,3},{3,0},{4,5},{5,6},{6,7},{7,4},{8,9},{9,10},{10,1... | collective-permute-start | bytes 307208 | tf_op jit(solution)/shard_map/ppermute | solution.py:310
  55.3 10.9 %copy-start.19 = (f32[2,8,32,200]{3,2,1,0:T(8,128)}, f32[2,8,32,200]{3,2,1,0:T(8,128)S(1)}, u32[]{:S(2)}) copy-start(f32[2,8,32,200]{3,2,1,0:T(8,128)S(1)} %get-tuple-element.68.sources) | copy-start | bytes 1228804
  55.3 7.1 %collective-permute-start.9 = (f32[2,32,200]{2,1,0:T(8,128)S(1)}, f32[2,32,200]{2,1,0:T(8,128)S(1)}, u32[]{:S(2)}, u32[]{:S(2)}) collective-permute-start(f32[2,32,200]{2,1,0:T(8,128)S(1)} %get-tuple-element.54.ends), channel_id=1, source_target_pairs={{0,4},{8,12},{1,5},{9,13},{2,6},{10,14},{3,7},{11,15},{16,20},{24,... | collective-permute-start | bytes 153608 | tf_op jit(solution)/shard_map/ppermute | solution.py:314
  62.6 5.5 %collective-permute-start.11 = (f32[2,32,200]{2,1,0:T(8,128)S(1)}, f32[2,32,200]{2,1,0:T(8,128)S(1)}, u32[]{:S(2)}, u32[]{:S(2)}) collective-permute-start(f32[2,32,200]{2,1,0:T(8,128)S(1)} %shard_map.51), channel_id=1, source_target_pairs={{4,12},{5,13},{6,14},{7,15},{20,28},{21,29},{22,30},{23,31},{36,44... | collective-permute-start | bytes 153608 | tf_op jit(solution)/shard_map/ppermute | solution.py:314
  63.3 4.8 %collective-permute-start.10 = (f32[2,32,200]{2,1,0:T(8,128)S(1)}, f32[2,32,200]{2,1,0:T(8,128)S(1)}, u32[]{:S(2)}, u32[]{:S(2)}) collective-permute-start(f32[2,32,200]{2,1,0:T(8,128)S(1)} %shard_map.51), channel_id=1, source_target_pairs={{4,8},{5,9},{6,10},{7,11},{20,24},{21,25},{22,26},{23,27},{36,40},... | collective-permute-start | bytes 153608 | tf_op jit(solution)/shard_map/ppermute | solution.py:314
  70.0 10.2 %collective-permute-start.13 = (f32[2,32,200]{2,1,0:T(8,128)}, f32[2,32,200]{2,1,0:T(8,128)S(1)}, u32[]{:S(2)}, u32[]{:S(2)}) collective-permute-start(f32[2,32,200]{2,1,0:T(8,128)} %get-tuple-element.60.ends), channel_id=1, source_target_pairs={{12,8},{8,12},{4,0},{13,9},{9,13},{5,1},{14,10},{10,14},{6,2},{15,... | collective-permute-start | bytes 153608 | tf_op jit(solution)/shard_map/ppermute | solution.py:314
  81.6 7.4 %collective-permute-start.15 = (f32[2,32,200]{2,1,0:T(8,128)S(1)}, f32[2,32,200]{2,1,0:T(8,128)S(1)}, u32[]{:S(2)}, u32[]{:S(2)}) collective-permute-start(f32[2,32,200]{2,1,0:T(8,128)S(1)} %shard_map.56), channel_id=1, source_target_pairs={{8,4},{12,0},{9,5},{13,1},{10,6},{14,2},{11,7},{15,3},{24,20},{28,... | collective-permute-start | bytes 153608 | tf_op jit(solution)/shard_map/ppermute | solution.py:314
  89.0 14.9 %copy-start.20 = (f32[2,8,32,200]{3,2,1,0:T(8,128)S(1)}, f32[2,8,32,200]{3,2,1,0:T(8,128)}, u32[]{:S(2)}) copy-start(f32[2,8,32,200]{3,2,1,0:T(8,128)} %copy-done.19) | copy-start | bytes 1228804
  91.4 8.6 %collective-permute-start.17 = (f32[2,8,32,200]{3,2,1,0:T(8,128)S(1)}, f32[2,8,32,200]{3,2,1,0:T(8,128)S(1)}, u32[]{:S(2)}, u32[]{:S(2)}) collective-permute-start(f32[2,8,32,200]{3,2,1,0:T(8,128)S(1)} %shard_map.58.own), channel_id=1, source_target_pairs={{16,0},{32,16},{48,32},{64,48},{80,64},{96,80},{112,96},{17,1},{33... | collective-permute-start | bytes 1228808 | tf_op jit(solution)/shard_map/ppermute | solution.py:382
  93.3 10.5 %collective-permute-start.16 = (f32[2,8,32,200]{3,2,1,0:T(8,128)S(1)}, f32[2,8,32,200]{3,2,1,0:T(8,128)S(1)}, u32[]{:S(2)}, u32[]{:S(2)}) collective-permute-start(f32[2,8,32,200]{3,2,1,0:T(8,128)S(1)} %shard_map.58.own), channel_id=1, source_target_pairs={{0,16},{16,32},{32,48},{48,64},{64,80},{80,96},{96,112},{1,17},{17... | collective-permute-start | bytes 1228808 | tf_op jit(solution)/shard_map/ppermute | solution.py:381
  103.8 8.2 %copy-start.11 = (f32[2,200,200]{2,1,0:T(8,128)S(1)}, f32[2,200,200]{2,1,0:T(8,128)}, u32[]{:S(2)}) copy-start(f32[2,200,200]{2,1,0:T(8,128)} %copy-done.10) | copy-start | bytes 960004
  103.8 8.2 %copy-start.13 = (f32[2,200,200]{2,1,0:T(8,128)S(1)}, f32[2,200,200]{2,1,0:T(8,128)}, u32[]{:S(2)}) copy-start(f32[2,200,200]{2,1,0:T(8,128)} %copy-done.12) | copy-start | bytes 960004
  105.9 6.2 %collective-permute-start.18 = (f32[2,32,200]{2,1,0:T(8,128)S(1)}, f32[2,32,200]{2,1,0:T(8,128)S(1)}, u32[]{:S(2)}, u32[]{:S(2)}) collective-permute-start(f32[2,32,200]{2,1,0:T(8,128)S(1)} %get-tuple-element.69.ends), channel_id=1, source_target_pairs={{0,4},{4,0},{8,12},{1,5},{5,1},{9,13},{2,6},{6,2},{10,14},{3,7},{7... | collective-permute-start | bytes 153608 | tf_op jit(solution)/shard_map/ppermute | solution.py:314
  112.3 7.6 %collective-permute-start.19 = (f32[2,32,200]{2,1,0:T(8,128)S(1)}, f32[2,32,200]{2,1,0:T(8,128)S(1)}, u32[]{:S(2)}, u32[]{:S(2)}) collective-permute-start(f32[2,32,200]{2,1,0:T(8,128)S(1)} %shard_map.60), channel_id=1, source_target_pairs={{4,8},{0,12},{5,9},{1,13},{6,10},{2,14},{7,11},{3,15},{20,24},{16,... | collective-permute-start | bytes 153608 | tf_op jit(solution)/shard_map/ppermute | solution.py:314
  118.0 11.2 %copy-start.9 = (bf16[2,8,200,200]{3,2,1,0:T(8,128)(2,1)S(1)}, bf16[2,8,200,200]{3,2,1,0:T(8,128)(2,1)}, u32[]{:S(2)}) copy-start(bf16[2,8,200,200]{3,2,1,0:T(8,128)(2,1)} %copy-done.7) | copy-start | bytes 3840004
  119.8 9.4 %copy-start.6 = (bf16[2,8,200,200]{3,2,1,0:T(8,128)(2,1)S(1)}, bf16[2,8,200,200]{3,2,1,0:T(8,128)(2,1)}, u32[]{:S(2)}) copy-start(bf16[2,8,200,200]{3,2,1,0:T(8,128)(2,1)} %copy-done.4) | copy-start | bytes 3840004
  120.4 6.2 %collective-permute-start.20 = (f32[2,32,200]{2,1,0:T(8,128)S(1)}, f32[2,32,200]{2,1,0:T(8,128)S(1)}, u32[]{:S(2)}, u32[]{:S(2)}) collective-permute-start(f32[2,32,200]{2,1,0:T(8,128)S(1)} %get-tuple-element.72.ends), channel_id=1, source_target_pairs={{12,8},{8,12},{4,0},{13,9},{9,13},{5,1},{14,10},{10,14},{6,2},{15,... | collective-permute-start | bytes 153608 | tf_op jit(solution)/shard_map/ppermute | solution.py:314
  127.9 7.4 %collective-permute-start.21 = (f32[2,32,200]{2,1,0:T(8,128)S(1)}, f32[2,32,200]{2,1,0:T(8,128)S(1)}, u32[]{:S(2)}, u32[]{:S(2)}) collective-permute-start(f32[2,32,200]{2,1,0:T(8,128)S(1)} %shard_map.63), channel_id=1, source_target_pairs={{8,4},{12,0},{9,5},{13,1},{10,6},{14,2},{11,7},{15,3},{24,20},{28,... | collective-permute-start | bytes 153608 | tf_op jit(solution)/shard_map/ppermute | solution.py:314
  137.7 5.0 %collective-permute-start.22 = (f32[2,2,32,200]{3,2,1,0:T(8,128)S(1)}, f32[2,2,32,200]{3,2,1,0:T(8,128)S(1)}, u32[]{:S(2)}, u32[]{:S(2)}) collective-permute-start(f32[2,2,32,200]{3,2,1,0:T(8,128)S(1)} %get-tuple-element.76), channel_id=1, source_target_pairs={{0,3},{1,0},{2,1},{3,2},{4,7},{5,4},{6,5},{7,6},{8,11},{9,8},{10,9... | collective-permute-start | bytes 307208 | tf_op jit(solution)/shard_map/ppermute | solution.py:310
  138.3 6.6 %collective-permute-start.23 = (f32[2,2,32,200]{3,2,1,0:T(8,128)S(1)}, f32[2,2,32,200]{3,2,1,0:T(8,128)S(1)}, u32[]{:S(2)}, u32[]{:S(2)}) collective-permute-start(f32[2,2,32,200]{3,2,1,0:T(8,128)S(1)} %get-tuple-element.77), channel_id=1, source_target_pairs={{0,2},{1,3},{2,0},{3,1},{4,6},{5,7},{6,4},{7,5},{8,10},{9,11},{10,... | collective-permute-start | bytes 307208 | tf_op jit(solution)/shard_map/ppermute | solution.py:310
  138.8 7.4 %collective-permute-start.24 = (f32[2,2,32,200]{3,2,1,0:T(8,128)S(1)}, f32[2,2,32,200]{3,2,1,0:T(8,128)S(1)}, u32[]{:S(2)}, u32[]{:S(2)}) collective-permute-start(f32[2,2,32,200]{3,2,1,0:T(8,128)S(1)} %get-tuple-element.78), channel_id=1, source_target_pairs={{0,1},{1,2},{2,3},{3,0},{4,5},{5,6},{6,7},{7,4},{8,9},{9,10},{10,1... | collective-permute-start | bytes 307208 | tf_op jit(solution)/shard_map/ppermute | solution.py:310
  (21 other events, 32.4 us)

commit v3 on v2

--- a/solution.py
+++ b/solution.py
@@ -51,7 +51,7 @@
     return run
 
 
-def pack_blocks(block_ref, radial_ref, axial_ref, first, second):
+def pack_blocks(mine_ref, place_ref, block_ref, radial_ref, axial_ref, first, second):
     for station, packed in enumerate((first, second)):
         for cell in range(2):
             packed[200 * cell : 200 * cell + 200] = block_ref[station, cell, :, 0:128]
@@ -232,8 +232,7 @@
         joined[station] = ends[station] + by_matrix(near[station], chain[station])
 
 
-def join(place_ref, ends, near, chain, chain_beside, joined):
-    outermost = place_ref[0] == 0
+def join(outermost, ends, near, chain, chain_beside, joined):
     for station in range(2):
         mine, other = ends[station], near[station]
         matrix = jnp.where(outermost, chain_beside[station], chain[station])
@@ -242,8 +241,15 @@
         )
 
 
-def incoming(place_ref, near, middle, chain_beside, station):
-    place = place_ref[0]
+def join_inner(place_ref, *refs):
+    join(place_ref[0] == 0, *refs)
+
+
+def join_outer(place_ref, *refs):
+    join(place_ref[0] == GROUP - 1, *refs)
+
+
+def incoming(place, near, middle, chain_beside, station):
     far = by_matrix(middle[station], chain_beside[station])
     arriving = near[station] + jnp.where(place == GROUP - 1, far, middle[station])
     return jnp.where(place == 0, 0.0, arriving)
@@ -258,7 +264,7 @@
 
 def turn(place_ref, near, middle, chain_beside, ends, matrix, arriving, turned):
     for station in range(2):
-        value = incoming(place_ref, near, middle, chain_beside, station)
+        value = incoming(place_ref[0], near, middle, chain_beside, station)
         arriving[station] = value
         turned[station] = ends[station] + by_matrix(value, matrix[station])
 
@@ -273,8 +279,9 @@
 
 
 def finish(place_ref, near, middle, chain_beside, outer, carry_high, carry_low, correction):
-    for station in range(2):
-        arriving = incoming(place_ref, near, middle, chain_beside, station)
+    place = GROUP - 1 - place_ref[0]
+    for station in range(2):
+        arriving = incoming(place, near, middle, chain_beside, station)
         for cell in range(outer.shape[1]):
             correction[station, cell] = outer[station, cell] + times(
                 arriving, carry_high[station, cell], carry_low[station, cell], 0
@@ -324,7 +331,6 @@
     width = columns // GROUP
     mine = lax.axis_index("rad_1").astype(jnp.int32).reshape(1)
     place = lax.axis_index("rad_0").astype(jnp.int32).reshape(1)
-    places = (place, GROUP - 1 - place)
     field = ((stations, cells, width, species), F32)
     square = ((stations, cells, species, species), BF16)
     wide = ((stations, cells, species, species), F32)
@@ -333,7 +339,9 @@
     message = [((stations, own_cells, width, species), F32)] * GROUP
     rows = [pltpu.VMEM((species, species), F32), pltpu.VMEM((8, species), F32)]
 
-    own = call(pack_blocks, [((664, 128), F32)] * 2)(block_inverse, radial_coupling, axial_coupling)
+    own = call(pack_blocks, [((664, 128), F32)] * 2, scalars=2)(
+        mine, place, block_inverse, radial_coupling, axial_coupling
+    )
     below = [shift(own[0], "rad_1", 1), None]
     above = [None, shift(own[1], "rad_1", -1)]
     below[1] = shift(own[1], "rad_1", 1)
@@ -383,21 +391,19 @@
             inner, last = call(next_inner, [field, edge])(up, correction, down, source, *system)
             near = hop(last, [(0, 1), (1, 0), (2, 3)])
             outer, ends = call(outer_local, [field, edge])(inner, *system)
-            (joined,) = call(join, [edge], scalars=1)(places[0], last, near, in_chain, in_beside)
+            (joined,) = call(join_inner, [edge], scalars=1)(place, last, near, in_chain, in_beside)
             middle = hop(joined, [(1, 2), (0, 3)])
             arriving, last = call(turn, [edge, edge], scalars=1)(
-                places[0], near, middle, in_beside, ends, turn_chain
+                place, near, middle, in_beside, ends, turn_chain
             )
         near = hop(last, mirrored([(0, 1), (1, 0), (2, 3)]))
         (outer,) = call(deepen, [field])(arriving, outer, turn_high, turn_low)
-        (joined,) = call(join, [edge], scalars=1)(places[1], last, near, out_chain, out_beside)
+        (joined,) = call(join_outer, [edge], scalars=1)(place, last, near, out_chain, out_beside)
         middle = hop(joined, mirrored([(1, 2), (0, 3)]))
         reach = (near, middle, out_beside, outer, out_high, out_low)
         if sweep_index + 1 < SWEEPS:
-            (correction,) = call(finish, [field], scalars=1)(places[1], *reach)
-    sent = call(
-        finish_last, message, scratch=[pltpu.VMEM(*field)], scalars=2
-    )(places[1], mine, *reach)
+            (correction,) = call(finish, [field], scalars=1)(place, *reach)
+    sent = call(finish_last, message, scratch=[pltpu.VMEM(*field)], scalars=2)(place, mine, *reach)
     got = [sent[0]] + [None] * 3
     for ahead in range(1, GROUP):
         got[GROUP - ahead] = shift(sent[ahead], "rad_1", ahead)

time: 148 us -> 131 us (0.89)
  local copies, waits for them, and re-layouts: 13.1 us -> 2.56 us
  Pallas kernels: 29.4 us -> 23.6 us
  starting transfers between devices: 40.7 us -> 36.6 us
  waiting for transfers between devices: 63.6 us -> 67.7 us
    unnamed x56 -> x8, local copies, waits for them, and re-layouts: 13.1 us -> 2.56 us
    pallas_call x21, Pallas kernels: 29.4 us -> 23.6 us  [run(): pl.pallas_call(body, out_shape=[jax.ShapeDtypeStruct(shape, kind) for sha...]
    ppermute x11, starting transfers between devices: 22 us -> 17.2 us  [hop(): return lax.ppermute(value, 'rad_0', pairs)]
    ppermute x11, waiting for transfers between devices: 25.9 us -> 29.8 us  [hop(): return lax.ppermute(value, 'rad_0', pairs)]
  transfers between devices with their start and end apart: 25 -> 25, of which waited for: 17 -> 18; matrix products, arithmetic and copies ran while one was open for 0% -> 0% of each run, Pallas kernels for 10% -> 11%
where the time goes in v3:
time: 131 us
  waiting for transfers between devices  67.7 us (52%)
  starting transfers between devices  36.6 us (28%)
  Pallas kernels  23.6 us (18%)
  local copies, waits for them, and re-layouts  2.56 us (2%)
    ppermute x12, waiting for transfers between devices, shift(): lax.ppermute(value, axis, [(i, (i + step) % count) for i in range(count)])  29.8 us
    ppermute x11, waiting for transfers between devices, hop(): return lax.ppermute(value, 'rad_0', pairs)  29.8 us
    pallas_call x21, Pallas kernels, run(): pl.pallas_call(body, out_shape=[jax.ShapeDtypeStruct(shape, kind) for sha...  23.6 us
    ppermute x11, starting transfers between devices, hop(): return lax.ppermute(value, 'rad_0', pairs)  17.2 us
    ppermute x12, starting transfers between devices, shift(): lax.ppermute(value, axis, [(i, (i + step) % count) for i in range(count)])  15.1 us
    ppermute x1, waiting for transfers between devices, relax(): lax.ppermute(correction, 'ax', [(i + 1, i) for i in range(count - 1)])  4.26 us
    ppermute x1, waiting for transfers between devices, relax(): up = lax.ppermute(correction, 'ax', [(i, i + 1) for i in range(count - 1)])  3.82 us
  transfers between devices with their start and end apart: 25, of which 18 were waited for; matrix products, arithmetic and copies ran while one was open for 0% of the time, Pallas kernels for 11%

profile of v3, /device:TPU:4, one launch (start us, length us, event | category | flops | bytes accessed | tf_op | source)
XLA Modules:
  0.0 130.7 jit_solution(9147911530171260957)
XLA Ops:
  2.8 1.6 %collective-permute-start.5 = (f32[664,128]{1,0:T(8,128)S(1)}, f32[664,128]{1,0:T(8,128)S(1)}, u32[]{:S(2)}, u32[]{:S(2)}) collective-permute-start(f32[664,128]{1,0:T(8,128)S(1)} %get-tuple-element.46.own0), channel_id=1, source_target_pairs={{0,1},{1,2},{2,3},{3,0},{4,5},{5,6},{6,7},{7,4},{8,9},{9,10},{10,1... | collective-permute-start | bytes 1019912 | tf_op jit(solution)/shard_map/ppermute | solution.py:317
  4.4 1.7 %collective-permute-start.4 = (f32[664,128]{1,0:T(8,128)S(1)}, f32[664,128]{1,0:T(8,128)S(1)}, u32[]{:S(2)}, u32[]{:S(2)}) collective-permute-start(f32[664,128]{1,0:T(8,128)S(1)} %get-tuple-element.47.own1), channel_id=1, source_target_pairs={{0,3},{1,0},{2,1},{3,2},{4,7},{5,4},{6,5},{7,6},{8,11},{9,8},{10,9... | collective-permute-start | bytes 1019912 | tf_op jit(solution)/shard_map/ppermute | solution.py:317
  6.1 1.8 %collective-permute-start.3 = (f32[664,128]{1,0:T(8,128)S(1)}, f32[664,128]{1,0:T(8,128)S(1)}, u32[]{:S(2)}, u32[]{:S(2)}) collective-permute-start(f32[664,128]{1,0:T(8,128)S(1)} %get-tuple-element.46.own0), channel_id=1, source_target_pairs={{0,3},{1,0},{2,1},{3,2},{4,7},{5,4},{6,5},{7,6},{8,11},{9,8},{10,9... | collective-permute-start | bytes 1019912 | tf_op jit(solution)/shard_map/ppermute | solution.py:317
  8.1 6.8 %collective-permute-done.5.below0 = f32[664,128]{1,0:T(8,128)S(1)} collective-permute-done((f32[664,128]{1,0:T(8,128)S(1)}, f32[664,128]{1,0:T(8,128)S(1)}, u32[]{:S(2)}, u32[]{:S(2)}) %collective-permute-start.5) | collective-permute-done | bytes 340000 | tf_op jit(solution)/shard_map/ppermute | solution.py:317
  15.3 2.9 %collective-permute-start.8 = (f32[664,128]{1,0:T(8,128)S(1)}, f32[664,128]{1,0:T(8,128)S(1)}, u32[]{:S(2)}, u32[]{:S(2)}) collective-permute-start(f32[664,128]{1,0:T(8,128)S(1)} %collective-permute-done.4.above1), channel_id=1, source_target_pairs={{0,3},{1,0},{2,1},{3,2},{4,7},{5,4},{6,5},{7,6},{8,11},{9,8},{10,9... | collective-permute-start | bytes 1019912 | tf_op jit(solution)/shard_map/ppermute | solution.py:317
  18.1 4.4 %collective-permute-done.3.above0 = f32[664,128]{1,0:T(8,128)S(1)} collective-permute-done((f32[664,128]{1,0:T(8,128)S(1)}, f32[664,128]{1,0:T(8,128)S(1)}, u32[]{:S(2)}, u32[]{:S(2)}) %collective-permute-start.3) | collective-permute-done | bytes 340000 | tf_op jit(solution)/shard_map/ppermute | solution.py:317
  23.2 5.2 %collective-permute-done.7.across0 = f32[664,128]{1,0:T(8,128)S(1)} collective-permute-done((f32[664,128]{1,0:T(8,128)S(1)}, f32[664,128]{1,0:T(8,128)S(1)}, u32[]{:S(2)}, u32[]{:S(2)}) %collective-permute-start.7) | collective-permute-done | bytes 340000 | tf_op jit(solution)/shard_map/ppermute | solution.py:317
  28.4 2.5 %shard_map.49 = (bf16[2,8,200,200]{3,2,1,0:T(8,128)(2,1)S(1)}, bf16[2,8,200,200]{3,2,1,0:T(8,128)(2,1)S(1)}, f32[2,8,8,200]{3,2,1,0:T(8,128)S(1)}, f32[2,8,200,200]{3,2,1,0:T(8,128)S(1)}, f32[2,200,200]{2,1,0:T(8,128)S(1)}) custom-call(s32[1]{0:T(128)} %bitcast.mine_ref, bf16[3,2,2,200,200]{4,3,2,1,0:T(8,128)(2,1)S(1)} %get-tuple-element.48.near_high, ...), custom_call_target="tpu_custom_call" | custom-call | flops 1000 | bytes 1000 | tf_op jit(solution)/shard_map/pallas_call | solution.py:39
  32.2 2.4 %shard_map.55 = (bf16[2,8,200,200]{3,2,1,0:T(8,128)(2,1)S(1)}, bf16[2,8,200,200]{3,2,1,0:T(8,128)(2,1)S(1)}, f32[2,200,200]{2,1,0:T(8,128)S(1)}) custom-call(bf16[2,8,200,200]{3,2,1,0:T(8,128)(2,1)S(1)} %get-tuple-element.51.high, bf16[2,8,200,200]{3,2,1,0:T(8,128)(2,1)S(1)} %get-tuple-element.52.low, f32[2,8,8,200]{3,2,1,0:T(8,128)S(1)} %get-tuple-element.53.coupling), custom_call_target="tpu_custom_call" | custom-call | flops 1000 | bytes 1000 | tf_op jit(solution)/shard_map/pallas_call | solution.py:39
  36.2 3.1 %collective-permute-start = (f32[2,2,32,200]{3,2,1,0:T(8,128)S(1)}, f32[2,2,32,200]{3,2,1,0:T(8,128)S(1)}, u32[]{:S(2)}, u32[]{:S(2)}) collective-permute-start(f32[2,2,32,200]{3,2,1,0:T(8,128)S(1)} %get-tuple-element.43), channel_id=1, source_target_pairs={{0,3},{1,0},{2,1},{3,2},{4,7},{5,4},{6,5},{7,6},{8,11},{9,8},{10,9... | collective-permute-start | bytes 307208 | tf_op jit(solution)/shard_map/ppermute | solution.py:317
  40.6 3.3 %collective-permute-done.m1 = f32[2,2,32,200]{3,2,1,0:T(8,128)S(1)} collective-permute-done((f32[2,2,32,200]{3,2,1,0:T(8,128)S(1)}, f32[2,2,32,200]{3,2,1,0:T(8,128)S(1)}, u32[]{:S(2)}, u32[]{:S(2)}) %collective-permute-start) | collective-permute-done | bytes 102432 | tf_op jit(solution)/shard_map/ppermute | solution.py:317
  43.8 2.3 %collective-permute-done.1.m2 = f32[2,2,32,200]{3,2,1,0:T(8,128)S(1)} collective-permute-done((f32[2,2,32,200]{3,2,1,0:T(8,128)S(1)}, f32[2,2,32,200]{3,2,1,0:T(8,128)S(1)}, u32[]{:S(2)}, u32[]{:S(2)}) %collective-permute-start.1) | collective-permute-done | bytes 102432 | tf_op jit(solution)/shard_map/ppermute | solution.py:317
  47.4 2.0 %shard_map.50 = (f32[2,8,32,200]{3,2,1,0:T(8,128)S(1)}, f32[2,8,32,200]{3,2,1,0:T(8,128)S(1)}, f32[2,32,200]{2,1,0:T(8,128)S(1)}) custom-call(s32[1]{0:T(128)} %bitcast.mine_ref, f32[2,2,32,200]{3,2,1,0:T(8,128)S(1)} %get-tuple-element.42.m0, f32[2,2,32,200]{3,2,1,0:T(8,128)S(1)} %collective-permute-done.m1, ...), custom_call_target="tpu_custom_call" | custom-call | flops 1000 | bytes 1000 | tf_op jit(solution)/shard_map/pallas_call | solution.py:39
  49.5 4.4 %collective-permute-start.9 = (f32[2,32,200]{2,1,0:T(8,128)S(1)}, f32[2,32,200]{2,1,0:T(8,128)S(1)}, u32[]{:S(2)}, u32[]{:S(2)}) collective-permute-start(f32[2,32,200]{2,1,0:T(8,128)S(1)} %get-tuple-element.54.ends), channel_id=1, source_target_pairs={{0,4},{8,12},{1,5},{9,13},{2,6},{10,14},{3,7},{11,15},{16,20},{24,... | collective-permute-start | bytes 153608 | tf_op jit(solution)/shard_map/ppermute | solution.py:321
  53.9 1.9 %collective-permute-done.9.near = f32[2,32,200]{2,1,0:T(8,128)S(1)} collective-permute-done((f32[2,32,200]{2,1,0:T(8,128)S(1)}, f32[2,32,200]{2,1,0:T(8,128)S(1)}, u32[]{:S(2)}, u32[]{:S(2)}) %collective-permute-start.9) | collective-permute-done | bytes 51232 | tf_op jit(solution)/shard_map/ppermute | solution.py:321
  57.4 2.2 %shard_map.53 = (bf16[2,8,200,200]{3,2,1,0:T(8,128)(2,1)S(1)}, bf16[2,8,200,200]{3,2,1,0:T(8,128)(2,1)S(1)}, f32[2,200,200]{2,1,0:T(8,128)S(1)}) custom-call(bf16[2,8,200,200]{3,2,1,0:T(8,128)(2,1)S(1)} %get-tuple-element.51.high, bf16[2,8,200,200]{3,2,1,0:T(8,128)(2,1)S(1)} %get-tuple-element.52.low, f32[2,8,8,200]{3,2,1,0:T(8,128)S(1)} %get-tuple-element.53.coupling, ...), custom_call_target="tpu_custom_call" | custom-call | flops 1000 | bytes 1000 | tf_op jit(solution)/shard_map/pallas_call | solution.py:39
  59.6 1.8 %shard_map.52 = (f32[2,8,32,200]{3,2,1,0:T(8,128)S(1)}, f32[2,32,200]{2,1,0:T(8,128)S(1)}) custom-call(f32[2,8,32,200]{3,2,1,0:T(8,128)S(1)} %get-tuple-element.56.inner, bf16[2,8,200,200]{3,2,1,0:T(8,128)(2,1)S(1)} %get-tuple-element.51.high, bf16[2,8,200,200]{3,2,1,0:T(8,128)(2,1)S(1)} %get-tuple-element.52.low, ...), custom_call_target="tpu_custom_call" | custom-call | flops 1000 | bytes 1000 | tf_op jit(solution)/shard_map/pallas_call | solution.py:39
  63.2 8.8 %collective-permute-done.13.refs_1_.near = f32[2,32,200]{2,1,0:T(8,128)S(1)} collective-permute-done((f32[2,32,200]{2,1,0:T(8,128)S(1)}, f32[2,32,200]{2,1,0:T(8,128)S(1)}, u32[]{:S(2)}, u32[]{:S(2)}) %collective-permute-start.13) | collective-permute-done | bytes 51232 | tf_op jit(solution)/shard_map/ppermute | solution.py:321
  74.8 4.9 %collective-permute-done.15.middle = f32[2,32,200]{2,1,0:T(8,128)S(1)} collective-permute-done((f32[2,32,200]{2,1,0:T(8,128)S(1)}, f32[2,32,200]{2,1,0:T(8,128)S(1)}, u32[]{:S(2)}, u32[]{:S(2)}) %collective-permute-start.15) | collective-permute-done | bytes 51232 | tf_op jit(solution)/shard_map/ppermute | solution.py:321
  81.0 1.9 %collective-permute-start.17 = (f32[2,8,32,200]{3,2,1,0:T(8,128)S(1)}, f32[2,8,32,200]{3,2,1,0:T(8,128)S(1)}, u32[]{:S(2)}, u32[]{:S(2)}) collective-permute-start(f32[2,8,32,200]{3,2,1,0:T(8,128)S(1)} %shard_map.58.own), channel_id=1, source_target_pairs={{16,0},{32,16},{48,32},{64,48},{80,64},{96,80},{112,96},{17,1},{33... | collective-permute-start | bytes 1228808 | tf_op jit(solution)/shard_map/ppermute | solution.py:390
  83.0 2.4 %collective-permute-start.16 = (f32[2,8,32,200]{3,2,1,0:T(8,128)S(1)}, f32[2,8,32,200]{3,2,1,0:T(8,128)S(1)}, u32[]{:S(2)}, u32[]{:S(2)}) collective-permute-start(f32[2,8,32,200]{3,2,1,0:T(8,128)S(1)} %shard_map.58.own), channel_id=1, source_target_pairs={{0,16},{16,32},{32,48},{48,64},{64,80},{80,96},{96,112},{1,17},{17... | collective-permute-start | bytes 1228808 | tf_op jit(solution)/shard_map/ppermute | solution.py:389
  85.4 4.3 %collective-permute-done.17.above = f32[2,8,32,200]{3,2,1,0:T(8,128)S(1)} collective-permute-done((f32[2,8,32,200]{3,2,1,0:T(8,128)S(1)}, f32[2,8,32,200]{3,2,1,0:T(8,128)S(1)}, u32[]{:S(2)}, u32[]{:S(2)}) %collective-permute-start.17) | collective-permute-done | bytes 409632 | tf_op jit(solution)/shard_map/ppermute | solution.py:390
  89.6 3.8 %collective-permute-done.16.below = f32[2,8,32,200]{3,2,1,0:T(8,128)S(1)} collective-permute-done((f32[2,8,32,200]{3,2,1,0:T(8,128)S(1)}, f32[2,8,32,200]{3,2,1,0:T(8,128)S(1)}, u32[]{:S(2)}, u32[]{:S(2)}) %collective-permute-start.16) | collective-permute-done | bytes 409632 | tf_op jit(solution)/shard_map/ppermute | solution.py:389
  93.5 2.0 %shard_map.59 = (f32[2,8,32,200]{3,2,1,0:T(8,128)S(1)}, f32[2,32,200]{2,1,0:T(8,128)S(1)}) custom-call(f32[2,8,32,200]{3,2,1,0:T(8,128)S(1)} %collective-permute-done.16.below, f32[2,8,32,200]{3,2,1,0:T(8,128)S(1)} %shard_map.58.own, f32[2,8,32,200]{3,2,1,0:T(8,128)S(1)} %collective-permute-done.17.above, f32[2,8,32,200]{3,2,1,0:T(8,128)S(1)} %get-tuple-element.68.sources, ...), custom_call_target="tpu_custom_call" | custom-call | flops 1000 | bytes 1000 | tf_op jit(solution)/shard_map/pallas_call | solution.py:39
  95.5 1.9 %collective-permute-start.18 = (f32[2,32,200]{2,1,0:T(8,128)S(1)}, f32[2,32,200]{2,1,0:T(8,128)S(1)}, u32[]{:S(2)}, u32[]{:S(2)}) collective-permute-start(f32[2,32,200]{2,1,0:T(8,128)S(1)} %get-tuple-element.69.refs_0_), channel_id=1, source_target_pairs={{0,4},{4,0},{8,12},{1,5},{5,1},{9,13},{2,6},{6,2},{10,14},{3,7},{7... | collective-permute-start | bytes 153608 | tf_op jit(solution)/shard_map/ppermute | solution.py:321
  97.4 4.2 %collective-permute-done.18.refs_1_.near = f32[2,32,200]{2,1,0:T(8,128)S(1)} collective-permute-done((f32[2,32,200]{2,1,0:T(8,128)S(1)}, f32[2,32,200]{2,1,0:T(8,128)S(1)}, u32[]{:S(2)}, u32[]{:S(2)}) %collective-permute-start.18) | collective-permute-done | bytes 51232 | tf_op jit(solution)/shard_map/ppermute | solution.py:321
  101.9 1.6 %collective-permute-start.19 = (f32[2,32,200]{2,1,0:T(8,128)S(1)}, f32[2,32,200]{2,1,0:T(8,128)S(1)}, u32[]{:S(2)}, u32[]{:S(2)}) collective-permute-start(f32[2,32,200]{2,1,0:T(8,128)S(1)} %shard_map.60), channel_id=1, source_target_pairs={{4,8},{0,12},{5,9},{1,13},{6,10},{2,14},{7,11},{3,15},{20,24},{16,... | collective-permute-start | bytes 153608 | tf_op jit(solution)/shard_map/ppermute | solution.py:321
  103.5 1.8 %shard_map.61 = (f32[2,8,32,200]{3,2,1,0:T(8,128)S(1)}, f32[2,32,200]{2,1,0:T(8,128)S(1)}) custom-call(f32[2,8,32,200]{3,2,1,0:T(8,128)S(1)} %get-tuple-element.70.inner, bf16[2,8,200,200]{3,2,1,0:T(8,128)(2,1)S(1)} %get-tuple-element.51.high, bf16[2,8,200,200]{3,2,1,0:T(8,128)(2,1)S(1)} %get-tuple-element.52.low, ...), custom_call_target="tpu_custom_call" | custom-call | flops 1000 | bytes 1000 | tf_op jit(solution)/shard_map/pallas_call | solution.py:39
  107.1 4.9 %collective-permute-done.20.refs_1_.near = f32[2,32,200]{2,1,0:T(8,128)S(1)} collective-permute-done((f32[2,32,200]{2,1,0:T(8,128)S(1)}, f32[2,32,200]{2,1,0:T(8,128)S(1)}, u32[]{:S(2)}, u32[]{:S(2)}) %collective-permute-start.20) | collective-permute-done | bytes 51232 | tf_op jit(solution)/shard_map/ppermute | solution.py:321
  114.6 5.0 %collective-permute-done.21.middle = f32[2,32,200]{2,1,0:T(8,128)S(1)} collective-permute-done((f32[2,32,200]{2,1,0:T(8,128)S(1)}, f32[2,32,200]{2,1,0:T(8,128)S(1)}, u32[]{:S(2)}, u32[]{:S(2)}) %collective-permute-start.21) | collective-permute-done | bytes 51232 | tf_op jit(solution)/shard_map/ppermute | solution.py:321
  123.1 2.9 %collective-permute-done.22.m1 = f32[2,2,32,200]{3,2,1,0:T(8,128)S(1)} collective-permute-done((f32[2,2,32,200]{3,2,1,0:T(8,128)S(1)}, f32[2,2,32,200]{3,2,1,0:T(8,128)S(1)}, u32[]{:S(2)}, u32[]{:S(2)}) %collective-permute-start.22) | collective-permute-done | bytes 102432 | tf_op jit(solution)/shard_map/ppermute | solution.py:317
  126.1 2.3 %collective-permute-done.23.m2 = f32[2,2,32,200]{3,2,1,0:T(8,128)S(1)} collective-permute-done((f32[2,2,32,200]{3,2,1,0:T(8,128)S(1)}, f32[2,2,32,200]{3,2,1,0:T(8,128)S(1)}, u32[]{:S(2)}, u32[]{:S(2)}) %collective-permute-start.23) | collective-permute-done | bytes 102432 | tf_op jit(solution)/shard_map/ppermute | solution.py:317
  (47 shorter events, 27.4 us)
Async XLA Ops:
  0.0 1.1 copy-start
  1.1 0.7 copy-start.2
  1.9 0.7 copy-start.3
  2.8 12.1 %collective-permute-start.5 = (f32[664,128]{1,0:T(8,128)S(1)}, f32[664,128]{1,0:T(8,128)S(1)}, u32[]{:S(2)}, u32[]{:S(2)}) collective-permute-start(f32[664,128]{1,0:T(8,128)S(1)} %get-tuple-element.46.own0), channel_id=1, source_target_pairs={{0,1},{1,2},{2,3},{3,0},{4,5},{5,6},{6,7},{7,4},{8,9},{9,10},{10,1... | collective-permute-start | bytes 1019912 | tf_op jit(solution)/shard_map/ppermute | solution.py:317
  4.4 10.8 %collective-permute-start.4 = (f32[664,128]{1,0:T(8,128)S(1)}, f32[664,128]{1,0:T(8,128)S(1)}, u32[]{:S(2)}, u32[]{:S(2)}) collective-permute-start(f32[664,128]{1,0:T(8,128)S(1)} %get-tuple-element.47.own1), channel_id=1, source_target_pairs={{0,3},{1,0},{2,1},{3,2},{4,7},{5,4},{6,5},{7,6},{8,11},{9,8},{10,9... | collective-permute-start | bytes 1019912 | tf_op jit(solution)/shard_map/ppermute | solution.py:317
  6.1 16.5 %collective-permute-start.3 = (f32[664,128]{1,0:T(8,128)S(1)}, f32[664,128]{1,0:T(8,128)S(1)}, u32[]{:S(2)}, u32[]{:S(2)}) collective-permute-start(f32[664,128]{1,0:T(8,128)S(1)} %get-tuple-element.46.own0), channel_id=1, source_target_pairs={{0,3},{1,0},{2,1},{3,2},{4,7},{5,4},{6,5},{7,6},{8,11},{9,8},{10,9... | collective-permute-start | bytes 1019912 | tf_op jit(solution)/shard_map/ppermute | solution.py:317
  7.9 14.7 %collective-permute-start.6 = (f32[664,128]{1,0:T(8,128)S(1)}, f32[664,128]{1,0:T(8,128)S(1)}, u32[]{:S(2)}, u32[]{:S(2)}) collective-permute-start(f32[664,128]{1,0:T(8,128)S(1)} %get-tuple-element.47.own1), channel_id=1, source_target_pairs={{0,1},{1,2},{2,3},{3,0},{4,5},{5,6},{6,7},{7,4},{8,9},{9,10},{10,1... | collective-permute-start | bytes 1019912 | tf_op jit(solution)/shard_map/ppermute | solution.py:317
  14.9 13.5 %collective-permute-start.7 = (f32[664,128]{1,0:T(8,128)S(1)}, f32[664,128]{1,0:T(8,128)S(1)}, u32[]{:S(2)}, u32[]{:S(2)}) collective-permute-start(f32[664,128]{1,0:T(8,128)S(1)} %collective-permute-done.5.below0), channel_id=1, source_target_pairs={{0,1},{1,2},{2,3},{3,0},{4,5},{5,6},{6,7},{7,4},{8,9},{9,10},{10,1... | collective-permute-start | bytes 1019912 | tf_op jit(solution)/shard_map/ppermute | solution.py:317
  15.3 13.2 %collective-permute-start.8 = (f32[664,128]{1,0:T(8,128)S(1)}, f32[664,128]{1,0:T(8,128)S(1)}, u32[]{:S(2)}, u32[]{:S(2)}) collective-permute-start(f32[664,128]{1,0:T(8,128)S(1)} %collective-permute-done.4.above1), channel_id=1, source_target_pairs={{0,3},{1,0},{2,1},{3,2},{4,7},{5,4},{6,5},{7,6},{8,11},{9,8},{10,9... | collective-permute-start | bytes 1019912 | tf_op jit(solution)/shard_map/ppermute | solution.py:317
  30.9 30.6 %collective-permute-start.12 = (f32[2,200,200]{2,1,0:T(8,128)S(1)}, f32[2,200,200]{2,1,0:T(8,128)S(1)}, u32[]{:S(2)}, u32[]{:S(2)}) collective-permute-start(f32[2,200,200]{2,1,0:T(8,128)S(1)} %get-tuple-element.55.chain.refs_2_), channel_id=1, source_target_pairs={{4,0},{8,12},{5,1},{9,13},{6,2},{10,14},{7,3},{11,15},{20,16},{24,... | collective-permute-start | bytes 960008 | tf_op jit(solution)/shard_map/ppermute | solution.py:321
  32.2 3.7 %copy-start.1 = (f32[2,2,200,128]{3,2,1,0:T(8,128)S(1)}, f32[2,2,200,128]{3,2,1,0:T(8,128)}, u32[]{:S(2)}) copy-start(f32[2,2,200,128]{3,2,1,0:T(8,128)} %sources_ref.1) | copy-start | bytes 1228804
  34.6 28.6 %collective-permute-start.14 = (f32[2,200,200]{2,1,0:T(8,128)S(1)}, f32[2,200,200]{2,1,0:T(8,128)S(1)}, u32[]{:S(2)}, u32[]{:S(2)}) collective-permute-start(f32[2,200,200]{2,1,0:T(8,128)S(1)} %get-tuple-element.61.refs_2_), channel_id=1, source_target_pairs={{4,0},{8,12},{5,1},{9,13},{6,2},{10,14},{7,3},{11,15},{20,16},{24,... | collective-permute-start | bytes 960008 | tf_op jit(solution)/shard_map/ppermute | solution.py:321
  36.2 7.7 %collective-permute-start = (f32[2,2,32,200]{3,2,1,0:T(8,128)S(1)}, f32[2,2,32,200]{3,2,1,0:T(8,128)S(1)}, u32[]{:S(2)}, u32[]{:S(2)}) collective-permute-start(f32[2,2,32,200]{3,2,1,0:T(8,128)S(1)} %get-tuple-element.43), channel_id=1, source_target_pairs={{0,3},{1,0},{2,1},{3,2},{4,7},{5,4},{6,5},{7,6},{8,11},{9,8},{10,9... | collective-permute-start | bytes 307208 | tf_op jit(solution)/shard_map/ppermute | solution.py:317
  39.2 6.9 %collective-permute-start.1 = (f32[2,2,32,200]{3,2,1,0:T(8,128)S(1)}, f32[2,2,32,200]{3,2,1,0:T(8,128)S(1)}, u32[]{:S(2)}, u32[]{:S(2)}) collective-permute-start(f32[2,2,32,200]{3,2,1,0:T(8,128)S(1)} %get-tuple-element.44), channel_id=1, source_target_pairs={{0,2},{1,3},{2,0},{3,1},{4,6},{5,7},{6,4},{7,5},{8,10},{9,11},{10,... | collective-permute-start | bytes 307208 | tf_op jit(solution)/shard_map/ppermute | solution.py:317
  39.9 7.6 %collective-permute-start.2 = (f32[2,2,32,200]{3,2,1,0:T(8,128)S(1)}, f32[2,2,32,200]{3,2,1,0:T(8,128)S(1)}, u32[]{:S(2)}, u32[]{:S(2)}) collective-permute-start(f32[2,2,32,200]{3,2,1,0:T(8,128)S(1)} %get-tuple-element.45), channel_id=1, source_target_pairs={{0,1},{1,2},{2,3},{3,0},{4,5},{5,6},{6,7},{7,4},{8,9},{9,10},{10,1... | collective-permute-start | bytes 307208 | tf_op jit(solution)/shard_map/ppermute | solution.py:317
  49.5 6.3 %collective-permute-start.9 = (f32[2,32,200]{2,1,0:T(8,128)S(1)}, f32[2,32,200]{2,1,0:T(8,128)S(1)}, u32[]{:S(2)}, u32[]{:S(2)}) collective-permute-start(f32[2,32,200]{2,1,0:T(8,128)S(1)} %get-tuple-element.54.ends), channel_id=1, source_target_pairs={{0,4},{8,12},{1,5},{9,13},{2,6},{10,14},{3,7},{11,15},{16,20},{24,... | collective-permute-start | bytes 153608 | tf_op jit(solution)/shard_map/ppermute | solution.py:321
  56.0 5.4 %collective-permute-start.11 = (f32[2,32,200]{2,1,0:T(8,128)S(1)}, f32[2,32,200]{2,1,0:T(8,128)S(1)}, u32[]{:S(2)}, u32[]{:S(2)}) collective-permute-start(f32[2,32,200]{2,1,0:T(8,128)S(1)} %shard_map.51), channel_id=1, source_target_pairs={{4,12},{5,13},{6,14},{7,15},{20,28},{21,29},{22,30},{23,31},{36,44... | collective-permute-start | bytes 153608 | tf_op jit(solution)/shard_map/ppermute | solution.py:321
  56.7 4.7 %collective-permute-start.10 = (f32[2,32,200]{2,1,0:T(8,128)S(1)}, f32[2,32,200]{2,1,0:T(8,128)S(1)}, u32[]{:S(2)}, u32[]{:S(2)}) collective-permute-start(f32[2,32,200]{2,1,0:T(8,128)S(1)} %shard_map.51), channel_id=1, source_target_pairs={{4,8},{5,9},{6,10},{7,11},{20,24},{21,25},{22,26},{23,27},{36,40},... | collective-permute-start | bytes 153608 | tf_op jit(solution)/shard_map/ppermute | solution.py:321
  61.9 10.1 %collective-permute-start.13 = (f32[2,32,200]{2,1,0:T(8,128)S(1)}, f32[2,32,200]{2,1,0:T(8,128)S(1)}, u32[]{:S(2)}, u32[]{:S(2)}) collective-permute-start(f32[2,32,200]{2,1,0:T(8,128)S(1)} %get-tuple-element.60.refs_0_), channel_id=1, source_target_pairs={{12,8},{8,12},{4,0},{13,9},{9,13},{5,1},{14,10},{10,14},{6,2},{15,... | collective-permute-start | bytes 153608 | tf_op jit(solution)/shard_map/ppermute | solution.py:321
  72.3 7.4 %collective-permute-start.15 = (f32[2,32,200]{2,1,0:T(8,128)S(1)}, f32[2,32,200]{2,1,0:T(8,128)S(1)}, u32[]{:S(2)}, u32[]{:S(2)}) collective-permute-start(f32[2,32,200]{2,1,0:T(8,128)S(1)} %shard_map.56), channel_id=1, source_target_pairs={{8,4},{12,0},{9,5},{13,1},{10,6},{14,2},{11,7},{15,3},{24,20},{28,... | collective-permute-start | bytes 153608 | tf_op jit(solution)/shard_map/ppermute | solution.py:321
  81.0 8.6 %collective-permute-start.17 = (f32[2,8,32,200]{3,2,1,0:T(8,128)S(1)}, f32[2,8,32,200]{3,2,1,0:T(8,128)S(1)}, u32[]{:S(2)}, u32[]{:S(2)}) collective-permute-start(f32[2,8,32,200]{3,2,1,0:T(8,128)S(1)} %shard_map.58.own), channel_id=1, source_target_pairs={{16,0},{32,16},{48,32},{64,48},{80,64},{96,80},{112,96},{17,1},{33... | collective-permute-start | bytes 1228808 | tf_op jit(solution)/shard_map/ppermute | solution.py:390
  83.0 10.5 %collective-permute-start.16 = (f32[2,8,32,200]{3,2,1,0:T(8,128)S(1)}, f32[2,8,32,200]{3,2,1,0:T(8,128)S(1)}, u32[]{:S(2)}, u32[]{:S(2)}) collective-permute-start(f32[2,8,32,200]{3,2,1,0:T(8,128)S(1)} %shard_map.58.own), channel_id=1, source_target_pairs={{0,16},{16,32},{32,48},{48,64},{64,80},{80,96},{96,112},{1,17},{17... | collective-permute-start | bytes 1228808 | tf_op jit(solution)/shard_map/ppermute | solution.py:389
  95.5 6.2 %collective-permute-start.18 = (f32[2,32,200]{2,1,0:T(8,128)S(1)}, f32[2,32,200]{2,1,0:T(8,128)S(1)}, u32[]{:S(2)}, u32[]{:S(2)}) collective-permute-start(f32[2,32,200]{2,1,0:T(8,128)S(1)} %get-tuple-element.69.refs_0_), channel_id=1, source_target_pairs={{0,4},{4,0},{8,12},{1,5},{5,1},{9,13},{2,6},{6,2},{10,14},{3,7},{7... | collective-permute-start | bytes 153608 | tf_op jit(solution)/shard_map/ppermute | solution.py:321
  101.9 3.5 %collective-permute-start.19 = (f32[2,32,200]{2,1,0:T(8,128)S(1)}, f32[2,32,200]{2,1,0:T(8,128)S(1)}, u32[]{:S(2)}, u32[]{:S(2)}) collective-permute-start(f32[2,32,200]{2,1,0:T(8,128)S(1)} %shard_map.60), channel_id=1, source_target_pairs={{4,8},{0,12},{5,9},{1,13},{6,10},{2,14},{7,11},{3,15},{20,24},{16,... | collective-permute-start | bytes 153608 | tf_op jit(solution)/shard_map/ppermute | solution.py:321
  105.8 6.2 %collective-permute-start.20 = (f32[2,32,200]{2,1,0:T(8,128)S(1)}, f32[2,32,200]{2,1,0:T(8,128)S(1)}, u32[]{:S(2)}, u32[]{:S(2)}) collective-permute-start(f32[2,32,200]{2,1,0:T(8,128)S(1)} %get-tuple-element.72.refs_0_), channel_id=1, source_target_pairs={{12,8},{8,12},{4,0},{13,9},{9,13},{5,1},{14,10},{10,14},{6,2},{15,... | collective-permute-start | bytes 153608 | tf_op jit(solution)/shard_map/ppermute | solution.py:321
  112.2 7.4 %collective-permute-start.21 = (f32[2,32,200]{2,1,0:T(8,128)S(1)}, f32[2,32,200]{2,1,0:T(8,128)S(1)}, u32[]{:S(2)}, u32[]{:S(2)}) collective-permute-start(f32[2,32,200]{2,1,0:T(8,128)S(1)} %shard_map.63), channel_id=1, source_target_pairs={{8,4},{12,0},{9,5},{13,1},{10,6},{14,2},{11,7},{15,3},{24,20},{28,... | collective-permute-start | bytes 153608 | tf_op jit(solution)/shard_map/ppermute | solution.py:321
  121.0 5.0 %collective-permute-start.22 = (f32[2,2,32,200]{3,2,1,0:T(8,128)S(1)}, f32[2,2,32,200]{3,2,1,0:T(8,128)S(1)}, u32[]{:S(2)}, u32[]{:S(2)}) collective-permute-start(f32[2,2,32,200]{3,2,1,0:T(8,128)S(1)} %get-tuple-element.76), channel_id=1, source_target_pairs={{0,3},{1,0},{2,1},{3,2},{4,7},{5,4},{6,5},{7,6},{8,11},{9,8},{10,9... | collective-permute-start | bytes 307208 | tf_op jit(solution)/shard_map/ppermute | solution.py:317
  121.8 6.6 %collective-permute-start.23 = (f32[2,2,32,200]{3,2,1,0:T(8,128)S(1)}, f32[2,2,32,200]{3,2,1,0:T(8,128)S(1)}, u32[]{:S(2)}, u32[]{:S(2)}) collective-permute-start(f32[2,2,32,200]{3,2,1,0:T(8,128)S(1)} %get-tuple-element.77), channel_id=1, source_target_pairs={{0,2},{1,3},{2,0},{3,1},{4,6},{5,7},{6,4},{7,5},{8,10},{9,11},{10,... | collective-permute-start | bytes 307208 | tf_op jit(solution)/shard_map/ppermute | solution.py:317
  122.3 7.4 %collective-permute-start.24 = (f32[2,2,32,200]{3,2,1,0:T(8,128)S(1)}, f32[2,2,32,200]{3,2,1,0:T(8,128)S(1)}, u32[]{:S(2)}, u32[]{:S(2)}) collective-permute-start(f32[2,2,32,200]{3,2,1,0:T(8,128)S(1)} %get-tuple-element.78), channel_id=1, source_target_pairs={{0,1},{1,2},{2,3},{3,0},{4,5},{5,6},{6,7},{7,4},{8,9},{9,10},{10,1... | collective-permute-start | bytes 307208 | tf_op jit(solution)/shard_map/ppermute | solution.py:317

commit v4 on v3

--- a/solution.py
+++ b/solution.py
@@ -32,10 +32,11 @@
     )
 
 
-def call(body, out, scratch=(), scalars=0):
+def call(body, out, scratch=(), scalars=0, space=pltpu.VMEM):
     def run(*operands):
         specs = [pl.BlockSpec(memory_space=pltpu.SMEM)] * scalars
-        specs += [pl.BlockSpec(memory_space=pltpu.VMEM)] * (len(operands) - scalars)
+        specs += [pl.BlockSpec(memory_space=space)] * (len(operands) - scalars)
+        moved = sum(o.size * o.dtype.itemsize for o in operands)
         return pl.pallas_call(
             body,
             out_shape=[jax.ShapeDtypeStruct(shape, kind) for shape, kind in out],
@@ -51,8 +52,23 @@
     return run
 
 
-def pack_blocks(mine_ref, place_ref, block_ref, radial_ref, axial_ref, first, second):
+def pack_blocks(
+    mine_ref, place_ref, block_far, radial_far, axial_far, first, second,
+    block_ref, radial_ref, axial_ref, arrives,
+):
+    pairs = [(block_far.at[s], block_ref.at[s]) for s in range(2)]
+    pairs += [(radial_far, radial_ref), (axial_far, axial_ref)]
+    copies = [
+        pltpu.make_async_copy(source, target, arrives.at[k])
+        for k, (source, target) in enumerate(pairs)
+    ]
+    for copy in copies:
+        copy.start()
     for station, packed in enumerate((first, second)):
+        copies[station].wait()
+        if not station:
+            copies[2].wait()
+            copies[3].wait()
         for cell in range(2):
             packed[200 * cell : 200 * cell + 200] = block_ref[station, cell, :, 0:128]
             packed[400:600, 64 * cell : 64 * cell + 64] = block_ref[station, cell, :, 128:192]
@@ -339,9 +355,15 @@
     message = [((stations, own_cells, width, species), F32)] * GROUP
     rows = [pltpu.VMEM((species, species), F32), pltpu.VMEM((8, species), F32)]
 
-    own = call(pack_blocks, [((664, 128), F32)] * 2, scalars=2)(
-        mine, place, block_inverse, radial_coupling, axial_coupling
-    )
+    arrays = (block_inverse, radial_coupling, axial_coupling)
+    own = call(
+        pack_blocks,
+        [((664, 128), F32)] * 2,
+        scratch=[pltpu.VMEM(array.shape, F32) for array in arrays]
+        + [pltpu.SemaphoreType.DMA((4,))],
+        scalars=2,
+        space=pltpu.HBM,
+    )(mine, place, *(pltpu.with_memory_space_constraint(array, pltpu.HBM) for array in arrays))
     below = [shift(own[0], "rad_1", 1), None]
     above = [None, shift(own[1], "rad_1", -1)]
     below[1] = shift(own[1], "rad_1", 1)

time: 131 us -> 130 us (level)
  local copies, waits for them, and re-layouts: 2.56 us -> 0.01 us
    unnamed x8 -> x2, local copies, waits for them, and re-layouts: 2.56 us -> 0.01 us
where the time goes in v4:
time: 130 us; the launch traced here: 129 us
  waiting for transfers between devices  67.7 us (52%)
  starting transfers between devices  36.6 us (28%)
  Pallas kernels  24.8 us (19%)
    ppermute x11, waiting for transfers between devices, hop(): return lax.ppermute(value, 'rad_0', pairs)  29.8 us
    ppermute x12, waiting for transfers between devices, shift(): lax.ppermute(value, axis, [(i, (i + step) % count) for i in range(count)])  29.8 us
    pallas_call x21, Pallas kernels, run(): pl.pallas_call(body, out_shape=[jax.ShapeDtypeStruct(shape, kind) for sha...  24.8 us
    ppermute x11, starting transfers between devices, hop(): return lax.ppermute(value, 'rad_0', pairs)  17.2 us
    ppermute x12, starting transfers between devices, shift(): lax.ppermute(value, axis, [(i, (i + step) % count) for i in range(count)])  15.1 us
    ppermute x1, waiting for transfers between devices, relax(): lax.ppermute(correction, 'ax', [(i + 1, i) for i in range(count - 1)])  4.26 us
    ppermute x1, waiting for transfers between devices, relax(): up = lax.ppermute(correction, 'ax', [(i, i + 1) for i in range(count - 1)])  3.82 us
  transfers between devices with their start and end apart: 25, of which 18 were waited for; matrix products, arithmetic and copies ran while one was open for 0% of the time, Pallas kernels for 11%

profile of v4, /device:TPU:4, one launch (start us, length us, event | category | flops | bytes accessed | tf_op | source)
XLA Modules:
  0.0 129.3 jit_solution(2477513416274033746)
XLA Ops:
  1.4 1.6 %collective-permute-start.5 = (f32[664,128]{1,0:T(8,128)S(1)}, f32[664,128]{1,0:T(8,128)S(1)}, u32[]{:S(2)}, u32[]{:S(2)}) collective-permute-start(f32[664,128]{1,0:T(8,128)S(1)} %get-tuple-element.46.own0), channel_id=1, source_target_pairs={{0,1},{1,2},{2,3},{3,0},{4,5},{5,6},{6,7},{7,4},{8,9},{9,10},{10,1... | collective-permute-start | bytes 1019912 | tf_op jit(solution)/shard_map/ppermute | solution.py:333
  3.0 1.7 %collective-permute-start.4 = (f32[664,128]{1,0:T(8,128)S(1)}, f32[664,128]{1,0:T(8,128)S(1)}, u32[]{:S(2)}, u32[]{:S(2)}) collective-permute-start(f32[664,128]{1,0:T(8,128)S(1)} %get-tuple-element.47.own1), channel_id=1, source_target_pairs={{0,3},{1,0},{2,1},{3,2},{4,7},{5,4},{6,5},{7,6},{8,11},{9,8},{10,9... | collective-permute-start | bytes 1019912 | tf_op jit(solution)/shard_map/ppermute | solution.py:333
  4.7 1.8 %collective-permute-start.3 = (f32[664,128]{1,0:T(8,128)S(1)}, f32[664,128]{1,0:T(8,128)S(1)}, u32[]{:S(2)}, u32[]{:S(2)}) collective-permute-start(f32[664,128]{1,0:T(8,128)S(1)} %get-tuple-element.46.own0), channel_id=1, source_target_pairs={{0,3},{1,0},{2,1},{3,2},{4,7},{5,4},{6,5},{7,6},{8,11},{9,8},{10,9... | collective-permute-start | bytes 1019912 | tf_op jit(solution)/shard_map/ppermute | solution.py:333
  6.7 6.8 %collective-permute-done.5.below0 = f32[664,128]{1,0:T(8,128)S(1)} collective-permute-done((f32[664,128]{1,0:T(8,128)S(1)}, f32[664,128]{1,0:T(8,128)S(1)}, u32[]{:S(2)}, u32[]{:S(2)}) %collective-permute-start.5) | collective-permute-done | bytes 340000 | tf_op jit(solution)/shard_map/ppermute | solution.py:333
  13.9 2.9 %collective-permute-start.8 = (f32[664,128]{1,0:T(8,128)S(1)}, f32[664,128]{1,0:T(8,128)S(1)}, u32[]{:S(2)}, u32[]{:S(2)}) collective-permute-start(f32[664,128]{1,0:T(8,128)S(1)} %collective-permute-done.4.above1), channel_id=1, source_target_pairs={{0,3},{1,0},{2,1},{3,2},{4,7},{5,4},{6,5},{7,6},{8,11},{9,8},{10,9... | collective-permute-start | bytes 1019912 | tf_op jit(solution)/shard_map/ppermute | solution.py:333
  16.7 4.4 %collective-permute-done.3.above0 = f32[664,128]{1,0:T(8,128)S(1)} collective-permute-done((f32[664,128]{1,0:T(8,128)S(1)}, f32[664,128]{1,0:T(8,128)S(1)}, u32[]{:S(2)}, u32[]{:S(2)}) %collective-permute-start.3) | collective-permute-done | bytes 340000 | tf_op jit(solution)/shard_map/ppermute | solution.py:333
  21.8 5.2 %collective-permute-done.7.across0 = f32[664,128]{1,0:T(8,128)S(1)} collective-permute-done((f32[664,128]{1,0:T(8,128)S(1)}, f32[664,128]{1,0:T(8,128)S(1)}, u32[]{:S(2)}, u32[]{:S(2)}) %collective-permute-start.7) | collective-permute-done | bytes 340000 | tf_op jit(solution)/shard_map/ppermute | solution.py:333
  27.0 2.5 %shard_map.49 = (bf16[2,8,200,200]{3,2,1,0:T(8,128)(2,1)S(1)}, bf16[2,8,200,200]{3,2,1,0:T(8,128)(2,1)S(1)}, f32[2,8,8,200]{3,2,1,0:T(8,128)S(1)}, f32[2,8,200,200]{3,2,1,0:T(8,128)S(1)}, f32[2,200,200]{2,1,0:T(8,128)S(1)}) custom-call(s32[1]{0:T(128)} %bitcast.mine_ref, bf16[3,2,2,200,200]{4,3,2,1,0:T(8,128)(2,1)S(1)} %get-tuple-element.48.near_high, ...), custom_call_target="tpu_custom_call" | custom-call | flops 1000 | bytes 1000 | tf_op jit(solution)/shard_map/pallas_call | solution.py:40
  30.8 2.4 %shard_map.55 = (bf16[2,8,200,200]{3,2,1,0:T(8,128)(2,1)S(1)}, bf16[2,8,200,200]{3,2,1,0:T(8,128)(2,1)S(1)}, f32[2,200,200]{2,1,0:T(8,128)S(1)}) custom-call(bf16[2,8,200,200]{3,2,1,0:T(8,128)(2,1)S(1)} %get-tuple-element.51.high, bf16[2,8,200,200]{3,2,1,0:T(8,128)(2,1)S(1)} %get-tuple-element.52.low, f32[2,8,8,200]{3,2,1,0:T(8,128)S(1)} %get-tuple-element.53.coupling), custom_call_target="tpu_custom_call" | custom-call | flops 1000 | bytes 1000 | tf_op jit(solution)/shard_map/pallas_call | solution.py:40
  34.7 3.1 %collective-permute-start = (f32[2,2,32,200]{3,2,1,0:T(8,128)S(1)}, f32[2,2,32,200]{3,2,1,0:T(8,128)S(1)}, u32[]{:S(2)}, u32[]{:S(2)}) collective-permute-start(f32[2,2,32,200]{3,2,1,0:T(8,128)S(1)} %get-tuple-element.43), channel_id=1, source_target_pairs={{0,3},{1,0},{2,1},{3,2},{4,7},{5,4},{6,5},{7,6},{8,11},{9,8},{10,9... | collective-permute-start | bytes 307208 | tf_op jit(solution)/shard_map/ppermute | solution.py:333
  39.1 3.3 %collective-permute-done.m1 = f32[2,2,32,200]{3,2,1,0:T(8,128)S(1)} collective-permute-done((f32[2,2,32,200]{3,2,1,0:T(8,128)S(1)}, f32[2,2,32,200]{3,2,1,0:T(8,128)S(1)}, u32[]{:S(2)}, u32[]{:S(2)}) %collective-permute-start) | collective-permute-done | bytes 102432 | tf_op jit(solution)/shard_map/ppermute | solution.py:333
  42.4 2.3 %collective-permute-done.1.m2 = f32[2,2,32,200]{3,2,1,0:T(8,128)S(1)} collective-permute-done((f32[2,2,32,200]{3,2,1,0:T(8,128)S(1)}, f32[2,2,32,200]{3,2,1,0:T(8,128)S(1)}, u32[]{:S(2)}, u32[]{:S(2)}) %collective-permute-start.1) | collective-permute-done | bytes 102432 | tf_op jit(solution)/shard_map/ppermute | solution.py:333
  46.0 2.1 %shard_map.50 = (f32[2,8,32,200]{3,2,1,0:T(8,128)S(1)}, f32[2,8,32,200]{3,2,1,0:T(8,128)S(1)}, f32[2,32,200]{2,1,0:T(8,128)S(1)}) custom-call(s32[1]{0:T(128)} %bitcast.mine_ref, f32[2,2,32,200]{3,2,1,0:T(8,128)S(1)} %get-tuple-element.42.m0, f32[2,2,32,200]{3,2,1,0:T(8,128)S(1)} %collective-permute-done.m1, ...), custom_call_target="tpu_custom_call" | custom-call | flops 1000 | bytes 1000 | tf_op jit(solution)/shard_map/pallas_call | solution.py:40
  48.1 4.4 %collective-permute-start.9 = (f32[2,32,200]{2,1,0:T(8,128)S(1)}, f32[2,32,200]{2,1,0:T(8,128)S(1)}, u32[]{:S(2)}, u32[]{:S(2)}) collective-permute-start(f32[2,32,200]{2,1,0:T(8,128)S(1)} %get-tuple-element.54.ends), channel_id=1, source_target_pairs={{0,4},{8,12},{1,5},{9,13},{2,6},{10,14},{3,7},{11,15},{16,20},{24,... | collective-permute-start | bytes 153608 | tf_op jit(solution)/shard_map/ppermute | solution.py:337
  52.5 1.9 %collective-permute-done.9.near = f32[2,32,200]{2,1,0:T(8,128)S(1)} collective-permute-done((f32[2,32,200]{2,1,0:T(8,128)S(1)}, f32[2,32,200]{2,1,0:T(8,128)S(1)}, u32[]{:S(2)}, u32[]{:S(2)}) %collective-permute-start.9) | collective-permute-done | bytes 51232 | tf_op jit(solution)/shard_map/ppermute | solution.py:337
  56.0 2.2 %shard_map.53 = (bf16[2,8,200,200]{3,2,1,0:T(8,128)(2,1)S(1)}, bf16[2,8,200,200]{3,2,1,0:T(8,128)(2,1)S(1)}, f32[2,200,200]{2,1,0:T(8,128)S(1)}) custom-call(bf16[2,8,200,200]{3,2,1,0:T(8,128)(2,1)S(1)} %get-tuple-element.51.high, bf16[2,8,200,200]{3,2,1,0:T(8,128)(2,1)S(1)} %get-tuple-element.52.low, f32[2,8,8,200]{3,2,1,0:T(8,128)S(1)} %get-tuple-element.53.coupling, ...), custom_call_target="tpu_custom_call" | custom-call | flops 1000 | bytes 1000 | tf_op jit(solution)/shard_map/pallas_call | solution.py:40
  58.2 1.8 %shard_map.52 = (f32[2,8,32,200]{3,2,1,0:T(8,128)S(1)}, f32[2,32,200]{2,1,0:T(8,128)S(1)}) custom-call(f32[2,8,32,200]{3,2,1,0:T(8,128)S(1)} %get-tuple-element.56.inner, bf16[2,8,200,200]{3,2,1,0:T(8,128)(2,1)S(1)} %get-tuple-element.51.high, bf16[2,8,200,200]{3,2,1,0:T(8,128)(2,1)S(1)} %get-tuple-element.52.low, ...), custom_call_target="tpu_custom_call" | custom-call | flops 1000 | bytes 1000 | tf_op jit(solution)/shard_map/pallas_call | solution.py:40
  61.8 8.8 %collective-permute-done.13.refs_1_.near = f32[2,32,200]{2,1,0:T(8,128)S(1)} collective-permute-done((f32[2,32,200]{2,1,0:T(8,128)S(1)}, f32[2,32,200]{2,1,0:T(8,128)S(1)}, u32[]{:S(2)}, u32[]{:S(2)}) %collective-permute-start.13) | collective-permute-done | bytes 51232 | tf_op jit(solution)/shard_map/ppermute | solution.py:337
  73.4 4.9 %collective-permute-done.15.middle = f32[2,32,200]{2,1,0:T(8,128)S(1)} collective-permute-done((f32[2,32,200]{2,1,0:T(8,128)S(1)}, f32[2,32,200]{2,1,0:T(8,128)S(1)}, u32[]{:S(2)}, u32[]{:S(2)}) %collective-permute-start.15) | collective-permute-done | bytes 51232 | tf_op jit(solution)/shard_map/ppermute | solution.py:337
  79.6 1.9 %collective-permute-start.17 = (f32[2,8,32,200]{3,2,1,0:T(8,128)S(1)}, f32[2,8,32,200]{3,2,1,0:T(8,128)S(1)}, u32[]{:S(2)}, u32[]{:S(2)}) collective-permute-start(f32[2,8,32,200]{3,2,1,0:T(8,128)S(1)} %shard_map.58.own), channel_id=1, source_target_pairs={{16,0},{32,16},{48,32},{64,48},{80,64},{96,80},{112,96},{17,1},{33... | collective-permute-start | bytes 1228808 | tf_op jit(solution)/shard_map/ppermute | solution.py:412
  81.6 2.4 %collective-permute-start.16 = (f32[2,8,32,200]{3,2,1,0:T(8,128)S(1)}, f32[2,8,32,200]{3,2,1,0:T(8,128)S(1)}, u32[]{:S(2)}, u32[]{:S(2)}) collective-permute-start(f32[2,8,32,200]{3,2,1,0:T(8,128)S(1)} %shard_map.58.own), channel_id=1, source_target_pairs={{0,16},{16,32},{32,48},{48,64},{64,80},{80,96},{96,112},{1,17},{17... | collective-permute-start | bytes 1228808 | tf_op jit(solution)/shard_map/ppermute | solution.py:411
  84.0 4.3 %collective-permute-done.17.above = f32[2,8,32,200]{3,2,1,0:T(8,128)S(1)} collective-permute-done((f32[2,8,32,200]{3,2,1,0:T(8,128)S(1)}, f32[2,8,32,200]{3,2,1,0:T(8,128)S(1)}, u32[]{:S(2)}, u32[]{:S(2)}) %collective-permute-start.17) | collective-permute-done | bytes 409632 | tf_op jit(solution)/shard_map/ppermute | solution.py:412
  88.2 3.8 %collective-permute-done.16.below = f32[2,8,32,200]{3,2,1,0:T(8,128)S(1)} collective-permute-done((f32[2,8,32,200]{3,2,1,0:T(8,128)S(1)}, f32[2,8,32,200]{3,2,1,0:T(8,128)S(1)}, u32[]{:S(2)}, u32[]{:S(2)}) %collective-permute-start.16) | collective-permute-done | bytes 409632 | tf_op jit(solution)/shard_map/ppermute | solution.py:411
  92.1 2.0 %shard_map.59 = (f32[2,8,32,200]{3,2,1,0:T(8,128)S(1)}, f32[2,32,200]{2,1,0:T(8,128)S(1)}) custom-call(f32[2,8,32,200]{3,2,1,0:T(8,128)S(1)} %collective-permute-done.16.below, f32[2,8,32,200]{3,2,1,0:T(8,128)S(1)} %shard_map.58.own, f32[2,8,32,200]{3,2,1,0:T(8,128)S(1)} %collective-permute-done.17.above, f32[2,8,32,200]{3,2,1,0:T(8,128)S(1)} %get-tuple-element.68.sources, ...), custom_call_target="tpu_custom_call" | custom-call | flops 1000 | bytes 1000 | tf_op jit(solution)/shard_map/pallas_call | solution.py:40
  94.1 1.9 %collective-permute-start.18 = (f32[2,32,200]{2,1,0:T(8,128)S(1)}, f32[2,32,200]{2,1,0:T(8,128)S(1)}, u32[]{:S(2)}, u32[]{:S(2)}) collective-permute-start(f32[2,32,200]{2,1,0:T(8,128)S(1)} %get-tuple-element.69.refs_0_), channel_id=1, source_target_pairs={{0,4},{4,0},{8,12},{1,5},{5,1},{9,13},{2,6},{6,2},{10,14},{3,7},{7... | collective-permute-start | bytes 153608 | tf_op jit(solution)/shard_map/ppermute | solution.py:337
  96.0 4.2 %collective-permute-done.18.refs_1_.near = f32[2,32,200]{2,1,0:T(8,128)S(1)} collective-permute-done((f32[2,32,200]{2,1,0:T(8,128)S(1)}, f32[2,32,200]{2,1,0:T(8,128)S(1)}, u32[]{:S(2)}, u32[]{:S(2)}) %collective-permute-start.18) | collective-permute-done | bytes 51232 | tf_op jit(solution)/shard_map/ppermute | solution.py:337
  100.5 1.6 %collective-permute-start.19 = (f32[2,32,200]{2,1,0:T(8,128)S(1)}, f32[2,32,200]{2,1,0:T(8,128)S(1)}, u32[]{:S(2)}, u32[]{:S(2)}) collective-permute-start(f32[2,32,200]{2,1,0:T(8,128)S(1)} %shard_map.60), channel_id=1, source_target_pairs={{4,8},{0,12},{5,9},{1,13},{6,10},{2,14},{7,11},{3,15},{20,24},{16,... | collective-permute-start | bytes 153608 | tf_op jit(solution)/shard_map/ppermute | solution.py:337
  102.1 1.8 %shard_map.61 = (f32[2,8,32,200]{3,2,1,0:T(8,128)S(1)}, f32[2,32,200]{2,1,0:T(8,128)S(1)}) custom-call(f32[2,8,32,200]{3,2,1,0:T(8,128)S(1)} %get-tuple-element.70.inner, bf16[2,8,200,200]{3,2,1,0:T(8,128)(2,1)S(1)} %get-tuple-element.51.high, bf16[2,8,200,200]{3,2,1,0:T(8,128)(2,1)S(1)} %get-tuple-element.52.low, ...), custom_call_target="tpu_custom_call" | custom-call | flops 1000 | bytes 1000 | tf_op jit(solution)/shard_map/pallas_call | solution.py:40
  105.7 4.9 %collective-permute-done.20.refs_1_.near = f32[2,32,200]{2,1,0:T(8,128)S(1)} collective-permute-done((f32[2,32,200]{2,1,0:T(8,128)S(1)}, f32[2,32,200]{2,1,0:T(8,128)S(1)}, u32[]{:S(2)}, u32[]{:S(2)}) %collective-permute-start.20) | collective-permute-done | bytes 51232 | tf_op jit(solution)/shard_map/ppermute | solution.py:337
  113.1 5.0 %collective-permute-done.21.middle = f32[2,32,200]{2,1,0:T(8,128)S(1)} collective-permute-done((f32[2,32,200]{2,1,0:T(8,128)S(1)}, f32[2,32,200]{2,1,0:T(8,128)S(1)}, u32[]{:S(2)}, u32[]{:S(2)}) %collective-permute-start.21) | collective-permute-done | bytes 51232 | tf_op jit(solution)/shard_map/ppermute | solution.py:337
  121.7 2.9 %collective-permute-done.22.m1 = f32[2,2,32,200]{3,2,1,0:T(8,128)S(1)} collective-permute-done((f32[2,2,32,200]{3,2,1,0:T(8,128)S(1)}, f32[2,2,32,200]{3,2,1,0:T(8,128)S(1)}, u32[]{:S(2)}, u32[]{:S(2)}) %collective-permute-start.22) | collective-permute-done | bytes 102432 | tf_op jit(solution)/shard_map/ppermute | solution.py:333
  124.7 2.3 %collective-permute-done.23.m2 = f32[2,2,32,200]{3,2,1,0:T(8,128)S(1)} collective-permute-done((f32[2,2,32,200]{3,2,1,0:T(8,128)S(1)}, f32[2,2,32,200]{3,2,1,0:T(8,128)S(1)}, u32[]{:S(2)}, u32[]{:S(2)}) %collective-permute-start.23) | collective-permute-done | bytes 102432 | tf_op jit(solution)/shard_map/ppermute | solution.py:333
  (41 shorter events, 26.0 us)
Async XLA Ops:
  1.4 12.1 %collective-permute-start.5 = (f32[664,128]{1,0:T(8,128)S(1)}, f32[664,128]{1,0:T(8,128)S(1)}, u32[]{:S(2)}, u32[]{:S(2)}) collective-permute-start(f32[664,128]{1,0:T(8,128)S(1)} %get-tuple-element.46.own0), channel_id=1, source_target_pairs={{0,1},{1,2},{2,3},{3,0},{4,5},{5,6},{6,7},{7,4},{8,9},{9,10},{10,1... | collective-permute-start | bytes 1019912 | tf_op jit(solution)/shard_map/ppermute | solution.py:333
  3.0 10.8 %collective-permute-start.4 = (f32[664,128]{1,0:T(8,128)S(1)}, f32[664,128]{1,0:T(8,128)S(1)}, u32[]{:S(2)}, u32[]{:S(2)}) collective-permute-start(f32[664,128]{1,0:T(8,128)S(1)} %get-tuple-element.47.own1), channel_id=1, source_target_pairs={{0,3},{1,0},{2,1},{3,2},{4,7},{5,4},{6,5},{7,6},{8,11},{9,8},{10,9... | collective-permute-start | bytes 1019912 | tf_op jit(solution)/shard_map/ppermute | solution.py:333
  4.7 16.5 %collective-permute-start.3 = (f32[664,128]{1,0:T(8,128)S(1)}, f32[664,128]{1,0:T(8,128)S(1)}, u32[]{:S(2)}, u32[]{:S(2)}) collective-permute-start(f32[664,128]{1,0:T(8,128)S(1)} %get-tuple-element.46.own0), channel_id=1, source_target_pairs={{0,3},{1,0},{2,1},{3,2},{4,7},{5,4},{6,5},{7,6},{8,11},{9,8},{10,9... | collective-permute-start | bytes 1019912 | tf_op jit(solution)/shard_map/ppermute | solution.py:333
  6.5 14.7 %collective-permute-start.6 = (f32[664,128]{1,0:T(8,128)S(1)}, f32[664,128]{1,0:T(8,128)S(1)}, u32[]{:S(2)}, u32[]{:S(2)}) collective-permute-start(f32[664,128]{1,0:T(8,128)S(1)} %get-tuple-element.47.own1), channel_id=1, source_target_pairs={{0,1},{1,2},{2,3},{3,0},{4,5},{5,6},{6,7},{7,4},{8,9},{9,10},{10,1... | collective-permute-start | bytes 1019912 | tf_op jit(solution)/shard_map/ppermute | solution.py:333
  13.5 13.5 %collective-permute-start.7 = (f32[664,128]{1,0:T(8,128)S(1)}, f32[664,128]{1,0:T(8,128)S(1)}, u32[]{:S(2)}, u32[]{:S(2)}) collective-permute-start(f32[664,128]{1,0:T(8,128)S(1)} %collective-permute-done.5.below0), channel_id=1, source_target_pairs={{0,1},{1,2},{2,3},{3,0},{4,5},{5,6},{6,7},{7,4},{8,9},{9,10},{10,1... | collective-permute-start | bytes 1019912 | tf_op jit(solution)/shard_map/ppermute | solution.py:333
  13.9 13.2 %collective-permute-start.8 = (f32[664,128]{1,0:T(8,128)S(1)}, f32[664,128]{1,0:T(8,128)S(1)}, u32[]{:S(2)}, u32[]{:S(2)}) collective-permute-start(f32[664,128]{1,0:T(8,128)S(1)} %collective-permute-done.4.above1), channel_id=1, source_target_pairs={{0,3},{1,0},{2,1},{3,2},{4,7},{5,4},{6,5},{7,6},{8,11},{9,8},{10,9... | collective-permute-start | bytes 1019912 | tf_op jit(solution)/shard_map/ppermute | solution.py:333
  29.5 30.6 %collective-permute-start.12 = (f32[2,200,200]{2,1,0:T(8,128)S(1)}, f32[2,200,200]{2,1,0:T(8,128)S(1)}, u32[]{:S(2)}, u32[]{:S(2)}) collective-permute-start(f32[2,200,200]{2,1,0:T(8,128)S(1)} %get-tuple-element.55.chain.refs_2_), channel_id=1, source_target_pairs={{4,0},{8,12},{5,1},{9,13},{6,2},{10,14},{7,3},{11,15},{20,16},{24,... | collective-permute-start | bytes 960008 | tf_op jit(solution)/shard_map/ppermute | solution.py:337
  30.8 3.7 %copy-start = (f32[2,2,200,128]{3,2,1,0:T(8,128)S(1)}, f32[2,2,200,128]{3,2,1,0:T(8,128)}, u32[]{:S(2)}) copy-start(f32[2,2,200,128]{3,2,1,0:T(8,128)} %sources_ref.1) | copy-start | bytes 1228804
  33.2 28.6 %collective-permute-start.14 = (f32[2,200,200]{2,1,0:T(8,128)S(1)}, f32[2,200,200]{2,1,0:T(8,128)S(1)}, u32[]{:S(2)}, u32[]{:S(2)}) collective-permute-start(f32[2,200,200]{2,1,0:T(8,128)S(1)} %get-tuple-element.61.refs_2_), channel_id=1, source_target_pairs={{4,0},{8,12},{5,1},{9,13},{6,2},{10,14},{7,3},{11,15},{20,16},{24,... | collective-permute-start | bytes 960008 | tf_op jit(solution)/shard_map/ppermute | solution.py:337
  34.7 7.7 %collective-permute-start = (f32[2,2,32,200]{3,2,1,0:T(8,128)S(1)}, f32[2,2,32,200]{3,2,1,0:T(8,128)S(1)}, u32[]{:S(2)}, u32[]{:S(2)}) collective-permute-start(f32[2,2,32,200]{3,2,1,0:T(8,128)S(1)} %get-tuple-element.43), channel_id=1, source_target_pairs={{0,3},{1,0},{2,1},{3,2},{4,7},{5,4},{6,5},{7,6},{8,11},{9,8},{10,9... | collective-permute-start | bytes 307208 | tf_op jit(solution)/shard_map/ppermute | solution.py:333
  37.8 6.9 %collective-permute-start.1 = (f32[2,2,32,200]{3,2,1,0:T(8,128)S(1)}, f32[2,2,32,200]{3,2,1,0:T(8,128)S(1)}, u32[]{:S(2)}, u32[]{:S(2)}) collective-permute-start(f32[2,2,32,200]{3,2,1,0:T(8,128)S(1)} %get-tuple-element.44), channel_id=1, source_target_pairs={{0,2},{1,3},{2,0},{3,1},{4,6},{5,7},{6,4},{7,5},{8,10},{9,11},{10,... | collective-permute-start | bytes 307208 | tf_op jit(solution)/shard_map/ppermute | solution.py:333
  38.4 7.6 %collective-permute-start.2 = (f32[2,2,32,200]{3,2,1,0:T(8,128)S(1)}, f32[2,2,32,200]{3,2,1,0:T(8,128)S(1)}, u32[]{:S(2)}, u32[]{:S(2)}) collective-permute-start(f32[2,2,32,200]{3,2,1,0:T(8,128)S(1)} %get-tuple-element.45), channel_id=1, source_target_pairs={{0,1},{1,2},{2,3},{3,0},{4,5},{5,6},{6,7},{7,4},{8,9},{9,10},{10,1... | collective-permute-start | bytes 307208 | tf_op jit(solution)/shard_map/ppermute | solution.py:333
  48.1 6.3 %collective-permute-start.9 = (f32[2,32,200]{2,1,0:T(8,128)S(1)}, f32[2,32,200]{2,1,0:T(8,128)S(1)}, u32[]{:S(2)}, u32[]{:S(2)}) collective-permute-start(f32[2,32,200]{2,1,0:T(8,128)S(1)} %get-tuple-element.54.ends), channel_id=1, source_target_pairs={{0,4},{8,12},{1,5},{9,13},{2,6},{10,14},{3,7},{11,15},{16,20},{24,... | collective-permute-start | bytes 153608 | tf_op jit(solution)/shard_map/ppermute | solution.py:337
  54.6 5.4 %collective-permute-start.11 = (f32[2,32,200]{2,1,0:T(8,128)S(1)}, f32[2,32,200]{2,1,0:T(8,128)S(1)}, u32[]{:S(2)}, u32[]{:S(2)}) collective-permute-start(f32[2,32,200]{2,1,0:T(8,128)S(1)} %shard_map.51), channel_id=1, source_target_pairs={{4,12},{5,13},{6,14},{7,15},{20,28},{21,29},{22,30},{23,31},{36,44... | collective-permute-start | bytes 153608 | tf_op jit(solution)/shard_map/ppermute | solution.py:337
  55.3 4.7 %collective-permute-start.10 = (f32[2,32,200]{2,1,0:T(8,128)S(1)}, f32[2,32,200]{2,1,0:T(8,128)S(1)}, u32[]{:S(2)}, u32[]{:S(2)}) collective-permute-start(f32[2,32,200]{2,1,0:T(8,128)S(1)} %shard_map.51), channel_id=1, source_target_pairs={{4,8},{5,9},{6,10},{7,11},{20,24},{21,25},{22,26},{23,27},{36,40},... | collective-permute-start | bytes 153608 | tf_op jit(solution)/shard_map/ppermute | solution.py:337
  60.5 10.1 %collective-permute-start.13 = (f32[2,32,200]{2,1,0:T(8,128)S(1)}, f32[2,32,200]{2,1,0:T(8,128)S(1)}, u32[]{:S(2)}, u32[]{:S(2)}) collective-permute-start(f32[2,32,200]{2,1,0:T(8,128)S(1)} %get-tuple-element.60.refs_0_), channel_id=1, source_target_pairs={{12,8},{8,12},{4,0},{13,9},{9,13},{5,1},{14,10},{10,14},{6,2},{15,... | collective-permute-start | bytes 153608 | tf_op jit(solution)/shard_map/ppermute | solution.py:337
  70.9 7.4 %collective-permute-start.15 = (f32[2,32,200]{2,1,0:T(8,128)S(1)}, f32[2,32,200]{2,1,0:T(8,128)S(1)}, u32[]{:S(2)}, u32[]{:S(2)}) collective-permute-start(f32[2,32,200]{2,1,0:T(8,128)S(1)} %shard_map.56), channel_id=1, source_target_pairs={{8,4},{12,0},{9,5},{13,1},{10,6},{14,2},{11,7},{15,3},{24,20},{28,... | collective-permute-start | bytes 153608 | tf_op jit(solution)/shard_map/ppermute | solution.py:337
  79.6 8.6 %collective-permute-start.17 = (f32[2,8,32,200]{3,2,1,0:T(8,128)S(1)}, f32[2,8,32,200]{3,2,1,0:T(8,128)S(1)}, u32[]{:S(2)}, u32[]{:S(2)}) collective-permute-start(f32[2,8,32,200]{3,2,1,0:T(8,128)S(1)} %shard_map.58.own), channel_id=1, source_target_pairs={{16,0},{32,16},{48,32},{64,48},{80,64},{96,80},{112,96},{17,1},{33... | collective-permute-start | bytes 1228808 | tf_op jit(solution)/shard_map/ppermute | solution.py:412
  81.6 10.5 %collective-permute-start.16 = (f32[2,8,32,200]{3,2,1,0:T(8,128)S(1)}, f32[2,8,32,200]{3,2,1,0:T(8,128)S(1)}, u32[]{:S(2)}, u32[]{:S(2)}) collective-permute-start(f32[2,8,32,200]{3,2,1,0:T(8,128)S(1)} %shard_map.58.own), channel_id=1, source_target_pairs={{0,16},{16,32},{32,48},{48,64},{64,80},{80,96},{96,112},{1,17},{17... | collective-permute-start | bytes 1228808 | tf_op jit(solution)/shard_map/ppermute | solution.py:411
  94.1 6.2 %collective-permute-start.18 = (f32[2,32,200]{2,1,0:T(8,128)S(1)}, f32[2,32,200]{2,1,0:T(8,128)S(1)}, u32[]{:S(2)}, u32[]{:S(2)}) collective-permute-start(f32[2,32,200]{2,1,0:T(8,128)S(1)} %get-tuple-element.69.refs_0_), channel_id=1, source_target_pairs={{0,4},{4,0},{8,12},{1,5},{5,1},{9,13},{2,6},{6,2},{10,14},{3,7},{7... | collective-permute-start | bytes 153608 | tf_op jit(solution)/shard_map/ppermute | solution.py:337
  100.5 3.5 %collective-permute-start.19 = (f32[2,32,200]{2,1,0:T(8,128)S(1)}, f32[2,32,200]{2,1,0:T(8,128)S(1)}, u32[]{:S(2)}, u32[]{:S(2)}) collective-permute-start(f32[2,32,200]{2,1,0:T(8,128)S(1)} %shard_map.60), channel_id=1, source_target_pairs={{4,8},{0,12},{5,9},{1,13},{6,10},{2,14},{7,11},{3,15},{20,24},{16,... | collective-permute-start | bytes 153608 | tf_op jit(solution)/shard_map/ppermute | solution.py:337
  104.4 6.2 %collective-permute-start.20 = (f32[2,32,200]{2,1,0:T(8,128)S(1)}, f32[2,32,200]{2,1,0:T(8,128)S(1)}, u32[]{:S(2)}, u32[]{:S(2)}) collective-permute-start(f32[2,32,200]{2,1,0:T(8,128)S(1)} %get-tuple-element.72.refs_0_), channel_id=1, source_target_pairs={{12,8},{8,12},{4,0},{13,9},{9,13},{5,1},{14,10},{10,14},{6,2},{15,... | collective-permute-start | bytes 153608 | tf_op jit(solution)/shard_map/ppermute | solution.py:337
  110.8 7.4 %collective-permute-start.21 = (f32[2,32,200]{2,1,0:T(8,128)S(1)}, f32[2,32,200]{2,1,0:T(8,128)S(1)}, u32[]{:S(2)}, u32[]{:S(2)}) collective-permute-start(f32[2,32,200]{2,1,0:T(8,128)S(1)} %shard_map.63), channel_id=1, source_target_pairs={{8,4},{12,0},{9,5},{13,1},{10,6},{14,2},{11,7},{15,3},{24,20},{28,... | collective-permute-start | bytes 153608 | tf_op jit(solution)/shard_map/ppermute | solution.py:337
  119.6 5.0 %collective-permute-start.22 = (f32[2,2,32,200]{3,2,1,0:T(8,128)S(1)}, f32[2,2,32,200]{3,2,1,0:T(8,128)S(1)}, u32[]{:S(2)}, u32[]{:S(2)}) collective-permute-start(f32[2,2,32,200]{3,2,1,0:T(8,128)S(1)} %get-tuple-element.76), channel_id=1, source_target_pairs={{0,3},{1,0},{2,1},{3,2},{4,7},{5,4},{6,5},{7,6},{8,11},{9,8},{10,9... | collective-permute-start | bytes 307208 | tf_op jit(solution)/shard_map/ppermute | solution.py:333
  120.4 6.6 %collective-permute-start.23 = (f32[2,2,32,200]{3,2,1,0:T(8,128)S(1)}, f32[2,2,32,200]{3,2,1,0:T(8,128)S(1)}, u32[]{:S(2)}, u32[]{:S(2)}) collective-permute-start(f32[2,2,32,200]{3,2,1,0:T(8,128)S(1)} %get-tuple-element.77), channel_id=1, source_target_pairs={{0,2},{1,3},{2,0},{3,1},{4,6},{5,7},{6,4},{7,5},{8,10},{9,11},{10,... | collective-permute-start | bytes 307208 | tf_op jit(solution)/shard_map/ppermute | solution.py:333
  120.8 7.4 %collective-permute-start.24 = (f32[2,2,32,200]{3,2,1,0:T(8,128)S(1)}, f32[2,2,32,200]{3,2,1,0:T(8,128)S(1)}, u32[]{:S(2)}, u32[]{:S(2)}) collective-permute-start(f32[2,2,32,200]{3,2,1,0:T(8,128)S(1)} %get-tuple-element.78), channel_id=1, source_target_pairs={{0,1},{1,2},{2,3},{3,0},{4,5},{5,6},{6,7},{7,4},{8,9},{9,10},{10,1... | collective-permute-start | bytes 307208 | tf_op jit(solution)/shard_map/ppermute | solution.py:333
